TPU v7x, 256 devices: a whole 4x4x8 slice. The times are simulated.
256 devices in a mesh: row: 8 (over z), col: 16 (over x, y_hi, core), img: 2 (over y_lo).
Axes of the slice: x: 4, y: 4 (y_hi: 2, y_lo: 2; y = y_hi * 2 + y_lo), z: 8, core: 2. Of those that a mesh axis runs over, the one named last changes fastest.
Arguments:
- tokens: bfloat16 [192, 576, 512], P(('img', 'row'), 'col'), parts along dimension 0, may hold values from -6 to 6
- qkv_weight: bfloat16 [2, 512, 1536], P(None, 'col'), may hold values from -0.25 to 0.25
- proj_weight: bfloat16 [2, 512, 512], P(None, 'col'), may hold values from -0.25 to 0.25
- hidden_weight: bfloat16 [2, 512, 2048], P(None, 'col'), may hold values from -0.25 to 0.25
- output_weight: bfloat16 [2, 2048, 512], P(None, 'col'), may hold values from -0.125 to 0.125
- norm_gain: float32 [2, 2, 512], replicated, may hold values from 0.25 to 1.75
- model_bias: float32 [2, 4, 512], replicated, may hold values from -2 to 2
- qkv_bias: float32 [2, 1536], replicated, may hold values from -2 to 2
- hidden_bias: float32 [2, 2048], replicated, may hold values from -2 to 2
- position_bias: float32 [2, 16, 23, 23], replicated, may hold values from -3 to 250
Outputs:
- result: bfloat16 [192, 576, 512], P(('img', 'row'), 'col'), parts along dimension 0
There are 2 independent parts, one for each index of `img`. A program takes and returns all parts, laid end to end along the dimension named above; an argument that names none is the same for every part. Nothing has to cross between parts.
All inputs are finite; a program needn't handle non-finite values.
Results may differ from a plain program's by a relative error of at most 0.012.
Values may be sent and summed in bfloat16 or wider, within the bound.
No kernel may reach another device: no remote copies, remote signals or barrier semaphores. Data moves between devices by JAX's collectives and lax.ppermute only.
A program may use at most 192 MiB of HBM per device.

v0:
```python
import jax
import jax.numpy as jnp
from jax import lax
from jax.sharding import PartitionSpec as P

HEADS = 16
WIN = 12
SHIFT = 6


def extended(block, sides, width):
    for axis, dim in sides:
        count = lax.axis_size(axis)
        forward = [(i, i + 1) for i in range(count - 1)]
        forward.append((count - 1, 0))
        backward = [(target, source) for source, target in forward]
        low = lax.ppermute(
            lax.slice_in_dim(block, block.shape[dim] - width, None, axis=dim), axis, forward
        )
        high = lax.ppermute(lax.slice_in_dim(block, 0, width, axis=dim), axis, backward)
        block = jnp.concatenate([low, block, high], axis=dim)
    return block


def side_by_side(arrays, axis, dim, along):
    both = jnp.concatenate(arrays, axis=along)
    whole, at, finished = (lax.all_gather(both, axis, axis=dim, tiled=True), 0, [])
    for a in arrays:
        finished.append(lax.slice_in_dim(whole, at, at + a.shape[along], axis=along))
        at += a.shape[along]
    return tuple(finished)


def layer_norm(values, gain, shift):
    center = values - jnp.mean(values, -1, keepdims=True)
    spread = jnp.mean(center * center, -1, keepdims=True)
    return center * lax.rsqrt(spread + 1e-05) * gain + shift


def bias_table(table):
    offsets = jnp.arange(WIN)
    levels = jnp.arange(2 * WIN - 1)
    onehot = (
        offsets[:, None, None] - offsets[None, :, None] + WIN - 1 == levels[None, None, :]
    ).astype(jnp.float32)
    partial_rows = jnp.einsum("ika,hab->hikb", onehot, table)
    picked = jnp.einsum("hikb,jlb->hijkl", partial_rows, onehot)
    return picked.reshape(table.shape[0], WIN * WIN, WIN * WIN)


def labels(start, count, total):
    index = start + jnp.arange(count)
    return (index >= total - WIN).astype(jnp.int32) + (index >= total - SHIFT).astype(jnp.int32)


def to_windows(grid):
    height, width, channels = grid.shape
    nwin = width // WIN
    return grid.reshape(height, nwin, WIN, channels).transpose(1, 0, 2, 3).reshape(-1, channels)


def from_windows(flat, height, width):
    channels = flat.shape[1]
    nwin = width // WIN
    return (
        flat.reshape(nwin, height, WIN, channels)
        .transpose(1, 0, 2, 3)
        .reshape(height, width, channels)
    )


def window_attention(normed, qkv_matrix, qkv_shift, proj_matrix, position, window_labels):
    channels = normed.shape[1]
    head_dim = channels // HEADS
    tokens_here = normed.shape[0]
    nwin = tokens_here // (WIN * WIN)
    qkv = (jnp.dot(normed, qkv_matrix, preferred_element_type=jnp.float32) + qkv_shift).astype(
        jnp.bfloat16
    )
    qkv = qkv.reshape(nwin, WIN * WIN, 3, HEADS, head_dim)
    scores = jnp.einsum(
        "wqhe,wkhe->whqk", qkv[:, :, 0], qkv[:, :, 1], preferred_element_type=jnp.float32
    )
    scores = scores / jnp.sqrt(jnp.float32(head_dim)) + position[None]
    if window_labels is not None:
        same = window_labels[:, :, None] == window_labels[:, None, :]
        scores = jnp.where(same[:, None], scores, -1000000000.0)
    attn = jax.nn.softmax(scores, -1).astype(jnp.bfloat16)
    heads_out = jnp.einsum(
        "whqk,wkhe->wqhe", attn, qkv[:, :, 2], preferred_element_type=jnp.float32
    ).astype(jnp.bfloat16)
    heads_out = heads_out.reshape(tokens_here, channels)
    return jnp.dot(heads_out, proj_matrix, preferred_element_type=jnp.float32)


def roll_tile(tile, direction):
    height, width = (tile.shape[0], tile.shape[1])
    padded = extended(tile, (("row", 0), ("col", 1)), SHIFT)
    if direction < 0:
        return padded[2 * SHIFT : height + 2 * SHIFT, 2 * SHIFT : width + 2 * SHIFT]
    return padded[:height, :width]


def swin_block(
    grid, layer, masked, matrix, norm_gain, model_bias, qkv_bias, hidden_bias, position_bias
):
    height, width, channels = grid.shape
    nwin = width // WIN
    flat = to_windows(grid).astype(jnp.float32)
    normed = layer_norm(flat, norm_gain[layer, 0], model_bias[layer, 0]).astype(jnp.bfloat16)
    position = bias_table(position_bias[layer])
    if masked:
        total_rows = WIN * lax.axis_size("row")
        total_cols = width * lax.axis_size("col")
        row_labels = labels(WIN * lax.axis_index("row"), height, total_rows)
        col_labels = labels(width * lax.axis_index("col"), width, total_cols)
        grid_labels = row_labels[:, None] * 3 + col_labels[None, :]
        window_labels = (
            grid_labels.reshape(WIN, nwin, WIN).transpose(1, 0, 2).reshape(nwin, WIN * WIN)
        )
    else:
        window_labels = None
    attended = window_attention(
        normed, matrix(0, layer), qkv_bias[layer], matrix(1, layer), position, window_labels
    )
    middle = flat + (attended + model_bias[layer, 2])
    normed2 = layer_norm(middle, norm_gain[layer, 1], model_bias[layer, 1]).astype(jnp.bfloat16)
    hidden = jax.nn.gelu(
        jnp.dot(normed2, matrix(2, layer), preferred_element_type=jnp.float32) + hidden_bias[layer],
        approximate=False,
    ).astype(jnp.bfloat16)
    final = middle + (
        jnp.dot(hidden, matrix(3, layer), preferred_element_type=jnp.float32) + model_bias[layer, 3]
    )
    return from_windows(final.astype(jnp.bfloat16), height, width)


def local(
    tokens,
    qkv_weight,
    proj_weight,
    hidden_weight,
    output_weight,
    norm_gain,
    model_bias,
    qkv_bias,
    hidden_bias,
    position_bias,
):
    whole = (
        *side_by_side((qkv_weight, proj_weight, hidden_weight), "col", 1, 2),
        lax.all_gather(output_weight, "col", axis=1, tiled=True),
    )

    def matrix(which, layer):
        return whole[which][layer]

    extras = (norm_gain, model_bias, qkv_bias, hidden_bias, position_bias)
    first = swin_block(tokens, 0, False, matrix, *extras)
    shifted = roll_tile(first, -1)
    second = swin_block(shifted, 1, True, matrix, *extras)
    return roll_tile(second, 1)


def solution(mesh):
    in_specs = (
        P(("img", "row"), "col", None),
        P(None, "col", None),
        P(None, "col", None),
        P(None, "col", None),
        P(None, "col", None),
        P(),
        P(),
        P(),
        P(),
        P(),
    )
    out_specs = P(("img", "row"), "col", None)
    return jax.shard_map(local, mesh=mesh, in_specs=in_specs, out_specs=out_specs, check_vma=False)
```

profile of v0, /device:TPU:64, one launch (start us, length us, event | category | flops | bytes accessed | tf_op | source)
XLA Modules:
  0.0 253.6 jit_solution(1671173112283670495)
XLA Ops:
  6.5 1.9 pad_maximum_fusion
  15.9 7.0 %convolution_bitcast_fusion.1 = f32[16,12,12,12,12]{0,4,3,1,2:T(8,128)} fusion(bf16[16,12,12,23]{3,2,0,1:T(8,128)(2,1)S(1)} %convolution_bitcast_fusion.3, s32[12,12]{1,0:T(8,128)S(1)} %subtract_add_fusion), kind=kOutput, calls=%fused_computation.3 | convolution fusion | flops 15265008 | bytes 1433664 | tf_op jit(solution)/shard_map/hikb,jlb->hijkl/dot_general | solution.py:47
  22.9 22.1 %copy.140 = f32[16,12,12,12,12]{2,1,4,3,0:T(8,128)} copy(f32[16,12,12,12,12]{0,4,3,1,2:T(8,128)} %convolution_bitcast_fusion.1) | data formatting | bytes 2654208 | tf_op jit(solution)/shard_map/add | solution.py:84
  45.0 13.6 %reshape.248 = f32[16,144,144]{1,2,0:T(8,128)} reshape(f32[16,12,12,12,12]{2,1,4,3,0:T(8,128)} %copy.140) | data formatting | bytes 2654208 | tf_op jit(solution)/shard_map/add | solution.py:84
  59.0 7.0 %convolution_bitcast_fusion = f32[16,12,12,12,12]{0,4,3,1,2:T(8,128)} fusion(bf16[16,12,12,23]{3,2,0,1:T(8,128)(2,1)S(1)} %convolution_bitcast_fusion.2, s32[12,12]{1,0:T(8,128)S(1)} %subtract_add_fusion), kind=kOutput, calls=%fused_computation.2 | convolution fusion | flops 15265008 | bytes 1433664 | tf_op jit(solution)/shard_map/hikb,jlb->hijkl/dot_general | solution.py:47
  66.0 21.9 %copy.141 = f32[16,12,12,12,12]{2,1,4,3,0:T(8,128)} copy(f32[16,12,12,12,12]{0,4,3,1,2:T(8,128)} %convolution_bitcast_fusion) | data formatting | bytes 2654208 | tf_op jit(solution)/shard_map/add | solution.py:84
  87.9 13.5 %reshape.249 = f32[16,144,144]{1,2,0:T(8,128)} reshape(f32[16,12,12,12,12]{2,1,4,3,0:T(8,128)} %copy.141) | data formatting | bytes 2654208 | tf_op jit(solution)/shard_map/add | solution.py:84
  102.7 2.3 fusion.32
  105.0 5.1 %reshape.250 = bf16[3,144,3,16,32]{4,3,2,1,0:T(8,128)(2,1)} reshape(bf16[432,1536]{1,0:T(8,128)(2,1)S(1)} %fusion.32) | data formatting | bytes 2654208 | tf_op jit(solution)/shard_map/reshape | solution.py:80
  110.1 4.8 %fusion.168 = (bf16[3,144,1,16,32]{4,3,2,1,0:T(8,128)(2,1)}, bf16[3,144,1,16,32]{4,3,2,1,0:T(8,128)(2,1)S(1)}, bf16[3,144,1,16,32]{4,3,2,1,0:T(8,128)(2,1)S(1)}) fusion(bf16[3,144,3,16,32]{4,3,2,1,0:T(8,128)(2,1)} %reshape.250), kind=kLoop, calls=%fused_computation.229 | loop fusion | bytes 2654208 | tf_op jit(solution)/shard_map/slice | solution.py:90
  115.0 2.9 %copy.148 = bf16[3,144,1,16,32]{1,4,3,0,2:T(8,128)(2,1)} copy(bf16[3,144,1,16,32]{4,3,2,1,0:T(8,128)(2,1)} %get-tuple-element.10) | data formatting | bytes 884736
  117.9 2.0 copy.149
  121.6 7.4 %fusion.175 = (f32[3,16,144]{2,1,0:T(8,128)S(1)}, f32[3,16,144,144]{2,3,1,0:T(8,128)}) fusion(f32[16,144,144]{1,2,0:T(8,128)} %reshape.248, bf16[3,144,1,16,32]{1,4,3,0,2:T(8,128)(2,1)S(1)} %copy.150, bf16[3,144,1,16,32]{1,4,3,0,2:T(8,128)(2,1)} %copy.149), kind=kOutput, calls=%fused_computation.236 | convolution fusion | flops 67682448 | bytes 6220800 | tf_op jit(solution)/shard_map/sub | solution.py:88
  129.0 3.6 %fusion.40 = bf16[3,144,16,32]{1,3,2,0:T(8,128)(2,1)S(1)} fusion(f32[3,16,144,144]{2,3,1,0:T(8,128)} %get-tuple-element.34, f32[3,16,144]{2,1,0:T(8,128)S(1)} %get-tuple-element.33, bf16[3,144,1,16,32]{1,4,3,0,2:T(8,128)(2,1)S(1)} %copy-done.4), kind=kOutput, calls=%fused_computation.78 | convolution fusion | flops 65912832 | bytes 4893696 | tf_op jit(solution)/shard_map/whqk,wkhe->wqhe/dot_general | solution.py:89
  135.8 16.4 %all-gather.5.cloned.1.call-done = bf16[2,2048,512]{2,1,0:T(8,128)(2,1)} async-done(((bf16[2,128,512]{2,1,0:T(8,128)(2,1)}), bf16[2,2048,512]{2,1,0:T(8,128)(2,1)}) %all-gather.5.cloned.1.call-update) | async-done | bytes 4194320 | tf_op jit(solution)/shard_map/all_gather | solution.py:152
  152.2 11.2 %fusion.47 = bf16[432,512]{1,0:T(8,128)(2,1)S(1)} fusion(f32[432,512]{1,0:T(8,128)S(1)} %get-tuple-element.36, bf16[2,2048,512]{2,1,0:T(8,128)(2,1)} %all-gather.5.cloned.1.call-done, bf16[2,512,4096]{2,1,0:T(8,128)(2,1)} %all-gather.3.cloned.1.call-done, f32[2048]{0:T(1024)S(1)} %bitcast.172, f32[512]{0:T(512)S(1)} %bitcast.177, f32[512]{0:T(512)S(1)} %bitcast.178, ...), kind=kOutput, calls=%fused_computation.85 | convolution fusion | flops 1872101376 | bytes 6424576 | tf_op jit(solution)/shard_map/dot_general | solution.py:133
  166.0 5.8 %collective-permute-done = bf16[6,36,512]{2,1,0:T(8,128)(2,1)S(1)} collective-permute-done((bf16[6,36,512]{2,1,0:T(8,128)(2,1)S(1)}, bf16[6,36,512]{2,1,0:T(8,128)(2,1)S(1)}, u32[]{:S(2)}, u32[]{:S(2)}) %collective-permute-start) | collective-permute-done | bytes 221216 | tf_op jit(solution)/shard_map/ppermute | solution.py:17
  171.9 2.5 collective-permute-done.1
  176.7 2.4 collective-permute-done.2
  181.5 2.3 fusion.33
  183.8 5.1 %reshape.251 = bf16[3,144,3,16,32]{4,3,2,1,0:T(8,128)(2,1)} reshape(bf16[432,1536]{1,0:T(8,128)(2,1)S(1)} %fusion.33) | data formatting | bytes 2654208 | tf_op jit(solution)/shard_map/reshape | solution.py:80
  188.9 4.8 %fusion.167 = (bf16[3,144,1,16,32]{4,3,2,1,0:T(8,128)(2,1)}, bf16[3,144,1,16,32]{4,3,2,1,0:T(8,128)(2,1)S(1)}, bf16[3,144,1,16,32]{4,3,2,1,0:T(8,128)(2,1)S(1)}) fusion(bf16[3,144,3,16,32]{4,3,2,1,0:T(8,128)(2,1)} %reshape.251), kind=kLoop, calls=%fused_computation.228 | loop fusion | bytes 2654208 | tf_op jit(solution)/shard_map/slice | solution.py:90
  193.7 2.9 %copy.152 = bf16[3,144,1,16,32]{1,4,3,0,2:T(8,128)(2,1)} copy(bf16[3,144,1,16,32]{4,3,2,1,0:T(8,128)(2,1)} %get-tuple-element.7) | data formatting | bytes 884736
  196.6 2.0 copy.153
  199.9 2.4 fusion.54
  202.4 4.2 %fusion.185 = (f32[3,16,144]{2,1,0:T(8,128)S(1)}, f32[3,16,144,144]{2,3,1,0:T(8,128)}) fusion(f32[3,16,144,144]{2,3,1,0:T(8,128)S(1)} %fusion.54, f32[16,144,144]{1,2,0:T(8,128)S(1)} %copy-done.2, pred[3,144,144]{1,2,0:T(8,128)(4,1)S(1)} %copy-done.5), kind=kOutput, calls=%fused_computation.238 | output fusion | flops 7962767 | bytes 9379584 | tf_op jit(solution)/shard_map/sub | solution.py:88
  206.5 3.6 %fusion.41 = bf16[3,144,16,32]{1,3,2,0:T(8,128)(2,1)S(1)} fusion(f32[3,16,144,144]{2,3,1,0:T(8,128)} %get-tuple-element.38, f32[3,16,144]{2,1,0:T(8,128)S(1)} %get-tuple-element.37, bf16[3,144,1,16,32]{1,4,3,0,2:T(8,128)(2,1)S(1)} %copy-done.3), kind=kOutput, calls=%fused_computation.79 | convolution fusion | flops 65912832 | bytes 4893696 | tf_op jit(solution)/shard_map/whqk,wkhe->wqhe/dot_general | solution.py:89
  213.6 11.2 %fusion.46 = bf16[432,512]{1,0:T(8,128)(2,1)S(1)} fusion(f32[432,512]{1,0:T(8,128)S(1)} %get-tuple-element.40, bf16[2,2048,512]{2,1,0:T(8,128)(2,1)} %all-gather.5.cloned.1.call-done, bf16[2,512,4096]{2,1,0:T(8,128)(2,1)} %all-gather.3.cloned.1.call-done, f32[2048]{0:T(1024)S(1)} %bitcast.171, f32[512]{0:T(512)S(1)} %bitcast.176, f32[512]{0:T(512)S(1)} %bitcast.175, ...), kind=kOutput, calls=%fused_computation.84 | convolution fusion | flops 1872101376 | bytes 6424576 | tf_op jit(solution)/shard_map/dot_general | solution.py:133
  225.1 2.7 %collective-permute-start.3 = (bf16[6,36,512]{2,1,0:T(8,128)(2,1)S(1)}, bf16[6,36,512]{2,1,0:T(8,128)(2,1)S(1)}, u32[]{:S(2)}, u32[]{:S(2)}) collective-permute-start(bf16[6,36,512]{2,1,0:T(8,128)(2,1)S(1)} %slice.182), channel_id=1, source_target_pairs={{0,32},{32,64},{64,96},{96,128},{128,160},{160,192},{192,224},{224... | collective-permute-start | bytes 663560 | tf_op jit(solution)/shard_map/ppermute | solution.py:17
  228.1 5.5 %collective-permute-done.3 = bf16[6,36,512]{2,1,0:T(8,128)(2,1)S(1)} collective-permute-done((bf16[6,36,512]{2,1,0:T(8,128)(2,1)S(1)}, bf16[6,36,512]{2,1,0:T(8,128)(2,1)S(1)}, u32[]{:S(2)}, u32[]{:S(2)}) %collective-permute-start.3) | collective-permute-done | bytes 221216 | tf_op jit(solution)/shard_map/ppermute | solution.py:17
  233.7 3.0 %collective-permute-done.4 = bf16[6,36,512]{2,1,0:T(8,128)(2,1)S(1)} collective-permute-done((bf16[6,36,512]{2,1,0:T(8,128)(2,1)S(1)}, bf16[6,36,512]{2,1,0:T(8,128)(2,1)S(1)}, u32[]{:S(2)}, u32[]{:S(2)}) %collective-permute-start.4) | collective-permute-done | bytes 221216 | tf_op jit(solution)/shard_map/ppermute | solution.py:20
  237.0 8.6 %collective-permute-done.5 = bf16[24,6,512]{2,1,0:T(8,128)(2,1)S(1)} collective-permute-done((bf16[24,6,512]{2,1,0:T(8,128)(2,1)S(1)}, bf16[24,6,512]{2,1,0:T(8,128)(2,1)S(1)}, u32[]{:S(2)}, u32[]{:S(2)}) %collective-permute-start.5) | collective-permute-done | bytes 147488 | tf_op jit(solution)/shard_map/ppermute | solution.py:17
  (127 shorter events, 27.4 us)
Async XLA Ops:
  6.5 96.1 %all-gather.3.cloned.1.call-start = ((), (), s32[]{:S(2)}) async-start(), calls=%async_computation | async-start | bytes 8912896 | tf_op jit(solution)/shard_map/all_gather | solution.py:27
  8.4 3.4 %copy-start.10 = (f32[2,2,512]{2,1,0:T(2,128)S(1)}, f32[2,2,512]{2,1,0:T(2,128)}, u32[]{:S(2)}) copy-start(f32[2,2,512]{2,1,0:T(2,128)} %param.15) | copy-start | bytes 24580
  8.5 4.0 %copy-start.6 = (f32[2,4,512]{2,1,0:T(4,128)S(1)}, f32[2,4,512]{2,1,0:T(4,128)}, u32[]{:S(2)}) copy-start(f32[2,4,512]{2,1,0:T(4,128)} %param.16) | copy-start | bytes 49156
  8.5 143.7 %all-gather.5.cloned.1.call-start = ((), (), s32[]{:S(2)}) async-start(), calls=%async_computation.1 | async-start | bytes 4456448 | tf_op jit(solution)/shard_map/all_gather | solution.py:152
  87.9 13.5 %copy-start.8 = (f32[2,1536]{1,0:T(2,128)S(1)}, f32[2,1536]{1,0:T(2,128)}, u32[]{:S(2)}) copy-start(f32[2,1536]{1,0:T(2,128)} %param.17) | copy-start | bytes 36868
  87.9 14.2 %copy-start.7 = (f32[2,2048]{1,0:T(2,128)S(1)}, f32[2,2048]{1,0:T(2,128)}, u32[]{:S(2)}) copy-start(f32[2,2048]{1,0:T(2,128)} %param.18) | copy-start | bytes 49156
  121.6 7.4 %copy-start.4 = (bf16[3,144,1,16,32]{1,4,3,0,2:T(8,128)(2,1)S(1)}, bf16[3,144,1,16,32]{1,4,3,0,2:T(8,128)(2,1)}, u32[]{:S(2)}) copy-start(bf16[3,144,1,16,32]{1,4,3,0,2:T(8,128)(2,1)} %copy.148) | copy-start | bytes 1327108
  129.0 5.0 %copy-start.13 = (f32[1,1,512]{2,1,0:T(1,128)S(1)}, f32[1,1,512]{2,1,0:T(1,128)}, u32[]{:S(2)}) copy-start(f32[1,1,512]{2,1,0:T(1,128)} %get-tuple-element.24) | copy-start | bytes 6148
  132.6 1.3 copy-start
  132.6 19.6 %copy-start.12 = (f32[1,2048]{1,0:T(1,128)S(1)}, f32[1,2048]{1,0:T(1,128)}, u32[]{:S(2)}) copy-start(f32[1,2048]{1,0:T(1,128)} %get-tuple-element.28) | copy-start | bytes 24580
  132.6 19.6 %copy-start.17 = (f32[1,1,512]{2,1,0:T(1,128)S(1)}, f32[1,1,512]{2,1,0:T(1,128)}, u32[]{:S(2)}) copy-start(f32[1,1,512]{2,1,0:T(1,128)} %get-tuple-element.22) | copy-start | bytes 6148
  132.6 19.5 %copy-start.18 = (f32[1,1,512]{2,1,0:T(1,128)S(1)}, f32[1,1,512]{2,1,0:T(1,128)}, u32[]{:S(2)}) copy-start(f32[1,1,512]{2,1,0:T(1,128)} %get-tuple-element.23) | copy-start | bytes 6148
  132.6 19.5 %copy-start.20 = (f32[1,1,512]{2,1,0:T(1,128)S(1)}, f32[1,1,512]{2,1,0:T(1,128)}, u32[]{:S(2)}) copy-start(f32[1,1,512]{2,1,0:T(1,128)} %get-tuple-element.30) | copy-start | bytes 6148
  163.4 1.9 copy-start.14
  163.6 8.2 %collective-permute-start = (bf16[6,36,512]{2,1,0:T(8,128)(2,1)S(1)}, bf16[6,36,512]{2,1,0:T(8,128)(2,1)S(1)}, u32[]{:S(2)}, u32[]{:S(2)}) collective-permute-start(bf16[6,36,512]{2,1,0:T(8,128)(2,1)S(1)} %slice.160), channel_id=1, source_target_pairs={{0,32},{32,64},{64,96},{96,128},{128,160},{160,192},{192,224},{224... | collective-permute-start | bytes 663560 | tf_op jit(solution)/shard_map/ppermute | solution.py:17
  165.4 8.9 %collective-permute-start.1 = (bf16[6,36,512]{2,1,0:T(8,128)(2,1)S(1)}, bf16[6,36,512]{2,1,0:T(8,128)(2,1)S(1)}, u32[]{:S(2)}, u32[]{:S(2)}) collective-permute-start(bf16[6,36,512]{2,1,0:T(8,128)(2,1)S(1)} %slice.162), channel_id=1, source_target_pairs={{32,0},{64,32},{96,64},{128,96},{160,128},{192,160},{224,192},{0,2... | collective-permute-start | bytes 663560 | tf_op jit(solution)/shard_map/ppermute | solution.py:20
  174.4 4.7 %collective-permute-start.2 = (bf16[24,6,512]{2,1,0:T(8,128)(2,1)S(1)}, bf16[24,6,512]{2,1,0:T(8,128)(2,1)S(1)}, u32[]{:S(2)}, u32[]{:S(2)}) collective-permute-start(bf16[24,6,512]{2,1,0:T(8,128)(2,1)S(1)} %slice.196), channel_id=1, source_target_pairs={{2,0},{4,2},{6,4},{8,6},{10,8},{12,10},{14,12},{16,14},{18,16},{20... | collective-permute-start | bytes 442376 | tf_op jit(solution)/shard_map/ppermute | solution.py:20
  180.2 1.3 copy-start.9
  199.9 2.4 copy-start.2
  199.9 2.4 copy-start.5
  202.4 4.2 %copy-start.3 = (bf16[3,144,1,16,32]{1,4,3,0,2:T(8,128)(2,1)S(1)}, bf16[3,144,1,16,32]{1,4,3,0,2:T(8,128)(2,1)}, u32[]{:S(2)}) copy-start(bf16[3,144,1,16,32]{1,4,3,0,2:T(8,128)(2,1)} %copy.152) | copy-start | bytes 1327108
  210.2 1.5 copy-start.1
  210.2 3.4 %copy-start.11 = (f32[1,2048]{1,0:T(1,128)S(1)}, f32[1,2048]{1,0:T(1,128)}, u32[]{:S(2)}) copy-start(f32[1,2048]{1,0:T(1,128)} %get-tuple-element.27) | copy-start | bytes 24580
  210.2 3.4 %copy-start.15 = (f32[1,1,512]{2,1,0:T(1,128)S(1)}, f32[1,1,512]{2,1,0:T(1,128)}, u32[]{:S(2)}) copy-start(f32[1,1,512]{2,1,0:T(1,128)} %get-tuple-element.19) | copy-start | bytes 6148
  210.2 3.4 %copy-start.16 = (f32[1,1,512]{2,1,0:T(1,128)S(1)}, f32[1,1,512]{2,1,0:T(1,128)}, u32[]{:S(2)}) copy-start(f32[1,1,512]{2,1,0:T(1,128)} %get-tuple-element.26) | copy-start | bytes 6148
  210.2 3.4 %copy-start.19 = (f32[1,1,512]{2,1,0:T(1,128)S(1)}, f32[1,1,512]{2,1,0:T(1,128)}, u32[]{:S(2)}) copy-start(f32[1,1,512]{2,1,0:T(1,128)} %get-tuple-element.29) | copy-start | bytes 6148
  225.1 8.6 %collective-permute-start.3 = (bf16[6,36,512]{2,1,0:T(8,128)(2,1)S(1)}, bf16[6,36,512]{2,1,0:T(8,128)(2,1)S(1)}, u32[]{:S(2)}, u32[]{:S(2)}) collective-permute-start(bf16[6,36,512]{2,1,0:T(8,128)(2,1)S(1)} %slice.182), channel_id=1, source_target_pairs={{0,32},{32,64},{64,96},{96,128},{128,160},{160,192},{192,224},{224... | collective-permute-start | bytes 663560 | tf_op jit(solution)/shard_map/ppermute | solution.py:17
  228.0 8.7 %collective-permute-start.4 = (bf16[6,36,512]{2,1,0:T(8,128)(2,1)S(1)}, bf16[6,36,512]{2,1,0:T(8,128)(2,1)S(1)}, u32[]{:S(2)}, u32[]{:S(2)}) collective-permute-start(bf16[6,36,512]{2,1,0:T(8,128)(2,1)S(1)} %slice.184), channel_id=1, source_target_pairs={{32,0},{64,32},{96,64},{128,96},{160,128},{192,160},{224,192},{0,2... | collective-permute-start | bytes 663560 | tf_op jit(solution)/shard_map/ppermute | solution.py:20
  236.8 8.8 %collective-permute-start.5 = (bf16[24,6,512]{2,1,0:T(8,128)(2,1)S(1)}, bf16[24,6,512]{2,1,0:T(8,128)(2,1)S(1)}, u32[]{:S(2)}, u32[]{:S(2)}) collective-permute-start(bf16[24,6,512]{2,1,0:T(8,128)(2,1)S(1)} %slice.206), channel_id=1, source_target_pairs={{0,2},{2,4},{4,6},{6,8},{8,10},{10,12},{12,14},{14,16},{16,18},{18... | collective-permute-start | bytes 442376 | tf_op jit(solution)/shard_map/ppermute | solution.py:17
Sparse Core Ops, SparseCore 0:
  10.1 80.1 all-gather.2
  93.0 59.1 all-gather.4
where the time goes:
time: 258 us; the launch traced here: 254 us
  local copies, waits for them, and re-layouts  116 us (45%)
  matrix products  62 us (24%)
  waiting for transfers between devices  44.9 us (17%)
  between operations  14.3 us (6%)
  other arithmetic  9.97 us (4%)
  starting transfers between devices  6.79 us (3%)
    add x4, local copies, waits for them, and re-layouts, window_attention(): scores = scores / jnp.sqrt(jnp.float32(head_dim)) + position[None]  71.1 us
    dot_general x2, matrix products, swin_block(): jnp.dot(hidden, matrix(3, layer), preferred_element_type=jnp.float32)  22.4 us
    ppermute x3, waiting for transfers between devices, extended(): lax.ppermute(lax.slice_in_dim(block, block.shape[dim] - width, None, axis...  20 us
    all_gather x1, waiting for transfers between devices, local(): lax.all_gather(output_weight, 'col', axis=1, tiled=True)  16.4 us
    dot_general x2, matrix products, bias_table(): picked = jnp.einsum('hikb,jlb->hijkl', partial_rows, onehot)  14 us
    unnamed x52, local copies, waits for them, and re-layouts  12.9 us
    reshape x2, local copies, waits for them, and re-layouts, window_attention(): qkv = qkv.reshape(nwin, WIN * WIN, 3, HEADS, head_dim)  10.2 us
    slice x2, local copies, waits for them, and re-layouts, window_attention(): qkv[:, :, 2]  9.66 us
  transfers between devices with their start and end apart: 8, of which 7 were waited for; matrix products, arithmetic and copies ran while one was open for 50% of the time, Pallas kernels for 0%

commit v1 on v0

v1 whole, which is shorter than its diff:
```python
import math

import jax
import jax.numpy as jnp
import numpy as np
from jax import lax
from jax.experimental import pallas as pl
from jax.experimental.pallas import tpu as pltpu
from jax.sharding import PartitionSpec as P


HEADS = 16
WIN = 12
SHIFT = 6
D = 512
FF = 2048
HD = 32
KEYS = WIN * WIN
NWIN = 3
TOK = KEYS * NWIN
LOG2E = math.log2(math.e)
BF = jnp.bfloat16
F32 = jnp.float32
VMEM_LIMIT = 60 * 1024 * 1024
NT = (((1,), (1,)), ((), ()))
NN = (((1,), (0,)), ((), ()))
AXES = ("row", "x", "yh", "c", "img")
SIZES = (8, 4, 2, 2, 2)


def dot(a, b, dims=NN):
    return lax.dot_general(a, b, dims, preferred_element_type=F32)


def layer_norm(values, gain, shift):
    center = values - jnp.mean(values, -1, keepdims=True)
    spread = jnp.mean(center * center, -1, keepdims=True)
    return center * lax.rsqrt(spread + 1e-05) * gain + shift


def bias_kernel(masked, t_ref, side_ref, out_ref, rows, mask):
    lane = lax.broadcasted_iota(jnp.int32, (HEADS, 128), 1)
    n_off = 2 * WIN - 1
    for cb in range(WIN):
        tiles = [jnp.zeros((HEADS, 128), F32) for _ in range(3)]
        for ro in range(n_off):
            moved = pltpu.roll(t_ref[ro], (ro * WIN - (WIN - 1 - cb)) % 128, 1)
            for tile in range(ro * WIN // 128, (ro * WIN + WIN - 1) // 128 + 1):
                low = ro * WIN - tile * 128
                tiles[tile] = jnp.where((lane >= low) & (lane < low + WIN), moved, tiles[tile])
        for tile in range(3):
            rows[tile, (cb + 4) * HEADS : (cb + 5) * HEADS, :] = tiles[tile] * LOG2E
    if masked:
        last_row = (lax.axis_index("row") == 7).astype(F32)
        col = (lax.axis_index("x") * 2 + lax.axis_index("yh")) * 2 + lax.axis_index("c")
        last_col = (col == 15).astype(F32)
        below = side_ref[0:1, :TOK]
        right = side_ref[1:2, :TOK]
        here = side_ref[2:3, :TOK]
        key_right = (lax.broadcasted_iota(jnp.int32, (WIN, 1), 0) >= SHIFT).astype(F32)
        across = last_col * here * jnp.abs(right - key_right)
        for rb in range(WIN):
            down = last_row * jnp.abs(below - (1.0 if rb >= SHIFT else 0.0))
            mask[rb * WIN : (rb + 1) * WIN, :] = jnp.maximum(across, down) * -1e9
    lane = lax.broadcasted_iota(jnp.int32, (16, 128), 1)
    upper = lax.broadcasted_iota(jnp.int32, (8, 128), 0) < 4

    def one_line(mine, at, t):
        value = None
        for w in range(NWIN):
            for s in range(3):
                low = max(KEYS * w, s * 128 + KEYS * w - at) - t * 128
                high = min(KEYS * (w + 1), (s + 1) * 128 + KEYS * w - at) - t * 128
                if max(low, 0) >= min(high, 128):
                    continue
                moved = pltpu.roll(mine[s], (KEYS * w - at) % 128, 1)
                value = moved if value is None else jnp.where(lane >= low, moved, value)
        return value

    def one_head(h, carry):
        even = [rows[tile, pl.ds(h + 4 * HEADS, 16, stride=HEADS), :] for tile in range(3)]
        odd = [rows[tile, pl.ds(h, 16, stride=HEADS), :] for tile in range(3)]
        for pair_at in range(WIN // 2):
            for t in range(4):
                first = one_line(even, (WIN - 1 - 2 * pair_at) * WIN, t)
                second = one_line(odd, (WIN - 2 - 2 * pair_at) * WIN, t)
                whole = jnp.concatenate(
                    [first[:8], jnp.where(upper, first[8:], second[:8]), second[8:]], axis=0)
                width = min(TOK - t * 128, 128)
                at = slice(pair_at * 24, (pair_at + 1) * 24), slice(t * 128, t * 128 + width)
                whole = whole[:, :width]
                if masked:
                    whole = whole + mask[at[0], at[1]]
                out_ref[h, at[0], at[1]] = whole
        return carry

    lax.fori_loop(0, HEADS, one_head, 0)


def bias_table(t, masked, after=()):
    vm = pl.BlockSpec(memory_space=pltpu.VMEM)
    at = np.arange(512)
    side = np.zeros((8, 512), np.float32)
    side[0] = at % KEYS >= SHIFT * WIN
    side[1] = at % WIN >= SHIFT
    side[2] = (at >= 2 * KEYS) & (at < TOK)

    def body(*refs):
        bias_kernel(masked, refs[0], refs[1], *refs[-3:])

    return pl.pallas_call(
        body,
        out_shape=jax.ShapeDtypeStruct((HEADS, KEYS, TOK), F32),
        in_specs=[vm, vm] + [pl.BlockSpec(memory_space=pl.ANY)] * len(after),
        out_specs=vm,
        scratch_shapes=[pltpu.VMEM((3, 20 * HEADS, 128), F32), pltpu.VMEM((KEYS, TOK), F32)],
        compiler_params=pltpu.CompilerParams(vmem_limit_bytes=VMEM_LIMIT),
        name="bias_table",
    )(t, jnp.asarray(side), *after)


def fetch_blocks(refs, tags, first, count, dst, sem, whole):
    core = lax.axis_index("c")
    my_yh = lax.axis_index("yh")
    my_x = lax.axis_index("x")
    copies = []
    for ref, (kind, flip, shift) in zip(refs, tags):
        c = 1 - core if flip else core
        for i in range(ref.shape[0]):
            if kind == "x":
                col = i * 4 + (1 - my_yh if shift else my_yh) * 2 + c
            else:
                col = lax.rem(my_x + 4 - shift, 4) * 4 + i * 2 + c
            if whole:
                to = dst.at[col]
            else:
                to = dst.at[:, pl.ds(pl.multiple_of(col * 32, 32), 32), :]
            copy = pltpu.make_async_copy(ref.at[i, pl.ds(first, count)], to, sem)
            copy.start()
            copies.append(copy)
    return copies


def attn_kernel(n_pieces, layer, tags, assemble, first, *refs):
    n_w = len(tags)
    pieces = refs[:n_pieces]
    wrefs = refs[n_pieces : n_pieces + n_w]
    (perm_ref, permt_ref, bq_all, gain_ref, mbias_ref, bt_ref, ho_ref,
     xs, qs, ks, vts, ots, bts, w_ref, sem) = refs[n_pieces + n_w :]
    bq_ref = bq_all.at[layer : layer + 1]
    weights = fetch_blocks(wrefs, tags, first, 3, w_ref, sem.at[0], False)
    fetch = pltpu.make_async_copy(bt_ref, bts, sem.at[1])
    fetch.start()
    assemble(pieces, xs)
    normed = layer_norm(xs[...], gain_ref[layer, 0:1], mbias_ref[layer, 0:1]).astype(BF)
    nw = dot(perm_ref[...], normed).astype(BF)
    for copy in weights:
        copy.wait()
    scale = LOG2E / math.sqrt(HD)
    for kind in range(2):
        y = dot(nw, w_ref[kind]) + bq_ref[:, kind * D : (kind + 1) * D]
        if kind == 0:
            y = y * scale
        dst = qs if kind == 0 else ks
        for w in range(NWIN):
            rows = slice(w * KEYS, (w + 1) * KEYS)
            for g in range(4):
                tile = y[rows, g * 128 : (g + 1) * 128]
                if w:
                    tile = pltpu.roll(tile, HD * w, 1)
                dst[rows, g * 128 : (g + 1) * 128] = tile.astype(BF)
    v = (dot(nw, w_ref[2]) + bq_ref[:, 2 * D :]).astype(BF)
    eye = (lax.broadcasted_iota(jnp.int32, (128, 128), 0)
           == lax.broadcasted_iota(jnp.int32, (128, 128), 1)).astype(BF)
    for w in range(NWIN):
        for g in range(4):
            vt = dot(eye, v[w * KEYS : (w + 1) * KEYS, g * 128 : (g + 1) * 128], NT).astype(BF)
            for hh in range(4):
                vts[g * 4 + hh, w * HD : (w + 1) * HD, :] = vt[hh * HD : (hh + 1) * HD]
    for h in range(HEADS):
        vts[h, NWIN * HD :, :] = jnp.ones((16, KEYS), BF)
    lane_slot = lax.broadcasted_iota(jnp.int32, (1, 128), 1) // HD
    slot = [(lane_slot == s).astype(F32).astype(BF) for s in range(4)]
    win = lax.broadcasted_iota(jnp.int32, (1, TOK), 1)
    fetch.wait()
    for h in range(HEADS):
        g, hh = divmod(h, 4)
        lanes = slice(g * 128, (g + 1) * 128)
        kcat = ks[0:KEYS, lanes] * slot[hh]
        for w in range(1, NWIN):
            kcat = kcat + ks[w * KEYS : (w + 1) * KEYS, lanes] * slot[(hh + w) % 4]
        qbd = jnp.concatenate(
            [qs[w * KEYS : (w + 1) * KEYS, lanes] * slot[(hh + w) % 4] for w in range(NWIN)], axis=0)
        st = dot(kcat, qbd, NT) + bts[h]
        p = jnp.exp2(st - jnp.max(st, axis=0, keepdims=True)).astype(BF)
        o = dot(vts[h], p)
        mine = jnp.where(win < KEYS, o[0:HD], jnp.where(win < 2 * KEYS, o[HD : 2 * HD], o[2 * HD : 3 * HD]))
        ots[h * HD : (h + 1) * HD, :] = (mine * (1.0 / o[3 * HD : 3 * HD + 1])).astype(BF)
    ho_ref[...] = dot(permt_ref[...], ots[...], NT).astype(BF)


def attention(layer, pieces, assemble, weights, perm, permt, bq, gain, mbias, bt):
    (blocks, tags), first = weights
    n, m = len(pieces), len(blocks)
    hbm = pl.BlockSpec(memory_space=pl.ANY)
    vm = pl.BlockSpec(memory_space=pltpu.VMEM)
    return pl.pallas_call(
        lambda *refs: attn_kernel(n, layer, tags, assemble, first, *refs),
        out_shape=jax.ShapeDtypeStruct((TOK, D), BF),
        in_specs=[vm] * n + [hbm] * m + [vm] * 5 + [hbm],
        out_specs=vm,
        scratch_shapes=[
            pltpu.VMEM((TOK, D), F32),
            pltpu.VMEM((TOK, D), BF),
            pltpu.VMEM((TOK, D), BF),
            pltpu.VMEM((HEADS, NWIN * HD + 16, KEYS), BF),
            pltpu.VMEM((D, TOK), BF),
            pltpu.VMEM((HEADS, KEYS, TOK), F32),
            pltpu.VMEM((3, D, D), BF),
            pltpu.SemaphoreType.DMA((2,)),
        ],
        compiler_params=pltpu.CompilerParams(vmem_limit_bytes=VMEM_LIMIT),
        cost_estimate=pl.CostEstimate(flops=10_000_000_000, bytes_accessed=8_000_000, transcendentals=0),
        name="attention",
    )(*pieces, *blocks, perm, permt, bq, gain, mbias, bt)


def mlp_kernel(n_pieces, layer, tags, firsts, assemble, finish, *refs):
    pieces = refs[:n_pieces]
    ho_ref, bh_all, gain_ref, mbias_ref = refs[n_pieces : n_pieces + 4]
    bh_ref = bh_all.at[layer : layer + 1]
    at = n_pieces + 4
    blocks = []
    for group in tags:
        blocks.append(refs[at : at + len(group)])
        at += len(group)
    outs = refs[at:-6]
    xs, acc, wp_ref, wh_ref, wo_ref, sem = refs[-6:]
    proj = fetch_blocks(blocks[0], tags[0], firsts[0], 1, wp_ref, sem.at[0], False)
    up = fetch_blocks(blocks[1], tags[1], firsts[1], 4, wh_ref, sem.at[1], False)
    down = fetch_blocks(blocks[2], tags[2], firsts[2], 4, wo_ref, sem.at[2], True)
    assemble(pieces, xs)
    for copy in proj:
        copy.wait()
    mid = xs[...] + (dot(ho_ref[...], wp_ref[0]) + mbias_ref[layer, 2:3])
    xs[...] = mid
    n2 = layer_norm(mid, gain_ref[layer, 1:2], mbias_ref[layer, 1:2]).astype(BF)
    step = 512
    for copy in up:
        copy.wait()
    for c in range(FF // step):
        cols = slice(c * step, (c + 1) * step)
        z = dot(n2, wh_ref[c]) + bh_ref[:, cols]
        hid = (0.5 * z * (1.0 + lax.erf(z * math.sqrt(0.5)))).astype(BF)
        if c == 0:
            for copy in down:
                copy.wait()
        part = dot(hid, wo_ref[4 * c : 4 * c + 4].reshape(step, D))
        acc[...] = part if c == 0 else acc[...] + part
    xs[...] = xs[...] + (acc[...] + mbias_ref[layer, 3:4])
    finish(xs, outs)


def mlp(layer, pieces, assemble, finish, weights, ho, bh, gain, mbias):
    outs = part_shapes()
    tags = [group[1] for group, _ in weights]
    firsts = [first for _, first in weights]
    blocks = [b for group, _ in weights for b in group[0]]
    n = len(pieces)
    vm = pl.BlockSpec(memory_space=pltpu.VMEM)
    return pl.pallas_call(
        lambda *refs: mlp_kernel(n, layer, tags, firsts, assemble, finish, *refs),
        out_shape=outs,
        in_specs=[vm] * (n + 4) + [pl.BlockSpec(memory_space=pl.ANY)] * len(blocks),
        out_specs=[vm] * len(outs),
        scratch_shapes=[
            pltpu.VMEM((TOK, D), F32),
            pltpu.VMEM((TOK, D), F32),
            pltpu.VMEM((1, D, D), BF),
            pltpu.VMEM((4, D, D), BF),
            pltpu.VMEM((16, 4, 32, D), BF),
            pltpu.SemaphoreType.DMA((3,)),
        ],
        compiler_params=pltpu.CompilerParams(vmem_limit_bytes=VMEM_LIMIT),
        cost_estimate=pl.CostEstimate(flops=10_000_000_000, bytes_accessed=8_000_000, transcendentals=0),
        name="mlp",
    )(*pieces, ho, bh, gain, mbias, *blocks)


ROWS = WIN
COLS = WIN * NWIN
KEEP = COLS - SHIFT


def assemble_plain(pieces, xs):
    for r in range(ROWS):
        xs[r * COLS : (r + 1) * COLS, :] = pieces[0][r].astype(F32)


def assemble_shifted(pieces, xs):
    own, right, below, corner = pieces
    for r in range(SHIFT):
        xs[r * COLS : r * COLS + KEEP, :] = own[r].astype(F32)
        xs[r * COLS + KEEP : (r + 1) * COLS, :] = right[r].astype(F32)
        at = (r + SHIFT) * COLS
        xs[at : at + KEEP, :] = below[r].astype(F32)
        xs[at + KEEP : at + COLS, :] = corner[r].astype(F32)


def finish_first(xs, outs):
    own, right, below, corner = outs
    for r in range(SHIFT):
        top = xs[r * COLS : (r + 1) * COLS, :].astype(BF)
        below[r] = top[SHIFT:]
        corner[r] = top[:SHIFT]
        low = xs[(r + SHIFT) * COLS : (r + SHIFT + 1) * COLS, :].astype(BF)
        own[r] = low[SHIFT:]
        right[r] = low[:SHIFT]


def finish_second(xs, outs):
    own, right, below, corner = outs
    for r in range(SHIFT):
        top = xs[r * COLS : (r + 1) * COLS, :].astype(BF)
        own[r] = top[:KEEP]
        right[r] = top[KEEP:]
        low = xs[(r + SHIFT) * COLS : (r + SHIFT + 1) * COLS, :].astype(BF)
        below[r] = low[:KEEP]
        corner[r] = low[KEEP:]


def join_kernel(own, right, below, corner, out):
    for r in range(SHIFT):
        out[r] = jnp.concatenate([corner[r].astype(F32), below[r].astype(F32)], axis=0).astype(BF)
        out[r + SHIFT] = jnp.concatenate([right[r].astype(F32), own[r].astype(F32)], axis=0).astype(BF)


def join(*pieces):
    return pl.pallas_call(
        join_kernel,
        out_shape=jax.ShapeDtypeStruct((ROWS, COLS, D), BF),
        name="join",
    )(*pieces)


def part_shapes():
    return (
        jax.ShapeDtypeStruct((SHIFT, KEEP, D), BF),
        jax.ShapeDtypeStruct((SHIFT, SHIFT, D), BF),
        jax.ShapeDtypeStruct((SHIFT, KEEP, D), BF),
        jax.ShapeDtypeStruct((SHIFT, SHIFT, D), BF),
    )


def permutations():
    perm = np.zeros((TOK, TOK), np.float32)
    for r in range(ROWS):
        for c in range(COLS):
            perm[(c // WIN) * KEYS + r * WIN + c % WIN, r * COLS + c] = 1
    return jnp.asarray(perm, BF), jnp.asarray(perm.T, BF)


def bias_rows(table):
    return jnp.pad(table.transpose(0, 2, 1, 3), ((0, 0), (0, 0), (0, 0), (0, 128 - (2 * WIN - 1))))


def send(block, where):
    pairs = []
    for at in np.ndindex(*SIZES):
        row, x, yh, c, img = at
        row2, x2, y2, c2 = where(row, x, yh * 2 + img, c)
        to = (row2 % 8, x2 % 4, y2 % 4 // 2, c2, y2 % 2)
        pairs.append((int(np.ravel_multi_index(at, SIZES)), int(np.ravel_multi_index(to, SIZES))))
    return lax.ppermute(block, AXES, pairs)


def shift_tokens(block, rows, cols):
    def where(row, x, y, c):
        col = (x * 4 + y // 2 * 2 + c + cols) % 16
        return row + rows, col // 4, col // 2 % 2 * 2 + y % 2, col % 2

    return send(block, where)


def swap_cores(block):
    return send(block, lambda row, x, y, c: (row, x, y, 1 - c))


def chunk_kernel(picks, n_after, qkv, proj, hidden, output, *refs):
    outs = refs[n_after:]
    arrays = (qkv, proj, hidden, output)
    for out, group in zip(outs, picks):
        at = 0
        for layer, which in group:
            ref = arrays[which]
            for rows in range(ref.shape[1] // 32):
                for lanes in range(ref.shape[2] // D):
                    out[at] = ref[layer, rows * 32 : (rows + 1) * 32, lanes * D : (lanes + 1) * D]
                    at += 1


def chunks(picks, weights, after=()):
    sizes = [w.shape[1] // 32 * (w.shape[2] // D) for w in weights]
    counts = [sum(sizes[which] for _, which in group) for group in picks]
    return pl.pallas_call(
        lambda *refs: chunk_kernel(picks, len(after), *refs),
        out_shape=[jax.ShapeDtypeStruct((n, 32, D), BF) for n in counts],
        in_specs=[pl.BlockSpec(memory_space=pltpu.VMEM)] * 4 + [pl.BlockSpec(memory_space=pl.ANY)] * len(after),
        name="chunks",
    )(*weights, *after)


X_MOVES = (1, 3, 2)


def join_x_kernel(n_after, own, *refs):
    came, out, sem = refs[:3], refs[3 + n_after], refs[-1]
    x = lax.axis_index("x")
    copies = []
    for k, ref in enumerate((own, *came)):
        slot = x if k == 0 else lax.rem(x + 4 - X_MOVES[k - 1], 4)
        copies.append(pltpu.make_async_copy(ref, out.at[slot], sem.at[k]))
    for copy in copies:
        copy.start()
    for copy in copies:
        copy.wait()


def join_x(own, came, after):
    hbm = pl.BlockSpec(memory_space=pl.ANY)
    return pl.pallas_call(
        lambda *refs: join_x_kernel(len(after), *refs),
        out_shape=jax.ShapeDtypeStruct((4, *own.shape), BF),
        in_specs=[pl.BlockSpec(memory_space=pltpu.VMEM)] * 4 + [hbm] * len(after),
        out_specs=hbm,
        scratch_shapes=[pltpu.SemaphoreType.DMA((4,))],
        name="join_x",
    )(own, *came, *after)


def pair_kernel(own, other, *refs):
    out, sem = refs[-2:]
    yh = lax.axis_index("yh")
    copies = [
        pltpu.make_async_copy(own, out.at[yh], sem.at[0]),
        pltpu.make_async_copy(other, out.at[1 - yh], sem.at[1]),
    ]
    for copy in copies:
        copy.start()
    for copy in copies:
        copy.wait()


def pair(own, other, after):
    hbm = pl.BlockSpec(memory_space=pl.ANY)
    return pl.pallas_call(
        pair_kernel,
        out_shape=jax.ShapeDtypeStruct((2, *own.shape), BF),
        in_specs=[pl.BlockSpec(memory_space=pltpu.VMEM)] * 2 + [hbm] * len(after),
        out_specs=hbm,
        scratch_shapes=[pltpu.SemaphoreType.DMA((2,))],
        name="pair",
    )(own, other, *after)


def along_x(block):
    return [send(block, lambda row, x, y, c, dx=dx: (row, x + dx, y, c)) for dx in X_MOVES]


def across_y(block):
    return send(block, lambda row, x, y, c: (row, x, 3 - y, c))


def spread_pair(both, came):
    blocks, tags = [], []
    for dx, block in zip((0, *X_MOVES), (both, *came)):
        blocks += [block, swap_cores(block)]
        tags += [("yh", 0, dx), ("yh", 1, dx)]
    return blocks, tags


def local(
    tokens,
    qkv_weight,
    proj_weight,
    hidden_weight,
    output_weight,
    norm_gain,
    model_bias,
    qkv_bias,
    hidden_bias,
    position_bias,
):
    weights = (qkv_weight, proj_weight, hidden_weight, output_weight)
    first, rest = chunks((((0, 0),), ((0, 1), (0, 2), (0, 3))), weights)
    rows = bias_rows(position_bias)
    first_y = across_y(first)
    rest_x = along_x(rest)
    first = pair(first, first_y, ())
    first_x = along_x(first)
    qkv0 = spread_pair(first, first_x)
    (second,) = chunks((((1, 0), (1, 1), (1, 2), (1, 3)),), weights, (first,))
    second_y = across_y(second)
    table0 = bias_table(rows[0], False, (second,))
    mine = join_x(rest, rest_x, (table0,))
    other = across_y(mine)
    second = pair(second, second_y, (mine,))
    second_x = along_x(second)
    perm, permt = permutations()

    def attn(k, pieces, assemble, blocks, table):
        params = (qkv_bias, norm_gain, model_bias, table)
        return attention(k, pieces, assemble, blocks, perm, permt, *params)

    def feed(k, pieces, assemble, finish, blocks, ho):
        return mlp(k, pieces, assemble, finish, blocks, ho, hidden_bias, norm_gain, model_bias)

    ho = attn(0, (tokens,), assemble_plain, (qkv0, 0), table0)
    table1 = bias_table(rows[1], True, (ho,))
    rest0 = (mine, swap_cores(mine), other, swap_cores(other)), (("x", 0, 0), ("x", 1, 0), ("x", 0, 1), ("x", 1, 1))
    own, right, below, corner = feed(
        0, (tokens,), assemble_plain, finish_first, ((rest0, 0), (rest0, 1), (rest0, 5)), ho
    )
    below, corner, right, table1 = lax.optimization_barrier((below, corner, right, table1))
    pieces = (
        own,
        shift_tokens(right, 0, -1),
        shift_tokens(below, -1, 0),
        shift_tokens(corner, -1, -1),
    )
    layer1 = spread_pair(second, second_x)
    ho = attn(1, pieces, assemble_shifted, (layer1, 0), table1)
    own, right, below, corner = feed(
        1, pieces, assemble_shifted, finish_second, ((layer1, 3), (layer1, 4), (layer1, 8)), ho
    )
    return join(
        own,
        shift_tokens(right, 0, 1),
        shift_tokens(below, 1, 0),
        shift_tokens(corner, 1, 1),
    )


def solution(mesh):
    fine = jax.sharding.Mesh(mesh.devices.reshape(SIZES), AXES)
    tokens = P(("img", "row"), ("x", "yh", "c"), None)
    weight = P(None, ("x", "yh", "c"), None)
    in_specs = (tokens, weight, weight, weight, weight, P(), P(), P(), P(), P())

    return jax.shard_map(local, mesh=fine, in_specs=in_specs, out_specs=tokens, check_vma=False)
```

time: 258 us -> 160 us (0.62)
  the two profiles are of different devices: /device:TPU:64 before, /device:TPU:8 now
where the time goes in v1:
time: 160 us; the launch traced here: 159 us
  waiting for transfers between devices  60.8 us (38%)
  Pallas kernels  58.3 us (36%)
  starting transfers between devices  32.8 us (20%)
  local copies, waits for them, and re-layouts  7.4 us (5%)
    ppermute x28, waiting for transfers between devices, send(): return lax.ppermute(block, AXES, pairs)  60.8 us
    ppermute x28, starting transfers between devices, send(): return lax.ppermute(block, AXES, pairs)  32.8 us
    pallas_call x2, Pallas kernels, attention(): pl.pallas_call(lambda *refs: attn_kernel(n, layer, tags, assemble, first,...  18.8 us
    pallas_call x2, Pallas kernels, bias_table(): pl.pallas_call(body, out_shape=jax.ShapeDtypeStruct((HEADS, KEYS, TOK), F...  14.6 us
    pallas_call x2, Pallas kernels, mlp(): pl.pallas_call(lambda *refs: mlp_kernel(n, layer, tags, firsts, assemble,...  13.1 us
    unnamed x40, local copies, waits for them, and re-layouts  5.62 us
    pallas_call x2, Pallas kernels, chunks(): pl.pallas_call(lambda *refs: chunk_kernel(picks, len(after), *refs), out_...  3.86 us
    pallas_call x2, Pallas kernels, pair(): pl.pallas_call(pair_kernel, out_shape=jax.ShapeDtypeStruct((2, *own.shape...  3.66 us
  transfers between devices with their start and end apart: 28, of which 9 were waited for; matrix products, arithmetic and copies ran while one was open for 1% of the time, Pallas kernels for 23%

profile of v1, /device:TPU:8, one launch (start us, length us, event | category | flops | bytes accessed | tf_op | source)
XLA Modules:
  0.0 159.5 jit_solution(16722009842856838550)
XLA Ops:
  0.0 1.9 %chunks.2 = (bf16[3,32,512]{2,1,0:T(8,128)(2,1)}, bf16[9,32,512]{2,1,0:T(8,128)(2,1)}) custom-call(bf16[2,32,1536]{2,1,0:T(8,128)(2,1)} %refs_0_.5, bf16[2,32,512]{2,1,0:T(8,128)(2,1)} %refs_1_.5, bf16[2,32,2048]{2,1,0:T(8,128)(2,1)} %refs_2_.4, bf16[2,128,512]{2,1,0:T(8,128)(2,1)} %refs_3_.4), custom_call_target="tpu_custom_call" | custom-call | tf_op jit(solution)/shard_map/chunks/pallas_call | solution.py:405
  1.9 3.0 %collective-permute-start.10 = (bf16[9,32,512]{2,1,0:T(8,128)(2,1)}, bf16[9,32,512]{2,1,0:T(8,128)(2,1)S(1)}, u32[]{:S(2)}, u32[]{:S(2)}) collective-permute-start(bf16[9,32,512]{2,1,0:T(8,128)(2,1)} %get-tuple-element.20.refs_0_), channel_id=1, source_target_pairs={{0,16},{1,17},{2,18},{3,19},{4,20},{5,21},{6,22},{7,23},{8,24},{9,... | collective-permute-start | bytes 884744 | tf_op jit(solution)/shard_map/ppermute | solution.py:374
  5.5 2.6 %collective-permute-start.9 = (bf16[9,32,512]{2,1,0:T(8,128)(2,1)}, bf16[9,32,512]{2,1,0:T(8,128)(2,1)S(1)}, u32[]{:S(2)}, u32[]{:S(2)}) collective-permute-start(bf16[9,32,512]{2,1,0:T(8,128)(2,1)} %get-tuple-element.20.refs_0_), channel_id=1, source_target_pairs={{0,24},{1,25},{2,26},{3,27},{4,28},{5,29},{6,30},{7,31},{8,0},{9,1... | collective-permute-start | bytes 884744 | tf_op jit(solution)/shard_map/ppermute | solution.py:374
  8.2 1.6 collective-permute-start
  9.8 1.8 %fusion.1 = (f32[23,16,128]{2,1,0:T(8,128)}, f32[23,16,128]{2,1,0:T(8,128)}) fusion(f32[2,23,16,23]{3,2,1,0:T(8,128)} %bitcast.5), kind=kLoop, calls=%fused_computation.3 | loop fusion | bytes 444544 | tf_op jit(solution)/shard_map/squeeze | solution.py:519
  11.5 1.5 collective-permute-done.other
  13.6 1.6 %pair.2.refs_4_.refs_1_ = bf16[2,3,32,512]{3,2,1,0:T(8,128)(2,1)} custom-call(bf16[3,32,512]{2,1,0:T(8,128)(2,1)} %get-tuple-element.19.own, bf16[3,32,512]{2,1,0:T(8,128)(2,1)} %copy-done.8), custom_call_target="tpu_custom_call" | custom-call | tf_op jit(solution)/shard_map/pair/pallas_call | solution.py:456
  15.3 1.9 %chunks.3.refs_2_.own = bf16[12,32,512]{2,1,0:T(8,128)(2,1)} custom-call(bf16[2,32,1536]{2,1,0:T(8,128)(2,1)} %refs_0_.5, bf16[2,32,512]{2,1,0:T(8,128)(2,1)} %refs_1_.5, bf16[2,32,2048]{2,1,0:T(8,128)(2,1)} %refs_2_.4, bf16[2,128,512]{2,1,0:T(8,128)(2,1)} %refs_3_.4, bf16[2,3,32,512]{3,2,1,0:T(8,128)(2,1)} %pair.2.refs_4_.refs_1_), custom_call_target="tpu_custom_call" | custom-call | tf_op jit(solution)/shard_map/chunks/pallas_call | solution.py:405
  17.2 7.3 %bias_table.2.refs_14_.refs_4_ = f32[16,144,432]{2,1,0:T(8,128)} custom-call(f32[23,16,128]{2,1,0:T(8,128)} %get-tuple-element.34.refs_0_, f32[8,512]{1,0:T(8,128)} %constant.9.clone.refs_1_, bf16[12,32,512]{2,1,0:T(8,128)(2,1)} %chunks.3.refs_2_.own), custom_call_target="tpu_custom_call" | custom-call | tf_op jit(solution)/shard_map/bias_table/pallas_call | solution.py:111
  26.0 2.3 %join_x.1.refs_5_.refs_9_.refs_13_.refs_0_ = bf16[4,9,32,512]{3,2,1,0:T(8,128)(2,1)} custom-call(bf16[9,32,512]{2,1,0:T(8,128)(2,1)} %get-tuple-element.20.refs_0_, bf16[9,32,512]{2,1,0:T(8,128)(2,1)} %copy-done.5, bf16[9,32,512]{2,1,0:T(8,128)(2,1)} %copy-done.6, bf16[9,32,512]{2,1,0:T(8,128)(2,1)} %copy-done.4, f32[16,144,432]{2,1,0:T(8,128)} %bias_table.2.refs_14_.refs_4_), custom_call_target="tpu_custom_call" | custom-call | tf_op jit(solution)/shard_map/join_x/pallas_call | solution.py:431
  28.3 1.7 %collective-permute-start.12 = (bf16[4,9,32,512]{3,2,1,0:T(8,128)(2,1)}, bf16[4,9,32,512]{3,2,1,0:T(8,128)(2,1)S(1)}, u32[]{:S(2)}, u32[]{:S(2)}) collective-permute-start(bf16[4,9,32,512]{3,2,1,0:T(8,128)(2,1)} %join_x.1.refs_5_.refs_9_.refs_13_.refs_0_), channel_id=1, source_target_pairs={{0,5},{1,4},{2,7},{3,6},{4,1},{5,0},{6,3},{7,2},{8,13},{9,12},{10,... | collective-permute-start | bytes 3538952 | tf_op jit(solution)/shard_map/ppermute | solution.py:374
  30.5 3.1 %collective-permute-start.4 = (bf16[2,3,32,512]{3,2,1,0:T(8,128)(2,1)S(1)}, bf16[2,3,32,512]{3,2,1,0:T(8,128)(2,1)}, u32[]{:S(2)}, u32[]{:S(2)}) collective-permute-start(bf16[2,3,32,512]{3,2,1,0:T(8,128)(2,1)S(1)} %copy-done.2), channel_id=1, source_target_pairs={{0,24},{1,25},{2,26},{3,27},{4,28},{5,29},{6,30},{7,31},{8,0},{9,1... | collective-permute-start | bytes 589832 | tf_op jit(solution)/shard_map/ppermute | solution.py:374
  33.7 7.4 %collective-permute-done.2.refs_3_ = bf16[2,3,32,512]{3,2,1,0:T(8,128)(2,1)S(1)} collective-permute-done((bf16[2,3,32,512]{3,2,1,0:T(8,128)(2,1)S(1)}, bf16[2,3,32,512]{3,2,1,0:T(8,128)(2,1)S(1)}, u32[]{:S(2)}, u32[]{:S(2)}) %collective-permute-start.2) | collective-permute-done | bytes 196640 | tf_op jit(solution)/shard_map/ppermute | solution.py:374
  41.6 15.9 %collective-permute-done.12.refs_7_.refs_11_.refs_15_ = bf16[4,9,32,512]{3,2,1,0:T(8,128)(2,1)S(1)} collective-permute-done((bf16[4,9,32,512]{3,2,1,0:T(8,128)(2,1)}, bf16[4,9,32,512]{3,2,1,0:T(8,128)(2,1)S(1)}, u32[]{:S(2)}, u32[]{:S(2)}) %collective-permute-start.12) | collective-permute-done | bytes 1179680 | tf_op jit(solution)/shard_map/ppermute | solution.py:374
  58.1 5.0 %collective-permute-done.17.other = bf16[12,32,512]{2,1,0:T(8,128)(2,1)S(1)} collective-permute-done((bf16[12,32,512]{2,1,0:T(8,128)(2,1)S(1)}, bf16[12,32,512]{2,1,0:T(8,128)(2,1)S(1)}, u32[]{:S(2)}, u32[]{:S(2)}) %collective-permute-start.17) | collective-permute-done | bytes 393248 | tf_op jit(solution)/shard_map/ppermute | solution.py:374
  63.1 0.8 copy-done.3
  63.9 2.0 %pair.3.refs_4_.refs_8_.refs_16_.refs_24_ = bf16[2,12,32,512]{3,2,1,0:T(8,128)(2,1)} custom-call(bf16[12,32,512]{2,1,0:T(8,128)(2,1)} %chunks.3.refs_2_.own, bf16[12,32,512]{2,1,0:T(8,128)(2,1)} %copy-done.3, bf16[4,9,32,512]{3,2,1,0:T(8,128)(2,1)} %join_x.1.refs_5_.refs_9_.refs_13_.refs_0_), custom_call_target="tpu_custom_call" | custom-call | tf_op jit(solution)/shard_map/pair/pallas_call | solution.py:456
  66.0 3.2 %collective-permute-start.21 = (bf16[2,12,32,512]{3,2,1,0:T(8,128)(2,1)}, bf16[2,12,32,512]{3,2,1,0:T(8,128)(2,1)}, u32[]{:S(2)}, u32[]{:S(2)}) collective-permute-start(bf16[2,12,32,512]{3,2,1,0:T(8,128)(2,1)} %pair.3.refs_4_.refs_8_.refs_16_.refs_24_), channel_id=1, source_target_pairs={{0,24},{1,25},{2,26},{3,27},{4,28},{5,29},{6,30},{7,31},{8,0},{9,1... | collective-permute-start | bytes 2359304 | tf_op jit(solution)/shard_map/ppermute | solution.py:374
  69.9 9.4 %attention.2.refs_1_.refs_2_ = bf16[432,512]{1,0:T(8,128)(2,1)} custom-call(bf16[12,36,512]{2,1,0:T(8,128)(2,1)} %refs_0_.7, bf16[2,3,32,512]{3,2,1,0:T(8,128)(2,1)} %pair.2.refs_4_.refs_1_, bf16[2,3,32,512]{3,2,1,0:T(8,128)(2,1)} %copy-done.14, bf16[2,3,32,512]{3,2,1,0:T(8,128)(2,1)} %copy-done.13, bf16[2,3,32,512]{3,2,1,0:T(8,128)(2,1)} %collective-permute-done.3.refs_4_, ...), custom_call_target="tpu_custom_call" | custom-call | flops 10000000000 | bytes 8000000 | tf_op jit(solution)/shard_map/attention/pallas_call | solution.py:207
  79.3 7.4 %bias_table.3.refs_17_ = f32[16,144,432]{2,1,0:T(8,128)} custom-call(f32[23,16,128]{2,1,0:T(8,128)} %get-tuple-element.33.refs_0_, f32[8,512]{1,0:T(8,128)} %constant.9.clone.refs_1_, bf16[432,512]{1,0:T(8,128)(2,1)} %attention.2.refs_1_.refs_2_), custom_call_target="tpu_custom_call" | custom-call | tf_op jit(solution)/shard_map/bias_table/pallas_call | solution.py:111
  86.7 16.8 %collective-permute-done.19.refs_6_.refs_10_.refs_18_.refs_26_ = bf16[2,12,32,512]{3,2,1,0:T(8,128)(2,1)} collective-permute-done((bf16[2,12,32,512]{3,2,1,0:T(8,128)(2,1)}, bf16[2,12,32,512]{3,2,1,0:T(8,128)(2,1)}, u32[]{:S(2)}, u32[]{:S(2)}) %collective-permute-start.19) | collective-permute-done | bytes 786464 | tf_op jit(solution)/shard_map/ppermute | solution.py:374
  105.2 6.5 %mlp.2 = (bf16[6,30,512]{2,1,0:T(8,128)(2,1)}, bf16[6,6,512]{2,1,0:T(8,128)(2,1)}, bf16[6,30,512]{2,1,0:T(8,128)(2,1)}, bf16[6,6,512]{2,1,0:T(8,128)(2,1)}) custom-call(bf16[12,36,512]{2,1,0:T(8,128)(2,1)} %refs_0_.7, bf16[432,512]{1,0:T(8,128)(2,1)} %attention.2.refs_1_.refs_2_, f32[2,2048]{1,0:T(2,128)} %refs_5_.1, f32[2,2,512]{2,1,0:T(2,128)} %refs_6_.1, ...), custom_call_target="tpu_custom_call" | custom-call | flops 10000000000 | bytes 8000000 | tf_op jit(solution)/shard_map/mlp/pallas_call | solution.py:271
  111.7 5.9 %collective-permute-start.15 = (bf16[6,30,512]{2,1,0:T(8,128)(2,1)}, bf16[6,30,512]{2,1,0:T(8,128)(2,1)S(1)}, u32[]{:S(2)}, u32[]{:S(2)}) collective-permute-start(bf16[6,30,512]{2,1,0:T(8,128)(2,1)} %get-tuple-element.26), channel_id=1, source_target_pairs={{0,224},{1,225},{2,226},{3,227},{4,228},{5,229},{6,230},{7,231},{8... | collective-permute-start | bytes 552968 | tf_op jit(solution)/shard_map/ppermute | solution.py:374
  117.6 6.3 %collective-permute-start.14 = (bf16[6,6,512]{2,1,0:T(8,128)(2,1)}, bf16[6,6,512]{2,1,0:T(8,128)(2,1)S(1)}, u32[]{:S(2)}, u32[]{:S(2)}) collective-permute-start(bf16[6,6,512]{2,1,0:T(8,128)(2,1)} %get-tuple-element.25), channel_id=1, source_target_pairs={{0,30},{1,31},{2,0},{3,1},{4,2},{5,3},{6,4},{7,5},{8,6},{9,7},{10,... | collective-permute-start | bytes 110600 | tf_op jit(solution)/shard_map/ppermute | solution.py:374
  124.0 1.2 collective-permute-start.16
  125.2 0.8 collective-permute-done.14.refs_1_
  126.0 1.7 %collective-permute-done.16.refs_3_ = bf16[6,6,512]{2,1,0:T(8,128)(2,1)S(1)} collective-permute-done((bf16[6,6,512]{2,1,0:T(8,128)(2,1)}, bf16[6,6,512]{2,1,0:T(8,128)(2,1)S(1)}, u32[]{:S(2)}, u32[]{:S(2)}) %collective-permute-start.16) | collective-permute-done | bytes 36896 | tf_op jit(solution)/shard_map/ppermute | solution.py:374
  128.4 9.4 %attention.3.refs_4_ = bf16[432,512]{1,0:T(8,128)(2,1)} custom-call(bf16[6,30,512]{2,1,0:T(8,128)(2,1)} %get-tuple-element.21.refs_0_, bf16[6,6,512]{2,1,0:T(8,128)(2,1)} %copy-done.18, bf16[6,30,512]{2,1,0:T(8,128)(2,1)} %copy-done.15, bf16[6,6,512]{2,1,0:T(8,128)(2,1)} %copy-done.19, bf16[2,12,32,512]{3,2,1,0:T(8,128)(2,1)} %pair.3.refs_4_.refs_8_.refs_16_.refs_24_, ...), custom_call_target="tpu_custom_call" | custom-call | flops 10000000000 | bytes 8000000 | tf_op jit(solution)/shard_map/attention/pallas_call | solution.py:207
  137.9 6.6 %mlp.3 = (bf16[6,30,512]{2,1,0:T(8,128)(2,1)}, bf16[6,6,512]{2,1,0:T(8,128)(2,1)}, bf16[6,30,512]{2,1,0:T(8,128)(2,1)}, bf16[6,6,512]{2,1,0:T(8,128)(2,1)}) custom-call(bf16[6,30,512]{2,1,0:T(8,128)(2,1)} %get-tuple-element.21.refs_0_, bf16[6,6,512]{2,1,0:T(8,128)(2,1)} %copy-done.18, bf16[6,30,512]{2,1,0:T(8,128)(2,1)} %copy-done.15, ...), custom_call_target="tpu_custom_call" | custom-call | flops 10000000000 | bytes 8000000 | tf_op jit(solution)/shard_map/mlp/pallas_call | solution.py:271
  145.1 7.3 %collective-permute-done.25.right = bf16[6,6,512]{2,1,0:T(8,128)(2,1)S(1)} collective-permute-done((bf16[6,6,512]{2,1,0:T(8,128)(2,1)}, bf16[6,6,512]{2,1,0:T(8,128)(2,1)S(1)}, u32[]{:S(2)}, u32[]{:S(2)}) %collective-permute-start.25) | collective-permute-done | bytes 36896 | tf_op jit(solution)/shard_map/ppermute | solution.py:374
  152.5 4.4 %collective-permute-done.27.corner = bf16[6,6,512]{2,1,0:T(8,128)(2,1)S(1)} collective-permute-done((bf16[6,6,512]{2,1,0:T(8,128)(2,1)}, bf16[6,6,512]{2,1,0:T(8,128)(2,1)S(1)}, u32[]{:S(2)}, u32[]{:S(2)}) %collective-permute-start.27) | collective-permute-done | bytes 36896 | tf_op jit(solution)/shard_map/ppermute | solution.py:374
  157.6 1.9 %join.1 = bf16[12,36,512]{2,1,0:T(8,128)(2,1)} custom-call(bf16[6,30,512]{2,1,0:T(8,128)(2,1)} %get-tuple-element.29.own, bf16[6,6,512]{2,1,0:T(8,128)(2,1)} %copy-done.9, bf16[6,30,512]{2,1,0:T(8,128)(2,1)} %copy-done.7, bf16[6,6,512]{2,1,0:T(8,128)(2,1)} %copy-done.10), custom_call_target="tpu_custom_call" | custom-call | tf_op jit(solution)/shard_map/join/pallas_call | solution.py:339
  (77 shorter events, 8.9 us)
Async XLA Ops:
  1.9 22.6 %collective-permute-start.10 = (bf16[9,32,512]{2,1,0:T(8,128)(2,1)}, bf16[9,32,512]{2,1,0:T(8,128)(2,1)S(1)}, u32[]{:S(2)}, u32[]{:S(2)}) collective-permute-start(bf16[9,32,512]{2,1,0:T(8,128)(2,1)} %get-tuple-element.20.refs_0_), channel_id=1, source_target_pairs={{0,16},{1,17},{2,18},{3,19},{4,20},{5,21},{6,22},{7,23},{8,24},{9,... | collective-permute-start | bytes 884744 | tf_op jit(solution)/shard_map/ppermute | solution.py:374
  4.9 19.6 %collective-permute-start.8 = (bf16[9,32,512]{2,1,0:T(8,128)(2,1)}, bf16[9,32,512]{2,1,0:T(8,128)(2,1)S(1)}, u32[]{:S(2)}, u32[]{:S(2)}) collective-permute-start(bf16[9,32,512]{2,1,0:T(8,128)(2,1)} %get-tuple-element.20.refs_0_), channel_id=1, source_target_pairs={{0,8},{1,9},{2,10},{3,11},{4,12},{5,13},{6,14},{7,15},{8,16},{9,17... | collective-permute-start | bytes 884744 | tf_op jit(solution)/shard_map/ppermute | solution.py:374
  5.5 19.0 %collective-permute-start.9 = (bf16[9,32,512]{2,1,0:T(8,128)(2,1)}, bf16[9,32,512]{2,1,0:T(8,128)(2,1)S(1)}, u32[]{:S(2)}, u32[]{:S(2)}) collective-permute-start(bf16[9,32,512]{2,1,0:T(8,128)(2,1)} %get-tuple-element.20.refs_0_), channel_id=1, source_target_pairs={{0,24},{1,25},{2,26},{3,27},{4,28},{5,29},{6,30},{7,31},{8,0},{9,1... | collective-permute-start | bytes 884744 | tf_op jit(solution)/shard_map/ppermute | solution.py:374
  8.2 4.8 %collective-permute-start = (bf16[3,32,512]{2,1,0:T(8,128)(2,1)}, bf16[3,32,512]{2,1,0:T(8,128)(2,1)S(1)}, u32[]{:S(2)}, u32[]{:S(2)}) collective-permute-start(bf16[3,32,512]{2,1,0:T(8,128)(2,1)} %get-tuple-element.19.own), channel_id=1, source_target_pairs={{0,5},{1,4},{2,7},{3,6},{4,1},{5,0},{6,3},{7,2},{8,13},{9,12},{10,... | collective-permute-start | bytes 294920 | tf_op jit(solution)/shard_map/ppermute | solution.py:374
  24.5 5.5 %copy-start = (bf16[12,32,512]{2,1,0:T(8,128)(2,1)S(1)}, bf16[12,32,512]{2,1,0:T(8,128)(2,1)}, u32[]{:S(2)}) copy-start(bf16[12,32,512]{2,1,0:T(8,128)(2,1)} %chunks.3.refs_2_.own) | copy-start | bytes 1179652
  28.3 29.1 %collective-permute-start.12 = (bf16[4,9,32,512]{3,2,1,0:T(8,128)(2,1)}, bf16[4,9,32,512]{3,2,1,0:T(8,128)(2,1)S(1)}, u32[]{:S(2)}, u32[]{:S(2)}) collective-permute-start(bf16[4,9,32,512]{3,2,1,0:T(8,128)(2,1)} %join_x.1.refs_5_.refs_9_.refs_13_.refs_0_), channel_id=1, source_target_pairs={{0,5},{1,4},{2,7},{3,6},{4,1},{5,0},{6,3},{7,2},{8,13},{9,12},{10,... | collective-permute-start | bytes 3538952 | tf_op jit(solution)/shard_map/ppermute | solution.py:374
  30.0 11.1 %collective-permute-start.2 = (bf16[2,3,32,512]{3,2,1,0:T(8,128)(2,1)S(1)}, bf16[2,3,32,512]{3,2,1,0:T(8,128)(2,1)S(1)}, u32[]{:S(2)}, u32[]{:S(2)}) collective-permute-start(bf16[2,3,32,512]{3,2,1,0:T(8,128)(2,1)S(1)} %copy-done.2), channel_id=1, source_target_pairs={{0,8},{1,9},{2,10},{3,11},{4,12},{5,13},{6,14},{7,15},{8,16},{9,17... | collective-permute-start | bytes 589832 | tf_op jit(solution)/shard_map/ppermute | solution.py:374
  30.0 33.1 %collective-permute-start.17 = (bf16[12,32,512]{2,1,0:T(8,128)(2,1)S(1)}, bf16[12,32,512]{2,1,0:T(8,128)(2,1)S(1)}, u32[]{:S(2)}, u32[]{:S(2)}) collective-permute-start(bf16[12,32,512]{2,1,0:T(8,128)(2,1)S(1)} %copy-done), channel_id=1, source_target_pairs={{0,5},{1,4},{2,7},{3,6},{4,1},{5,0},{6,3},{7,2},{8,13},{9,12},{10,... | collective-permute-start | bytes 1179656 | tf_op jit(solution)/shard_map/ppermute | solution.py:374
  30.5 10.6 %collective-permute-start.4 = (bf16[2,3,32,512]{3,2,1,0:T(8,128)(2,1)S(1)}, bf16[2,3,32,512]{3,2,1,0:T(8,128)(2,1)}, u32[]{:S(2)}, u32[]{:S(2)}) collective-permute-start(bf16[2,3,32,512]{3,2,1,0:T(8,128)(2,1)S(1)} %copy-done.2), channel_id=1, source_target_pairs={{0,24},{1,25},{2,26},{3,27},{4,28},{5,29},{6,30},{7,31},{8,0},{9,1... | collective-permute-start | bytes 589832 | tf_op jit(solution)/shard_map/ppermute | solution.py:374
  33.7 23.8 %collective-permute-start.6 = (bf16[2,3,32,512]{3,2,1,0:T(8,128)(2,1)S(1)}, bf16[2,3,32,512]{3,2,1,0:T(8,128)(2,1)}, u32[]{:S(2)}, u32[]{:S(2)}) collective-permute-start(bf16[2,3,32,512]{3,2,1,0:T(8,128)(2,1)S(1)} %copy-done.2), channel_id=1, source_target_pairs={{0,16},{1,17},{2,18},{3,19},{4,20},{5,21},{6,22},{7,23},{8,24},{9,... | collective-permute-start | bytes 589832 | tf_op jit(solution)/shard_map/ppermute | solution.py:374
  41.1 28.1 %copy-start.13 = (bf16[2,3,32,512]{3,2,1,0:T(8,128)(2,1)}, bf16[2,3,32,512]{3,2,1,0:T(8,128)(2,1)S(1)}, u32[]{:S(2)}) copy-start(bf16[2,3,32,512]{3,2,1,0:T(8,128)(2,1)S(1)} %collective-permute-done.2.refs_3_) | copy-start | bytes 589828
  41.1 16.9 %collective-permute-start.1 = (bf16[2,3,32,512]{3,2,1,0:T(8,128)(2,1)S(1)}, bf16[2,3,32,512]{3,2,1,0:T(8,128)(2,1)S(1)}, u32[]{:S(2)}, u32[]{:S(2)}) collective-permute-start(bf16[2,3,32,512]{3,2,1,0:T(8,128)(2,1)S(1)} %copy-done.2), channel_id=1, source_target_pairs={{0,2},{1,3},{2,0},{3,1},{4,6},{5,7},{6,4},{7,5},{8,10},{9,11},{10,... | collective-permute-start | bytes 589832 | tf_op jit(solution)/shard_map/ppermute | solution.py:374
  41.1 63.1 %collective-permute-start.11 = (bf16[4,9,32,512]{3,2,1,0:T(8,128)(2,1)}, bf16[4,9,32,512]{3,2,1,0:T(8,128)(2,1)S(1)}, u32[]{:S(2)}, u32[]{:S(2)}) collective-permute-start(bf16[4,9,32,512]{3,2,1,0:T(8,128)(2,1)} %join_x.1.refs_5_.refs_9_.refs_13_.refs_0_), channel_id=1, source_target_pairs={{0,2},{1,3},{2,0},{3,1},{4,6},{5,7},{6,4},{7,5},{8,10},{9,11},{10,... | collective-permute-start | bytes 3538952 | tf_op jit(solution)/shard_map/ppermute | solution.py:374
  57.5 21.8 %copy-start.11 = (bf16[4,9,32,512]{3,2,1,0:T(8,128)(2,1)}, bf16[4,9,32,512]{3,2,1,0:T(8,128)(2,1)S(1)}, u32[]{:S(2)}) copy-start(bf16[4,9,32,512]{3,2,1,0:T(8,128)(2,1)S(1)} %collective-permute-done.12.refs_7_.refs_11_.refs_15_) | copy-start | bytes 3538948
  57.5 47.1 %collective-permute-start.13 = (bf16[4,9,32,512]{3,2,1,0:T(8,128)(2,1)S(1)}, bf16[4,9,32,512]{3,2,1,0:T(8,128)(2,1)}, u32[]{:S(2)}, u32[]{:S(2)}) collective-permute-start(bf16[4,9,32,512]{3,2,1,0:T(8,128)(2,1)S(1)} %collective-permute-done.12.refs_7_.refs_11_.refs_15_), channel_id=1, source_target_pairs={{0,2},{1,3},{2,0},{3,1},{4,6},{5,7},{6,4},{7,5},{8,10},{9,11},{10,... | collective-permute-start | bytes 3538952 | tf_op jit(solution)/shard_map/ppermute | solution.py:374
  57.5 8.4 %collective-permute-start.3 = (bf16[2,3,32,512]{3,2,1,0:T(8,128)(2,1)S(1)}, bf16[2,3,32,512]{3,2,1,0:T(8,128)(2,1)}, u32[]{:S(2)}, u32[]{:S(2)}) collective-permute-start(bf16[2,3,32,512]{3,2,1,0:T(8,128)(2,1)S(1)} %collective-permute-done.2.refs_3_), channel_id=1, source_target_pairs={{0,2},{1,3},{2,0},{3,1},{4,6},{5,7},{6,4},{7,5},{8,10},{9,11},{10,... | collective-permute-start | bytes 589832 | tf_op jit(solution)/shard_map/ppermute | solution.py:374
  58.0 8.0 %collective-permute-start.5 = (bf16[2,3,32,512]{3,2,1,0:T(8,128)(2,1)}, bf16[2,3,32,512]{3,2,1,0:T(8,128)(2,1)S(1)}, u32[]{:S(2)}, u32[]{:S(2)}) collective-permute-start(bf16[2,3,32,512]{3,2,1,0:T(8,128)(2,1)} %collective-permute-done.4.refs_5_), channel_id=1, source_target_pairs={{0,2},{1,3},{2,0},{3,1},{4,6},{5,7},{6,4},{7,5},{8,10},{9,11},{10,... | collective-permute-start | bytes 589832 | tf_op jit(solution)/shard_map/ppermute | solution.py:374
  63.1 6.1 %collective-permute-start.7 = (bf16[2,3,32,512]{3,2,1,0:T(8,128)(2,1)}, bf16[2,3,32,512]{3,2,1,0:T(8,128)(2,1)S(1)}, u32[]{:S(2)}, u32[]{:S(2)}) collective-permute-start(bf16[2,3,32,512]{3,2,1,0:T(8,128)(2,1)} %collective-permute-done.6.refs_7_), channel_id=1, source_target_pairs={{0,2},{1,3},{2,0},{3,1},{4,6},{5,7},{6,4},{7,5},{8,10},{9,11},{10,... | collective-permute-start | bytes 589832 | tf_op jit(solution)/shard_map/ppermute | solution.py:374
  65.9 37.6 %collective-permute-start.19 = (bf16[2,12,32,512]{3,2,1,0:T(8,128)(2,1)}, bf16[2,12,32,512]{3,2,1,0:T(8,128)(2,1)}, u32[]{:S(2)}, u32[]{:S(2)}) collective-permute-start(bf16[2,12,32,512]{3,2,1,0:T(8,128)(2,1)} %pair.3.refs_4_.refs_8_.refs_16_.refs_24_), channel_id=1, source_target_pairs={{0,8},{1,9},{2,10},{3,11},{4,12},{5,13},{6,14},{7,15},{8,16},{9,17... | collective-permute-start | bytes 2359304 | tf_op jit(solution)/shard_map/ppermute | solution.py:374
  66.0 37.5 %collective-permute-start.21 = (bf16[2,12,32,512]{3,2,1,0:T(8,128)(2,1)}, bf16[2,12,32,512]{3,2,1,0:T(8,128)(2,1)}, u32[]{:S(2)}, u32[]{:S(2)}) collective-permute-start(bf16[2,12,32,512]{3,2,1,0:T(8,128)(2,1)} %pair.3.refs_4_.refs_8_.refs_16_.refs_24_), channel_id=1, source_target_pairs={{0,24},{1,25},{2,26},{3,27},{4,28},{5,29},{6,30},{7,31},{8,0},{9,1... | collective-permute-start | bytes 2359304 | tf_op jit(solution)/shard_map/ppermute | solution.py:374
  69.2 34.8 %collective-permute-start.23 = (bf16[2,12,32,512]{3,2,1,0:T(8,128)(2,1)}, bf16[2,12,32,512]{3,2,1,0:T(8,128)(2,1)}, u32[]{:S(2)}, u32[]{:S(2)}) collective-permute-start(bf16[2,12,32,512]{3,2,1,0:T(8,128)(2,1)} %pair.3.refs_4_.refs_8_.refs_16_.refs_24_), channel_id=1, source_target_pairs={{0,16},{1,17},{2,18},{3,19},{4,20},{5,21},{6,22},{7,23},{8,24},{9,... | collective-permute-start | bytes 2359304 | tf_op jit(solution)/shard_map/ppermute | solution.py:374
  79.3 24.2 %copy-start.1 = (bf16[2,12,32,512]{3,2,1,0:T(8,128)(2,1)S(1)}, bf16[2,12,32,512]{3,2,1,0:T(8,128)(2,1)}, u32[]{:S(2)}) copy-start(bf16[2,12,32,512]{3,2,1,0:T(8,128)(2,1)} %pair.3.refs_4_.refs_8_.refs_16_.refs_24_) | copy-start | bytes 2359300
  103.5 14.1 %collective-permute-start.18 = (bf16[2,12,32,512]{3,2,1,0:T(8,128)(2,1)S(1)}, bf16[2,12,32,512]{3,2,1,0:T(8,128)(2,1)}, u32[]{:S(2)}, u32[]{:S(2)}) collective-permute-start(bf16[2,12,32,512]{3,2,1,0:T(8,128)(2,1)S(1)} %copy-done.1), channel_id=1, source_target_pairs={{0,2},{1,3},{2,0},{3,1},{4,6},{5,7},{6,4},{7,5},{8,10},{9,11},{10,... | collective-permute-start | bytes 2359304 | tf_op jit(solution)/shard_map/ppermute | solution.py:374
  103.6 20.4 %collective-permute-start.20 = (bf16[2,12,32,512]{3,2,1,0:T(8,128)(2,1)}, bf16[2,12,32,512]{3,2,1,0:T(8,128)(2,1)}, u32[]{:S(2)}, u32[]{:S(2)}) collective-permute-start(bf16[2,12,32,512]{3,2,1,0:T(8,128)(2,1)} %collective-permute-done.19.refs_6_.refs_10_.refs_18_.refs_26_), channel_id=1, source_target_pairs={{0,2},{1,3},{2,0},{3,1},{4,6},{5,7},{6,4},{7,5},{8,10},{9,11},{10,... | collective-permute-start | bytes 2359304 | tf_op jit(solution)/shard_map/ppermute | solution.py:374
  104.1 21.1 %collective-permute-start.22 = (bf16[2,12,32,512]{3,2,1,0:T(8,128)(2,1)}, bf16[2,12,32,512]{3,2,1,0:T(8,128)(2,1)}, u32[]{:S(2)}, u32[]{:S(2)}) collective-permute-start(bf16[2,12,32,512]{3,2,1,0:T(8,128)(2,1)} %collective-permute-done.21.refs_8_.refs_12_.refs_20_.refs_28_), channel_id=1, source_target_pairs={{0,2},{1,3},{2,0},{3,1},{4,6},{5,7},{6,4},{7,5},{8,10},{9,11},{10,... | collective-permute-start | bytes 2359304 | tf_op jit(solution)/shard_map/ppermute | solution.py:374
  104.2 21.0 %collective-permute-start.24 = (bf16[2,12,32,512]{3,2,1,0:T(8,128)(2,1)}, bf16[2,12,32,512]{3,2,1,0:T(8,128)(2,1)}, u32[]{:S(2)}, u32[]{:S(2)}) collective-permute-start(bf16[2,12,32,512]{3,2,1,0:T(8,128)(2,1)} %collective-permute-done.23.refs_10_.refs_14_.refs_22_.refs_30_), channel_id=1, source_target_pairs={{0,2},{1,3},{2,0},{3,1},{4,6},{5,7},{6,4},{7,5},{8,10},{9,11},{10,... | collective-permute-start | bytes 2359304 | tf_op jit(solution)/shard_map/ppermute | solution.py:374
  111.7 16.0 %collective-permute-start.15 = (bf16[6,30,512]{2,1,0:T(8,128)(2,1)}, bf16[6,30,512]{2,1,0:T(8,128)(2,1)S(1)}, u32[]{:S(2)}, u32[]{:S(2)}) collective-permute-start(bf16[6,30,512]{2,1,0:T(8,128)(2,1)} %get-tuple-element.26), channel_id=1, source_target_pairs={{0,224},{1,225},{2,226},{3,227},{4,228},{5,229},{6,230},{7,231},{8... | collective-permute-start | bytes 552968 | tf_op jit(solution)/shard_map/ppermute | solution.py:374
  117.6 8.4 %collective-permute-start.14 = (bf16[6,6,512]{2,1,0:T(8,128)(2,1)}, bf16[6,6,512]{2,1,0:T(8,128)(2,1)S(1)}, u32[]{:S(2)}, u32[]{:S(2)}) collective-permute-start(bf16[6,6,512]{2,1,0:T(8,128)(2,1)} %get-tuple-element.25), channel_id=1, source_target_pairs={{0,30},{1,31},{2,0},{3,1},{4,2},{5,3},{6,4},{7,5},{8,6},{9,7},{10,... | collective-permute-start | bytes 110600 | tf_op jit(solution)/shard_map/ppermute | solution.py:374
  124.0 3.7 %collective-permute-start.16 = (bf16[6,6,512]{2,1,0:T(8,128)(2,1)}, bf16[6,6,512]{2,1,0:T(8,128)(2,1)S(1)}, u32[]{:S(2)}, u32[]{:S(2)}) collective-permute-start(bf16[6,6,512]{2,1,0:T(8,128)(2,1)} %get-tuple-element.27), channel_id=1, source_target_pairs={{0,254},{1,255},{2,224},{3,225},{4,226},{5,227},{6,228},{7,229},{8... | collective-permute-start | bytes 110600 | tf_op jit(solution)/shard_map/ppermute | solution.py:374
  144.4 12.4 %collective-permute-start.26 = (bf16[6,30,512]{2,1,0:T(8,128)(2,1)}, bf16[6,30,512]{2,1,0:T(8,128)(2,1)S(1)}, u32[]{:S(2)}, u32[]{:S(2)}) collective-permute-start(bf16[6,30,512]{2,1,0:T(8,128)(2,1)} %get-tuple-element.31), channel_id=1, source_target_pairs={{0,32},{1,33},{2,34},{3,35},{4,36},{5,37},{6,38},{7,39},{8,40},{9,... | collective-permute-start | bytes 552968 | tf_op jit(solution)/shard_map/ppermute | solution.py:374
  145.1 7.3 %collective-permute-start.25 = (bf16[6,6,512]{2,1,0:T(8,128)(2,1)}, bf16[6,6,512]{2,1,0:T(8,128)(2,1)S(1)}, u32[]{:S(2)}, u32[]{:S(2)}) collective-permute-start(bf16[6,6,512]{2,1,0:T(8,128)(2,1)} %get-tuple-element.30), channel_id=1, source_target_pairs={{0,2},{1,3},{2,4},{3,5},{4,6},{5,7},{6,8},{7,9},{8,10},{9,11},{10,... | collective-permute-start | bytes 110600 | tf_op jit(solution)/shard_map/ppermute | solution.py:374
  145.1 11.7 %collective-permute-start.27 = (bf16[6,6,512]{2,1,0:T(8,128)(2,1)}, bf16[6,6,512]{2,1,0:T(8,128)(2,1)S(1)}, u32[]{:S(2)}, u32[]{:S(2)}) collective-permute-start(bf16[6,6,512]{2,1,0:T(8,128)(2,1)} %get-tuple-element.32), channel_id=1, source_target_pairs={{0,34},{1,35},{2,36},{3,37},{4,38},{5,39},{6,40},{7,41},{8,42},{9,... | collective-permute-start | bytes 110600 | tf_op jit(solution)/shard_map/ppermute | solution.py:374
  (16 other events, 27.9 us)

commit v2 on v1

v2 whole, which is shorter than its diff:
```python
import math

import jax
import jax.numpy as jnp
import numpy as np
from jax import lax
from jax.experimental import pallas as pl
from jax.experimental.pallas import tpu as pltpu
from jax.sharding import PartitionSpec as P


HEADS = 16
WIN = 12
SHIFT = 6
D = 512
FF = 2048
HD = 32
KEYS = WIN * WIN
NWIN = 3
TOK = KEYS * NWIN
LOG2E = math.log2(math.e)
BF = jnp.bfloat16
F32 = jnp.float32
MIB = 1024 * 1024
NT = (((1,), (1,)), ((), ()))
NN = (((1,), (0,)), ((), ()))
AXES = ("row", "x", "yh", "c", "img")
SIZES = (8, 4, 2, 2, 2)


def dot(a, b, dims=NN):
    return lax.dot_general(a, b, dims, preferred_element_type=F32)


def layer_norm(values, gain, shift):
    center = values - jnp.mean(values, -1, keepdims=True)
    spread = jnp.mean(center * center, -1, keepdims=True)
    return center * lax.rsqrt(spread + 1e-05) * gain + shift


def bias_kernel(masked, t_ref, side_ref, out_ref, rows, mask):
    lane = lax.broadcasted_iota(jnp.int32, (HEADS, 128), 1)
    n_off = 2 * WIN - 1
    for cb in range(WIN):
        tiles = [jnp.zeros((HEADS, 128), F32) for _ in range(3)]
        for ro in range(n_off):
            moved = pltpu.roll(t_ref[ro], (ro * WIN - (WIN - 1 - cb)) % 128, 1)
            for tile in range(ro * WIN // 128, (ro * WIN + WIN - 1) // 128 + 1):
                low = ro * WIN - tile * 128
                tiles[tile] = jnp.where((lane >= low) & (lane < low + WIN), moved, tiles[tile])
        for tile in range(3):
            rows[tile, (cb + 4) * HEADS : (cb + 5) * HEADS, :] = tiles[tile] * LOG2E
    if masked:
        last_row = (lax.axis_index("row") == 7).astype(F32)
        col = (lax.axis_index("x") * 2 + lax.axis_index("yh")) * 2 + lax.axis_index("c")
        last_col = (col == 15).astype(F32)
        below = side_ref[0:1, :TOK]
        right = side_ref[1:2, :TOK]
        here = side_ref[2:3, :TOK]
        key_right = (lax.broadcasted_iota(jnp.int32, (WIN, 1), 0) >= SHIFT).astype(F32)
        across = last_col * here * jnp.abs(right - key_right)
        for rb in range(WIN):
            down = last_row * jnp.abs(below - (1.0 if rb >= SHIFT else 0.0))
            mask[rb * WIN : (rb + 1) * WIN, :] = jnp.maximum(across, down) * -1e9
    lane = lax.broadcasted_iota(jnp.int32, (16, 128), 1)
    upper = lax.broadcasted_iota(jnp.int32, (8, 128), 0) < 4

    def one_line(mine, at, t):
        value = None
        for w in range(NWIN):
            for s in range(3):
                low = max(KEYS * w, s * 128 + KEYS * w - at) - t * 128
                high = min(KEYS * (w + 1), (s + 1) * 128 + KEYS * w - at) - t * 128
                if max(low, 0) >= min(high, 128):
                    continue
                moved = pltpu.roll(mine[s], (KEYS * w - at) % 128, 1)
                value = moved if value is None else jnp.where(lane >= low, moved, value)
        return value

    def one_head(h, carry):
        even = [rows[tile, pl.ds(h + 4 * HEADS, 16, stride=HEADS), :] for tile in range(3)]
        odd = [rows[tile, pl.ds(h, 16, stride=HEADS), :] for tile in range(3)]
        for pair_at in range(WIN // 2):
            for t in range(4):
                first = one_line(even, (WIN - 1 - 2 * pair_at) * WIN, t)
                second = one_line(odd, (WIN - 2 - 2 * pair_at) * WIN, t)
                whole = jnp.concatenate(
                    [first[:8], jnp.where(upper, first[8:], second[:8]), second[8:]], axis=0)
                width = min(TOK - t * 128, 128)
                at = slice(pair_at * 24, (pair_at + 1) * 24), slice(t * 128, t * 128 + width)
                whole = whole[:, :width]
                if masked:
                    whole = whole + mask[at[0], at[1]]
                out_ref[h, at[0], at[1]] = whole
        return carry

    lax.fori_loop(0, HEADS, one_head, 0)


def bias_table(t, masked, after=()):
    vm = pl.BlockSpec(memory_space=pltpu.VMEM)
    at = np.arange(512)
    side = np.zeros((8, 512), np.float32)
    side[0] = at % KEYS >= SHIFT * WIN
    side[1] = at % WIN >= SHIFT
    side[2] = (at >= 2 * KEYS) & (at < TOK)

    def body(*refs):
        bias_kernel(masked, refs[0], refs[1], *refs[-3:])

    return pl.pallas_call(
        body,
        out_shape=jax.ShapeDtypeStruct((HEADS, KEYS, TOK), F32),
        in_specs=[vm, vm] + [pl.BlockSpec(memory_space=pl.ANY)] * len(after),
        out_specs=vm,
        scratch_shapes=[pltpu.VMEM((3, 20 * HEADS, 128), F32), pltpu.VMEM((KEYS, TOK), F32)],
        compiler_params=pltpu.CompilerParams(vmem_limit_bytes=8 * MIB),
        name="bias_table",
    )(t, jnp.asarray(side), *after)


def fetch_blocks(refs, tags, first, count, dst, whole):
    core = lax.axis_index("c")
    my_yh = lax.axis_index("yh")
    my_x = lax.axis_index("x")
    for ref, (kind, flip, shift) in zip(refs, tags):
        c = 1 - core if flip else core
        for i in range(ref.shape[0]):
            if kind == "x":
                col = i * 4 + (1 - my_yh if shift else my_yh) * 2 + c
            else:
                col = lax.rem(my_x + 4 - shift, 4) * 4 + i * 2 + c
            block = ref[i, first : first + count]
            if whole:
                dst[col] = block
            else:
                dst[:, pl.ds(pl.multiple_of(col * 32, 32), 32), :] = block


def one_hot(where_ref, which, start, count):
    i = lax.broadcasted_iota(jnp.int32, (count, TOK), 0) + start
    return (i == where_ref[which : which + 1, :TOK]).astype(F32).astype(BF)


def attn_kernel(n_pieces, layer, tags, assemble, first, *refs):
    n_w = len(tags)
    pieces = refs[:n_pieces]
    wrefs = refs[n_pieces : n_pieces + n_w]
    at = n_pieces + n_w
    where_ref, bq_all, gain_ref, mbias_ref, bt_ref = refs[at : at + 5]
    hos = refs[at + 5 : -6]
    xs, qs, ks, vts, ots, w_ref = refs[-6:]
    bq_ref = bq_all.at[layer : layer + 1]
    fetch_blocks(wrefs, tags, first, 3, w_ref, False)
    assemble(pieces, xs)
    normed = layer_norm(xs[...], gain_ref[layer, 0:1], mbias_ref[layer, 0:1]).astype(BF)
    nw = dot(one_hot(where_ref, 0, 0, TOK), normed).astype(BF)
    scale = LOG2E / math.sqrt(HD)
    for kind in range(2):
        y = dot(nw, w_ref[kind]) + bq_ref[:, kind * D : (kind + 1) * D]
        if kind == 0:
            y = y * scale
        dst = qs if kind == 0 else ks
        for w in range(NWIN):
            rows = slice(w * KEYS, (w + 1) * KEYS)
            for g in range(4):
                tile = y[rows, g * 128 : (g + 1) * 128]
                if w:
                    tile = pltpu.roll(tile, HD * w, 1)
                dst[g, rows, :] = tile.astype(BF)
    v = (dot(nw, w_ref[2]) + bq_ref[:, 2 * D :]).astype(BF)
    eye = (lax.broadcasted_iota(jnp.int32, (128, 128), 0)
           == lax.broadcasted_iota(jnp.int32, (128, 128), 1)).astype(BF)
    for w in range(NWIN):
        for g in range(4):
            vt = dot(eye, v[w * KEYS : (w + 1) * KEYS, g * 128 : (g + 1) * 128], NT).astype(BF)
            for hh in range(4):
                vts[g * 4 + hh, w * HD : (w + 1) * HD, :] = vt[hh * HD : (hh + 1) * HD]
    for h in range(HEADS):
        vts[h, NWIN * HD :, :] = jnp.ones((16, KEYS), BF)
    lane_slot = lax.broadcasted_iota(jnp.int32, (1, 128), 1) // HD
    slot = [(lane_slot == s).astype(F32).astype(BF) for s in range(4)]
    win = lax.broadcasted_iota(jnp.int32, (1, TOK), 1)

    def four_heads(g, carry):
        for hh in range(4):
            h = g * 4 + hh
            kcat = ks[g, 0:KEYS, :] * slot[hh]
            for w in range(1, NWIN):
                kcat = kcat + ks[g, w * KEYS : (w + 1) * KEYS, :] * slot[(hh + w) % 4]
            qbd = jnp.concatenate(
                [qs[g, w * KEYS : (w + 1) * KEYS, :] * slot[(hh + w) % 4] for w in range(NWIN)], axis=0)
            st = dot(kcat, qbd, NT) + bt_ref[h]
            p = jnp.exp2(st - jnp.max(st, axis=0, keepdims=True)).astype(BF)
            o = dot(vts[h], p)
            mine = jnp.where(win < KEYS, o[0:HD], jnp.where(win < 2 * KEYS, o[HD : 2 * HD], o[2 * HD : 3 * HD]))
            ots[h] = (mine * (1.0 / o[3 * HD : 3 * HD + 1])).astype(BF)
        return carry

    lax.fori_loop(0, HEADS // 4, four_heads, 0)
    first_token = 0
    for ho_ref in hos:
        pick = one_hot(where_ref, 1, first_token, ho_ref.shape[0])
        ho_ref[...] = dot(pick, ots[...].reshape(D, TOK), NT).astype(BF)
        first_token += ho_ref.shape[0]


def attention(layer, pieces, assemble, weights, where, counts, bq, gain, mbias, bt):
    (blocks, tags), first = weights
    n, m = len(pieces), len(blocks)
    vm = pl.BlockSpec(memory_space=pltpu.VMEM)
    return pl.pallas_call(
        lambda *refs: attn_kernel(n, layer, tags, assemble, first, *refs),
        out_shape=[jax.ShapeDtypeStruct((count, D), BF) for count in counts],
        in_specs=[vm] * (n + m + 5),
        out_specs=[vm] * len(counts),
        scratch_shapes=[
            pltpu.VMEM((TOK, D), F32),
            pltpu.VMEM((4, TOK, 128), BF),
            pltpu.VMEM((4, TOK, 128), BF),
            pltpu.VMEM((HEADS, NWIN * HD + 16, KEYS), BF),
            pltpu.VMEM((HEADS, HD, TOK), BF),
            pltpu.VMEM((3, D, D), BF),
        ],
        compiler_params=pltpu.CompilerParams(vmem_limit_bytes=20 * MIB),
        cost_estimate=pl.CostEstimate(flops=10_000_000_000, bytes_accessed=8_000_000, transcendentals=0),
        name="attention",
    )(*pieces, *blocks, where, bq, gain, mbias, bt)


def mlp_kernel(n_pieces, layer, tags, firsts, assemble, finish, *refs):
    pieces = refs[:n_pieces]
    ho_ref, bh_all, gain_ref, mbias_ref = refs[n_pieces : n_pieces + 4]
    bh_ref = bh_all.at[layer : layer + 1]
    at = n_pieces + 4
    blocks = []
    for shared, group in tags:
        if shared is not None:
            blocks.append(blocks[shared])
            continue
        blocks.append(refs[at : at + len(group)])
        at += len(group)
    tags = [group for _, group in tags]
    outs = refs[at:-5]
    xs, acc, wp_ref, wh_ref, wo_ref = refs[-5:]
    fetch_blocks(blocks[0], tags[0], firsts[0], 1, wp_ref, False)
    fetch_blocks(blocks[1], tags[1], firsts[1], 4, wh_ref, False)
    fetch_blocks(blocks[2], tags[2], firsts[2], 4, wo_ref, True)
    assemble(pieces, xs)
    mid = xs[...] + (dot(ho_ref[...], wp_ref[0]) + mbias_ref[layer, 2:3])
    xs[...] = mid
    n2 = layer_norm(mid, gain_ref[layer, 1:2], mbias_ref[layer, 1:2]).astype(BF)
    step = 512
    for c in range(FF // step):
        cols = slice(c * step, (c + 1) * step)
        z = dot(n2, wh_ref[c]) + bh_ref[:, cols]
        hid = (0.5 * z * (1.0 + lax.erf(z * math.sqrt(0.5)))).astype(BF)
        part = dot(hid, wo_ref[4 * c : 4 * c + 4].reshape(step, D))
        acc[...] = part if c == 0 else acc[...] + part
    xs[...] = xs[...] + (acc[...] + mbias_ref[layer, 3:4])
    finish(xs, outs)


def mlp(layer, pieces, assemble, finish, outs, weights, ho, bh, gain, mbias):
    tokens = ho.shape[0]
    tags, blocks = [], []
    for i, (group, _) in enumerate(weights):
        same = [j for j in range(i) if weights[j][0] is group]
        tags.append((same[0] if same else None, group[1]))
        blocks += () if same else group[0]
    firsts = [first for _, first in weights]
    n = len(pieces)
    vm = pl.BlockSpec(memory_space=pltpu.VMEM)
    return pl.pallas_call(
        lambda *refs: mlp_kernel(n, layer, tags, firsts, assemble, finish, *refs),
        out_shape=outs,
        in_specs=[vm] * (n + 4 + len(blocks)),
        out_specs=[vm] * len(outs),
        scratch_shapes=[
            pltpu.VMEM((tokens, D), F32),
            pltpu.VMEM((tokens, D), F32),
            pltpu.VMEM((1, D, D), BF),
            pltpu.VMEM((4, D, D), BF),
            pltpu.VMEM((16, 4, 32, D), BF),
        ],
        compiler_params=pltpu.CompilerParams(vmem_limit_bytes=20 * MIB),
        cost_estimate=pl.CostEstimate(flops=10_000_000_000, bytes_accessed=8_000_000, transcendentals=0),
        name="mlp",
    )(*pieces, ho, bh, gain, mbias, *blocks)


ROWS = WIN
COLS = WIN * NWIN
KEEP = COLS - SHIFT


def assemble_plain(pieces, xs):
    for r in range(ROWS):
        xs[r * COLS : (r + 1) * COLS, :] = pieces[0][r].astype(F32)


SENT = SHIFT * (COLS + SHIFT)


def assemble_sent(pieces, xs):
    right, below, corner = pieces
    for r in range(SHIFT):
        xs[r * COLS : r * COLS + KEEP, :] = below[r].astype(F32)
        xs[r * COLS + KEEP : (r + 1) * COLS, :] = corner[r].astype(F32)
        at = SHIFT * (COLS + r)
        xs[at : at + SHIFT, :] = right[r].astype(F32)


def assemble_kept(pieces, xs, base=0):
    for r in range(SHIFT):
        xs[base + r * KEEP : base + (r + 1) * KEEP, :] = pieces[0][r].astype(F32)


def assemble_shifted(pieces, xs):
    assemble_sent(pieces[1:], xs)
    assemble_kept(pieces, xs, SENT)


def finish_first(xs, outs):
    own, right, below, corner = outs
    for r in range(SHIFT):
        top = xs[r * COLS : (r + 1) * COLS, :].astype(BF)
        below[r] = top[SHIFT:]
        corner[r] = top[:SHIFT]
        low = xs[(r + SHIFT) * COLS : (r + SHIFT + 1) * COLS, :].astype(BF)
        own[r] = low[SHIFT:]
        right[r] = low[:SHIFT]


def finish_sent(xs, outs):
    right, below, corner = outs
    for r in range(SHIFT):
        low = xs[r * COLS : (r + 1) * COLS, :].astype(BF)
        below[r] = low[:KEEP]
        corner[r] = low[KEEP:]
        at = SHIFT * (COLS + r)
        right[r] = xs[at : at + SHIFT, :].astype(BF)


def finish_kept(xs, outs):
    for r in range(SHIFT):
        outs[0][r] = xs[r * KEEP : (r + 1) * KEEP, :].astype(BF)


def join_kernel(own, right, below, corner, out):
    for r in range(SHIFT):
        out[r] = jnp.concatenate([corner[r].astype(F32), below[r].astype(F32)], axis=0).astype(BF)
        out[r + SHIFT] = jnp.concatenate([right[r].astype(F32), own[r].astype(F32)], axis=0).astype(BF)


def join(*pieces):
    return pl.pallas_call(
        join_kernel,
        out_shape=jax.ShapeDtypeStruct((ROWS, COLS, D), BF),
        compiler_params=pltpu.CompilerParams(vmem_limit_bytes=4 * MIB),
        name="join",
    )(*pieces)


def part_shapes():
    return (
        jax.ShapeDtypeStruct((SHIFT, KEEP, D), BF),
        jax.ShapeDtypeStruct((SHIFT, SHIFT, D), BF),
        jax.ShapeDtypeStruct((SHIFT, KEEP, D), BF),
        jax.ShapeDtypeStruct((SHIFT, SHIFT, D), BF),
    )


def places(shifted):
    table = np.full((8, 512), -1, np.int32)
    for r in range(ROWS):
        for c in range(COLS):
            if not shifted:
                at = r * COLS + c
            elif r >= SHIFT:
                at = (r - SHIFT) * COLS + c
            elif c >= KEEP:
                at = SHIFT * (COLS + r) + c - KEEP
            else:
                at = SENT + r * KEEP + c
            place = (c // WIN) * KEYS + r * WIN + c % WIN
            table[0, at] = place
            table[1, place] = at
    return jnp.asarray(table)


def bias_rows(table):
    return jnp.pad(table.transpose(0, 2, 1, 3), ((0, 0), (0, 0), (0, 0), (0, 128 - (2 * WIN - 1))))


def send(block, where):
    pairs = []
    for at in np.ndindex(*SIZES):
        row, x, yh, c, img = at
        row2, x2, y2, c2 = where(row, x, yh * 2 + img, c)
        to = (row2 % 8, x2 % 4, y2 % 4 // 2, c2, y2 % 2)
        pairs.append((int(np.ravel_multi_index(at, SIZES)), int(np.ravel_multi_index(to, SIZES))))
    return lax.ppermute(block, AXES, pairs)


def shift_tokens(block, rows, cols):
    def where(row, x, y, c):
        col = (x * 4 + y // 2 * 2 + c + cols) % 16
        return row + rows, col // 4, col // 2 % 2 * 2 + y % 2, col % 2

    return send(block, where)


def swap_cores(block):
    return send(block, lambda row, x, y, c: (row, x, y, 1 - c))


def chunk_kernel(picks, n_in, *refs):
    arrays, outs, sem = refs[:n_in], refs[n_in:-1], refs[-1]
    copies = []
    for g, (out, group) in enumerate(zip(outs, picks)):
        at = 0
        for layer, which in group:
            ref = arrays[which]
            for rows in range(ref.shape[1] // 32):
                for lanes in range(ref.shape[2] // D):
                    part = ref.at[layer, pl.ds(rows * 32, 32), pl.ds(lanes * D, D)]
                    copies.append(pltpu.make_async_copy(part, out.at[at], sem.at[g, at]))
                    at += 1
    for copy in copies:
        copy.start()
    for copy in copies:
        copy.wait()


def chunks(picks, weights):
    sizes = [w.shape[1] // 32 * (w.shape[2] // D) for w in weights]
    counts = [sum(sizes[which] for _, which in group) for group in picks]
    return pl.pallas_call(
        lambda *refs: chunk_kernel(picks, len(weights), *refs),
        out_shape=[jax.ShapeDtypeStruct((n, 32, D), BF) for n in counts],
        in_specs=[pl.BlockSpec(memory_space=pltpu.HBM)] * len(weights),
        out_specs=[pl.BlockSpec(memory_space=pltpu.VMEM)] * len(counts),
        scratch_shapes=[pltpu.SemaphoreType.DMA((len(counts), max(counts)))],
        compiler_params=pltpu.CompilerParams(vmem_limit_bytes=8 * MIB),
        name="chunks",
    )(*weights)


X_MOVES = (1, 3, 2)


def join_x_kernel(n_after, own, *refs):
    came, out = refs[:3], refs[3 + n_after]
    x = lax.axis_index("x")
    for k, ref in enumerate((own, *came)):
        out[x if k == 0 else lax.rem(x + 4 - X_MOVES[k - 1], 4)] = ref[...]


def join_x(own, came, after):
    vm = pl.BlockSpec(memory_space=pltpu.VMEM)
    return pl.pallas_call(
        lambda *refs: join_x_kernel(len(after), *refs),
        out_shape=jax.ShapeDtypeStruct((4, *own.shape), BF),
        in_specs=[vm] * 4 + [pl.BlockSpec(memory_space=pl.ANY)] * len(after),
        out_specs=vm,
        compiler_params=pltpu.CompilerParams(vmem_limit_bytes=8 * MIB),
        name="join_x",
    )(own, *came, *after)


def pair_kernel(cuts, own, other, *refs):
    yh = lax.axis_index("yh")
    for (lo, hi), out in zip(cuts, refs[-len(cuts) :]):
        out[yh] = own[lo:hi]
        out[1 - yh] = other[lo:hi]


def pair(own, other, cuts, after):
    vm = pl.BlockSpec(memory_space=pltpu.VMEM)
    return pl.pallas_call(
        lambda *refs: pair_kernel(cuts, *refs),
        out_shape=[jax.ShapeDtypeStruct((2, hi - lo, 32, D), BF) for lo, hi in cuts],
        in_specs=[vm] * 2 + [pl.BlockSpec(memory_space=pl.ANY)] * len(after),
        out_specs=[vm] * len(cuts),
        compiler_params=pltpu.CompilerParams(vmem_limit_bytes=8 * MIB),
        name="pair",
    )(own, other, *after)


def along_x(block):
    return [send(block, lambda row, x, y, c, dx=dx: (row, x + dx, y, c)) for dx in X_MOVES]


def across_y(block):
    return send(block, lambda row, x, y, c: (row, x, 3 - y, c))


def spread_pair(both, came):
    blocks, tags = [], []
    for dx, block in zip((0, *X_MOVES), (both, *came)):
        blocks += [block, swap_cores(block)]
        tags += [("yh", 0, dx), ("yh", 1, dx)]
    return blocks, tags


def local(
    tokens,
    qkv_weight,
    proj_weight,
    hidden_weight,
    output_weight,
    norm_gain,
    model_bias,
    qkv_bias,
    hidden_bias,
    position_bias,
):
    weights = (qkv_weight, proj_weight, hidden_weight, output_weight)
    (first,) = chunks((((0, 0),),), (qkv_weight,))
    rest, second = chunks((((0, 1), (0, 2), (0, 3)), ((1, 0), (1, 1), (1, 2), (1, 3))), weights)
    rows = bias_rows(position_bias)
    first_y = across_y(first)
    second_y = across_y(second)
    rest_x = along_x(rest)
    (first,) = pair(first, first_y, ((0, 3),), ())
    first_x = along_x(first)
    qkv0 = spread_pair(first, first_x)
    attn1, mlp1 = pair(second, second_y, ((0, 4), (4, 12)), (first,))
    mine = join_x(rest, rest_x, (mlp1,))
    other = across_y(mine)
    attn1_x = along_x(attn1)
    mlp1_x = along_x(mlp1)
    table0 = bias_table(rows[0], False, (mine,))

    def attn(k, pieces, assemble, blocks, table, counts):
        params = (qkv_bias, norm_gain, model_bias, table)
        return attention(k, pieces, assemble, blocks, places(k), counts, *params)

    def feed(k, pieces, assemble, finish, outs, blocks, ho):
        return mlp(k, pieces, assemble, finish, outs, blocks, ho, hidden_bias, norm_gain, model_bias)

    def exchange(right, below, corner, way):
        corner = shift_tokens(corner, way, way)
        right = shift_tokens(right, 0, way)
        below = shift_tokens(below, way, 0)
        return right, below, corner

    (ho,) = attn(0, (tokens,), assemble_plain, (qkv0, 0), table0, (TOK,))
    rest0 = (mine, swap_cores(mine), other, swap_cores(other)), (("x", 0, 0), ("x", 1, 0), ("x", 0, 1), ("x", 1, 1))
    shapes = part_shapes()
    own, *halo = feed(
        0, (tokens,), assemble_plain, finish_first, shapes, ((rest0, 0), (rest0, 1), (rest0, 5)), ho
    )
    table1 = bias_table(rows[1], True, tuple(halo))
    pieces = (own, *exchange(*halo, -1))
    attn1 = spread_pair(attn1, attn1_x)
    mlp1 = spread_pair(mlp1, mlp1_x)
    sent_ho, kept_ho = attn(1, pieces, assemble_shifted, (attn1, 0), table1, (SENT, TOK - SENT))
    blocks = ((attn1, 3), (mlp1, 0), (mlp1, 4))
    sent = feed(1, pieces[1:], assemble_sent, finish_sent, shapes[1:], blocks, sent_ho)
    (own,) = feed(1, (pieces[0],), assemble_kept, finish_kept, shapes[:1], blocks, kept_ho)
    return join(own, *exchange(*sent, 1))


def solution(mesh):
    fine = jax.sharding.Mesh(mesh.devices.reshape(SIZES), AXES)
    tokens = P(("img", "row"), ("x", "yh", "c"), None)
    weight = P(None, ("x", "yh", "c"), None)
    in_specs = (tokens, weight, weight, weight, weight, P(), P(), P(), P(), P())

    return jax.shard_map(local, mesh=fine, in_specs=in_specs, out_specs=tokens, check_vma=False)
```

time: 160 us -> 120 us (0.75)
  the two profiles are of different devices: /device:TPU:8 before, /device:TPU:0 now
where the time goes in v2:
time: 120 us
  starting transfers between devices  42.5 us (35%)
  waiting for transfers between devices  41.9 us (35%)
  Pallas kernels  31.3 us (26%)
  local copies, waits for them, and re-layouts  3.74 us (3%)
    ppermute x35, starting transfers between devices, send(): return lax.ppermute(block, AXES, pairs)  42.5 us
    ppermute x35, waiting for transfers between devices, send(): return lax.ppermute(block, AXES, pairs)  41.9 us
    pallas_call x2, Pallas kernels, attention(): pl.pallas_call(lambda *refs: attn_kernel(n, layer, tags, assemble, first,...  13.4 us
    pallas_call x2, Pallas kernels, bias_table(): pl.pallas_call(body, out_shape=jax.ShapeDtypeStruct((HEADS, KEYS, TOK), F...  8.41 us
    pallas_call x3, Pallas kernels, mlp(): pl.pallas_call(lambda *refs: mlp_kernel(n, layer, tags, firsts, assemble,...  7.63 us
    unnamed x26, local copies, waits for them, and re-layouts  3.71 us
  transfers between devices with their start and end apart: 35, of which 12 were waited for; matrix products, arithmetic and copies ran while one was open for 0% of the time, Pallas kernels for 23%

profile of v2, /device:TPU:0, one launch (start us, length us, event | category | flops | bytes accessed | tf_op | source)
XLA Modules:
  0.0 119.8 jit_solution(2398110242321328446)
XLA Ops:
  4.4 1.4 %collective-permute-start.11 = (bf16[12,32,512]{2,1,0:T(8,128)(2,1)S(1)}, bf16[12,32,512]{2,1,0:T(8,128)(2,1)S(1)}, u32[]{:S(2)}, u32[]{:S(2)}) collective-permute-start(bf16[12,32,512]{2,1,0:T(8,128)(2,1)S(1)} %get-tuple-element.19.refs_0_), channel_id=1, source_target_pairs={{0,5},{1,4},{2,7},{3,6},{4,1},{5,0},{6,3},{7,2},{8,13},{9,12},{10,... | collective-permute-start | bytes 1179656 | tf_op jit(solution)/shard_map/ppermute | solution.py:403
  5.8 3.0 %collective-permute-start.10 = (bf16[9,32,512]{2,1,0:T(8,128)(2,1)S(1)}, bf16[9,32,512]{2,1,0:T(8,128)(2,1)S(1)}, u32[]{:S(2)}, u32[]{:S(2)}) collective-permute-start(bf16[9,32,512]{2,1,0:T(8,128)(2,1)S(1)} %get-tuple-element.18.refs_0_), channel_id=1, source_target_pairs={{0,16},{1,17},{2,18},{3,19},{4,20},{5,21},{6,22},{7,23},{8,24},{9,... | collective-permute-start | bytes 884744 | tf_op jit(solution)/shard_map/ppermute | solution.py:403
  9.4 2.6 %collective-permute-start.9 = (bf16[9,32,512]{2,1,0:T(8,128)(2,1)S(1)}, bf16[9,32,512]{2,1,0:T(8,128)(2,1)S(1)}, u32[]{:S(2)}, u32[]{:S(2)}) collective-permute-start(bf16[9,32,512]{2,1,0:T(8,128)(2,1)S(1)} %get-tuple-element.18.refs_0_), channel_id=1, source_target_pairs={{0,24},{1,25},{2,26},{3,27},{4,28},{5,29},{6,30},{7,31},{8,0},{9,1... | collective-permute-start | bytes 884744 | tf_op jit(solution)/shard_map/ppermute | solution.py:403
  12.4 5.6 %collective-permute-done.refs_1_ = bf16[3,32,512]{2,1,0:T(8,128)(2,1)S(1)} collective-permute-done((bf16[3,32,512]{2,1,0:T(8,128)(2,1)S(1)}, bf16[3,32,512]{2,1,0:T(8,128)(2,1)S(1)}, u32[]{:S(2)}, u32[]{:S(2)}) %collective-permute-start) | collective-permute-done | bytes 98336 | tf_op jit(solution)/shard_map/ppermute | solution.py:403
  18.2 3.9 %collective-permute-done.8.refs_1_ = bf16[9,32,512]{2,1,0:T(8,128)(2,1)S(1)} collective-permute-done((bf16[9,32,512]{2,1,0:T(8,128)(2,1)S(1)}, bf16[9,32,512]{2,1,0:T(8,128)(2,1)S(1)}, u32[]{:S(2)}, u32[]{:S(2)}) %collective-permute-start.8) | collective-permute-done | bytes 294944 | tf_op jit(solution)/shard_map/ppermute | solution.py:403
  22.8 1.4 %collective-permute-start.2 = (bf16[2,3,32,512]{3,2,1,0:T(8,128)(2,1)S(1)}, bf16[2,3,32,512]{3,2,1,0:T(8,128)(2,1)S(1)}, u32[]{:S(2)}, u32[]{:S(2)}) collective-permute-start(bf16[2,3,32,512]{3,2,1,0:T(8,128)(2,1)S(1)} %pair.2.refs_2_.refs_1_), channel_id=1, source_target_pairs={{0,8},{1,9},{2,10},{3,11},{4,12},{5,13},{6,14},{7,15},{8,16},{9,17... | collective-permute-start | bytes 589832 | tf_op jit(solution)/shard_map/ppermute | solution.py:403
  24.3 1.8 %collective-permute-start.4 = (bf16[2,3,32,512]{3,2,1,0:T(8,128)(2,1)S(1)}, bf16[2,3,32,512]{3,2,1,0:T(8,128)(2,1)S(1)}, u32[]{:S(2)}, u32[]{:S(2)}) collective-permute-start(bf16[2,3,32,512]{3,2,1,0:T(8,128)(2,1)S(1)} %pair.2.refs_2_.refs_1_), channel_id=1, source_target_pairs={{0,24},{1,25},{2,26},{3,27},{4,28},{5,29},{6,30},{7,31},{8,0},{9,1... | collective-permute-start | bytes 589832 | tf_op jit(solution)/shard_map/ppermute | solution.py:403
  26.9 3.8 %collective-permute-done.2.refs_3_ = bf16[2,3,32,512]{3,2,1,0:T(8,128)(2,1)S(1)} collective-permute-done((bf16[2,3,32,512]{3,2,1,0:T(8,128)(2,1)S(1)}, bf16[2,3,32,512]{3,2,1,0:T(8,128)(2,1)S(1)}, u32[]{:S(2)}, u32[]{:S(2)}) %collective-permute-start.2) | collective-permute-done | bytes 196640 | tf_op jit(solution)/shard_map/ppermute | solution.py:403
  30.7 1.4 %collective-permute-done.4.refs_5_ = bf16[2,3,32,512]{3,2,1,0:T(8,128)(2,1)S(1)} collective-permute-done((bf16[2,3,32,512]{3,2,1,0:T(8,128)(2,1)S(1)}, bf16[2,3,32,512]{3,2,1,0:T(8,128)(2,1)S(1)}, u32[]{:S(2)}, u32[]{:S(2)}) %collective-permute-start.4) | collective-permute-done | bytes 196640 | tf_op jit(solution)/shard_map/ppermute | solution.py:403
  32.0 3.6 %collective-permute-done.6.refs_7_ = bf16[2,3,32,512]{3,2,1,0:T(8,128)(2,1)S(1)} collective-permute-done((bf16[2,3,32,512]{3,2,1,0:T(8,128)(2,1)S(1)}, bf16[2,3,32,512]{3,2,1,0:T(8,128)(2,1)S(1)}, u32[]{:S(2)}, u32[]{:S(2)}) %collective-permute-start.6) | collective-permute-done | bytes 196640 | tf_op jit(solution)/shard_map/ppermute | solution.py:403
  35.6 1.1 collective-permute-start.19
  36.8 2.1 %collective-permute-start.21 = (bf16[2,4,32,512]{3,2,1,0:T(8,128)(2,1)S(1)}, bf16[2,4,32,512]{3,2,1,0:T(8,128)(2,1)S(1)}, u32[]{:S(2)}, u32[]{:S(2)}) collective-permute-start(bf16[2,4,32,512]{3,2,1,0:T(8,128)(2,1)S(1)} %get-tuple-element.25.refs_4_.refs_5_.refs_7_), channel_id=1, source_target_pairs={{0,24},{1,25},{2,26},{3,27},{4,28},{5,29},{6,30},{7,31},{8,0},{9,1... | collective-permute-start | bytes 786440 | tf_op jit(solution)/shard_map/ppermute | solution.py:403
  38.9 12.5 %collective-permute-done.13.refs_7_ = bf16[4,9,32,512]{3,2,1,0:T(8,128)(2,1)S(1)} collective-permute-done((bf16[4,9,32,512]{3,2,1,0:T(8,128)(2,1)S(1)}, bf16[4,9,32,512]{3,2,1,0:T(8,128)(2,1)S(1)}, u32[]{:S(2)}, u32[]{:S(2)}) %collective-permute-start.13) | collective-permute-done | bytes 1179680 | tf_op jit(solution)/shard_map/ppermute | solution.py:403
  52.0 4.2 %bias_table.2.refs_13_ = f32[16,144,432]{2,1,0:T(8,128)S(1)} custom-call(f32[23,16,128]{2,1,0:T(8,128)S(1)} %get-tuple-element.32.refs_0_, f32[8,512]{1,0:T(8,128)S(1)} %copy-done.3, bf16[4,9,32,512]{3,2,1,0:T(8,128)(2,1)S(1)} %join_x.1.refs_2_.refs_5_), custom_call_target="tpu_custom_call" | custom-call | tf_op jit(solution)/shard_map/bias_table/pallas_call | solution.py:111
  56.2 1.6 %collective-permute-start.23 = (bf16[2,4,32,512]{3,2,1,0:T(8,128)(2,1)S(1)}, bf16[2,4,32,512]{3,2,1,0:T(8,128)(2,1)S(1)}, u32[]{:S(2)}, u32[]{:S(2)}) collective-permute-start(bf16[2,4,32,512]{3,2,1,0:T(8,128)(2,1)S(1)} %get-tuple-element.25.refs_4_.refs_5_.refs_7_), channel_id=1, source_target_pairs={{0,16},{1,17},{2,18},{3,19},{4,20},{5,21},{6,22},{7,23},{8,24},{9,... | collective-permute-start | bytes 786440 | tf_op jit(solution)/shard_map/ppermute | solution.py:403
  58.3 6.7 %attention.2.refs_1_ = bf16[432,512]{1,0:T(8,128)(2,1)S(1)} custom-call(bf16[12,36,512]{2,1,0:T(8,128)(2,1)S(1)} %copy-done.5, bf16[2,3,32,512]{3,2,1,0:T(8,128)(2,1)S(1)} %pair.2.refs_2_.refs_1_, bf16[2,3,32,512]{3,2,1,0:T(8,128)(2,1)S(1)} %collective-permute-done.1.refs_2_, bf16[2,3,32,512]{3,2,1,0:T(8,128)(2,1)S(1)} %collective-permute-done.2.refs_3_, ...), custom_call_target="tpu_custom_call" | custom-call | flops 10000000000 | bytes 8000000 | tf_op jit(solution)/shard_map/attention/pallas_call | solution.py:212
  65.0 1.2 %collective-permute-done.23.refs_10_.refs_11_.refs_13_ = bf16[2,4,32,512]{3,2,1,0:T(8,128)(2,1)S(1)} collective-permute-done((bf16[2,4,32,512]{3,2,1,0:T(8,128)(2,1)S(1)}, bf16[2,4,32,512]{3,2,1,0:T(8,128)(2,1)S(1)}, u32[]{:S(2)}, u32[]{:S(2)}) %collective-permute-start.23) | collective-permute-done | bytes 262176 | tf_op jit(solution)/shard_map/ppermute | solution.py:403
  66.2 1.5 %collective-permute-start.26 = (bf16[2,8,32,512]{3,2,1,0:T(8,128)(2,1)S(1)}, bf16[2,8,32,512]{3,2,1,0:T(8,128)(2,1)S(1)}, u32[]{:S(2)}, u32[]{:S(2)}) collective-permute-start(bf16[2,8,32,512]{3,2,1,0:T(8,128)(2,1)S(1)} %get-tuple-element.20.refs_4_.refs_13_.refs_15_), channel_id=1, source_target_pairs={{0,8},{1,9},{2,10},{3,11},{4,12},{5,13},{6,14},{7,15},{8,16},{9,17... | collective-permute-start | bytes 1572872 | tf_op jit(solution)/shard_map/ppermute | solution.py:403
  67.7 1.8 %collective-permute-start.28 = (bf16[2,8,32,512]{3,2,1,0:T(8,128)(2,1)S(1)}, bf16[2,8,32,512]{3,2,1,0:T(8,128)(2,1)S(1)}, u32[]{:S(2)}, u32[]{:S(2)}) collective-permute-start(bf16[2,8,32,512]{3,2,1,0:T(8,128)(2,1)S(1)} %get-tuple-element.20.refs_4_.refs_13_.refs_15_), channel_id=1, source_target_pairs={{0,24},{1,25},{2,26},{3,27},{4,28},{5,29},{6,30},{7,31},{8,0},{9,1... | collective-permute-start | bytes 1572872 | tf_op jit(solution)/shard_map/ppermute | solution.py:403
  69.5 1.1 collective-permute-start.30
  71.1 3.2 %mlp.3 = (bf16[6,30,512]{2,1,0:T(8,128)(2,1)S(1)}, bf16[6,6,512]{2,1,0:T(8,128)(2,1)S(1)}, bf16[6,30,512]{2,1,0:T(8,128)(2,1)S(1)}, bf16[6,6,512]{2,1,0:T(8,128)(2,1)S(1)}) custom-call(bf16[12,36,512]{2,1,0:T(8,128)(2,1)S(1)} %copy-done.5, bf16[432,512]{1,0:T(8,128)(2,1)S(1)} %attention.2.refs_1_, f32[2,2048]{1,0:T(2,128)S(1)} %copy-done.7, ...), custom_call_target="tpu_custom_call" | custom-call | flops 10000000000 | bytes 8000000 | tf_op jit(solution)/shard_map/mlp/pallas_call | solution.py:274
  74.3 5.9 %collective-permute-start.16 = (bf16[6,30,512]{2,1,0:T(8,128)(2,1)S(1)}, bf16[6,30,512]{2,1,0:T(8,128)(2,1)S(1)}, u32[]{:S(2)}, u32[]{:S(2)}) collective-permute-start(bf16[6,30,512]{2,1,0:T(8,128)(2,1)S(1)} %get-tuple-element.23.refs_3_), channel_id=1, source_target_pairs={{0,224},{1,225},{2,226},{3,227},{4,228},{5,229},{6,230},{7,231},{8... | collective-permute-start | bytes 552968 | tf_op jit(solution)/shard_map/ppermute | solution.py:403
  81.3 2.8 %collective-permute-start.17 = (bf16[6,6,512]{2,1,0:T(8,128)(2,1)S(1)}, bf16[6,6,512]{2,1,0:T(8,128)(2,1)S(1)}, u32[]{:S(2)}, u32[]{:S(2)}) collective-permute-start(bf16[6,6,512]{2,1,0:T(8,128)(2,1)S(1)} %get-tuple-element.24.refs_4_), channel_id=1, source_target_pairs={{0,254},{1,255},{2,224},{3,225},{4,226},{5,227},{6,228},{7,229},{8... | collective-permute-start | bytes 110600 | tf_op jit(solution)/shard_map/ppermute | solution.py:403
  84.0 4.2 %bias_table.3.refs_16_ = f32[16,144,432]{2,1,0:T(8,128)S(1)} custom-call(f32[23,16,128]{2,1,0:T(8,128)S(1)} %get-tuple-element.31.refs_0_, f32[8,512]{1,0:T(8,128)S(1)} %copy-done.3, bf16[6,6,512]{2,1,0:T(8,128)(2,1)S(1)} %get-tuple-element.22.refs_2_, bf16[6,30,512]{2,1,0:T(8,128)(2,1)S(1)} %get-tuple-element.23.refs_3_, ...), custom_call_target="tpu_custom_call" | custom-call | tf_op jit(solution)/shard_map/bias_table/pallas_call | solution.py:111
  88.3 3.3 %collective-permute-start.25 = (bf16[2,8,32,512]{3,2,1,0:T(8,128)(2,1)S(1)}, bf16[2,8,32,512]{3,2,1,0:T(8,128)(2,1)S(1)}, u32[]{:S(2)}, u32[]{:S(2)}) collective-permute-start(bf16[2,8,32,512]{3,2,1,0:T(8,128)(2,1)S(1)} %get-tuple-element.20.refs_4_.refs_13_.refs_15_), channel_id=1, source_target_pairs={{0,2},{1,3},{2,0},{3,1},{4,6},{5,7},{6,4},{7,5},{8,10},{9,11},{10,... | collective-permute-start | bytes 1572872 | tf_op jit(solution)/shard_map/ppermute | solution.py:403
  91.6 1.1 collective-permute-done.30.refs_19_.refs_21_
  93.3 6.8 %attention.3 = (bf16[252,512]{1,0:T(8,128)(2,1)S(1)}, bf16[180,512]{1,0:T(8,128)(2,1)S(1)}) custom-call(bf16[6,30,512]{2,1,0:T(8,128)(2,1)S(1)} %get-tuple-element.21.refs_0_, bf16[6,6,512]{2,1,0:T(8,128)(2,1)S(1)} %collective-permute-done.15.refs_1_.refs_0_, bf16[6,30,512]{2,1,0:T(8,128)(2,1)S(1)} %collective-permute-done.16.refs_2_.refs_1_, ...), custom_call_target="tpu_custom_call" | custom-call | flops 10000000000 | bytes 8000000 | tf_op jit(solution)/shard_map/attention/pallas_call | solution.py:212
  100.1 2.4 %mlp.5 = (bf16[6,6,512]{2,1,0:T(8,128)(2,1)S(1)}, bf16[6,30,512]{2,1,0:T(8,128)(2,1)S(1)}, bf16[6,6,512]{2,1,0:T(8,128)(2,1)S(1)}) custom-call(bf16[6,6,512]{2,1,0:T(8,128)(2,1)S(1)} %collective-permute-done.15.refs_1_.refs_0_, bf16[6,30,512]{2,1,0:T(8,128)(2,1)S(1)} %collective-permute-done.16.refs_2_.refs_1_, ...), custom_call_target="tpu_custom_call" | custom-call | flops 10000000000 | bytes 8000000 | tf_op jit(solution)/shard_map/mlp/pallas_call | solution.py:274
  102.4 2.0 %collective-permute-start.33 = (bf16[6,30,512]{2,1,0:T(8,128)(2,1)S(1)}, bf16[6,30,512]{2,1,0:T(8,128)(2,1)S(1)}, u32[]{:S(2)}, u32[]{:S(2)}) collective-permute-start(bf16[6,30,512]{2,1,0:T(8,128)(2,1)S(1)} %get-tuple-element.29), channel_id=1, source_target_pairs={{0,32},{1,33},{2,34},{3,35},{4,36},{5,37},{6,38},{7,39},{8,40},{9,... | collective-permute-start | bytes 552968 | tf_op jit(solution)/shard_map/ppermute | solution.py:403
  104.6 4.5 %collective-permute-start.34 = (bf16[6,6,512]{2,1,0:T(8,128)(2,1)S(1)}, bf16[6,6,512]{2,1,0:T(8,128)(2,1)S(1)}, u32[]{:S(2)}, u32[]{:S(2)}) collective-permute-start(bf16[6,6,512]{2,1,0:T(8,128)(2,1)S(1)} %get-tuple-element.30), channel_id=1, source_target_pairs={{0,34},{1,35},{2,36},{3,37},{4,38},{5,39},{6,40},{7,41},{8,42},{9,... | collective-permute-start | bytes 110600 | tf_op jit(solution)/shard_map/ppermute | solution.py:403
  109.0 2.0 %mlp.4.own = bf16[6,30,512]{2,1,0:T(8,128)(2,1)S(1)} custom-call(bf16[6,30,512]{2,1,0:T(8,128)(2,1)S(1)} %get-tuple-element.21.refs_0_, bf16[180,512]{1,0:T(8,128)(2,1)S(1)} %get-tuple-element.26.refs_1_, f32[2,2048]{1,0:T(2,128)S(1)} %copy-done.7, f32[2,2,512]{2,1,0:T(2,128)S(1)} %copy-done.9, f32[2,4,512]{2,1,0:T(4,128)S(1)} %copy-done.6, ...), custom_call_target="tpu_custom_call" | custom-call | flops 10000000000 | bytes 8000000 | tf_op jit(solution)/shard_map/mlp/pallas_call | solution.py:274
  111.6 7.3 %collective-permute-done.34.corner = bf16[6,6,512]{2,1,0:T(8,128)(2,1)S(1)} collective-permute-done((bf16[6,6,512]{2,1,0:T(8,128)(2,1)S(1)}, bf16[6,6,512]{2,1,0:T(8,128)(2,1)S(1)}, u32[]{:S(2)}, u32[]{:S(2)}) %collective-permute-start.34) | collective-permute-done | bytes 36896 | tf_op jit(solution)/shard_map/ppermute | solution.py:403
  (78 shorter events, 11.8 us)
Async XLA Ops:
  4.4 13.7 %collective-permute-start.11 = (bf16[12,32,512]{2,1,0:T(8,128)(2,1)S(1)}, bf16[12,32,512]{2,1,0:T(8,128)(2,1)S(1)}, u32[]{:S(2)}, u32[]{:S(2)}) collective-permute-start(bf16[12,32,512]{2,1,0:T(8,128)(2,1)S(1)} %get-tuple-element.19.refs_0_), channel_id=1, source_target_pairs={{0,5},{1,4},{2,7},{3,6},{4,1},{5,0},{6,3},{7,2},{8,13},{9,12},{10,... | collective-permute-start | bytes 1179656 | tf_op jit(solution)/shard_map/ppermute | solution.py:403
  5.8 12.3 %collective-permute-start.10 = (bf16[9,32,512]{2,1,0:T(8,128)(2,1)S(1)}, bf16[9,32,512]{2,1,0:T(8,128)(2,1)S(1)}, u32[]{:S(2)}, u32[]{:S(2)}) collective-permute-start(bf16[9,32,512]{2,1,0:T(8,128)(2,1)S(1)} %get-tuple-element.18.refs_0_), channel_id=1, source_target_pairs={{0,16},{1,17},{2,18},{3,19},{4,20},{5,21},{6,22},{7,23},{8,24},{9,... | collective-permute-start | bytes 884744 | tf_op jit(solution)/shard_map/ppermute | solution.py:403
  8.8 13.3 %collective-permute-start.8 = (bf16[9,32,512]{2,1,0:T(8,128)(2,1)S(1)}, bf16[9,32,512]{2,1,0:T(8,128)(2,1)S(1)}, u32[]{:S(2)}, u32[]{:S(2)}) collective-permute-start(bf16[9,32,512]{2,1,0:T(8,128)(2,1)S(1)} %get-tuple-element.18.refs_0_), channel_id=1, source_target_pairs={{0,8},{1,9},{2,10},{3,11},{4,12},{5,13},{6,14},{7,15},{8,16},{9,17... | collective-permute-start | bytes 884744 | tf_op jit(solution)/shard_map/ppermute | solution.py:403
  9.4 12.8 %collective-permute-start.9 = (bf16[9,32,512]{2,1,0:T(8,128)(2,1)S(1)}, bf16[9,32,512]{2,1,0:T(8,128)(2,1)S(1)}, u32[]{:S(2)}, u32[]{:S(2)}) collective-permute-start(bf16[9,32,512]{2,1,0:T(8,128)(2,1)S(1)} %get-tuple-element.18.refs_0_), channel_id=1, source_target_pairs={{0,24},{1,25},{2,26},{3,27},{4,28},{5,29},{6,30},{7,31},{8,0},{9,1... | collective-permute-start | bytes 884744 | tf_op jit(solution)/shard_map/ppermute | solution.py:403
  22.3 29.1 %collective-permute-start.13 = (bf16[4,9,32,512]{3,2,1,0:T(8,128)(2,1)S(1)}, bf16[4,9,32,512]{3,2,1,0:T(8,128)(2,1)S(1)}, u32[]{:S(2)}, u32[]{:S(2)}) collective-permute-start(bf16[4,9,32,512]{3,2,1,0:T(8,128)(2,1)S(1)} %join_x.1.refs_2_.refs_5_), channel_id=1, source_target_pairs={{0,5},{1,4},{2,7},{3,6},{4,1},{5,0},{6,3},{7,2},{8,13},{9,12},{10,... | collective-permute-start | bytes 3538952 | tf_op jit(solution)/shard_map/ppermute | solution.py:403
  22.8 7.9 %collective-permute-start.2 = (bf16[2,3,32,512]{3,2,1,0:T(8,128)(2,1)S(1)}, bf16[2,3,32,512]{3,2,1,0:T(8,128)(2,1)S(1)}, u32[]{:S(2)}, u32[]{:S(2)}) collective-permute-start(bf16[2,3,32,512]{3,2,1,0:T(8,128)(2,1)S(1)} %pair.2.refs_2_.refs_1_), channel_id=1, source_target_pairs={{0,8},{1,9},{2,10},{3,11},{4,12},{5,13},{6,14},{7,15},{8,16},{9,17... | collective-permute-start | bytes 589832 | tf_op jit(solution)/shard_map/ppermute | solution.py:403
  24.3 7.8 %collective-permute-start.4 = (bf16[2,3,32,512]{3,2,1,0:T(8,128)(2,1)S(1)}, bf16[2,3,32,512]{3,2,1,0:T(8,128)(2,1)S(1)}, u32[]{:S(2)}, u32[]{:S(2)}) collective-permute-start(bf16[2,3,32,512]{3,2,1,0:T(8,128)(2,1)S(1)} %pair.2.refs_2_.refs_1_), channel_id=1, source_target_pairs={{0,24},{1,25},{2,26},{3,27},{4,28},{5,29},{6,30},{7,31},{8,0},{9,1... | collective-permute-start | bytes 589832 | tf_op jit(solution)/shard_map/ppermute | solution.py:403
  26.0 9.6 %collective-permute-start.6 = (bf16[2,3,32,512]{3,2,1,0:T(8,128)(2,1)S(1)}, bf16[2,3,32,512]{3,2,1,0:T(8,128)(2,1)S(1)}, u32[]{:S(2)}, u32[]{:S(2)}) collective-permute-start(bf16[2,3,32,512]{3,2,1,0:T(8,128)(2,1)S(1)} %pair.2.refs_2_.refs_1_), channel_id=1, source_target_pairs={{0,16},{1,17},{2,18},{3,19},{4,20},{5,21},{6,22},{7,23},{8,24},{9,... | collective-permute-start | bytes 589832 | tf_op jit(solution)/shard_map/ppermute | solution.py:403
  26.9 9.9 %collective-permute-start.1 = (bf16[2,3,32,512]{3,2,1,0:T(8,128)(2,1)S(1)}, bf16[2,3,32,512]{3,2,1,0:T(8,128)(2,1)S(1)}, u32[]{:S(2)}, u32[]{:S(2)}) collective-permute-start(bf16[2,3,32,512]{3,2,1,0:T(8,128)(2,1)S(1)} %pair.2.refs_2_.refs_1_), channel_id=1, source_target_pairs={{0,2},{1,3},{2,0},{3,1},{4,6},{5,7},{6,4},{7,5},{8,10},{9,11},{10,... | collective-permute-start | bytes 589832 | tf_op jit(solution)/shard_map/ppermute | solution.py:403
  30.7 8.2 %collective-permute-start.3 = (bf16[2,3,32,512]{3,2,1,0:T(8,128)(2,1)S(1)}, bf16[2,3,32,512]{3,2,1,0:T(8,128)(2,1)S(1)}, u32[]{:S(2)}, u32[]{:S(2)}) collective-permute-start(bf16[2,3,32,512]{3,2,1,0:T(8,128)(2,1)S(1)} %collective-permute-done.2.refs_3_), channel_id=1, source_target_pairs={{0,2},{1,3},{2,0},{3,1},{4,6},{5,7},{6,4},{7,5},{8,10},{9,11},{10,... | collective-permute-start | bytes 589832 | tf_op jit(solution)/shard_map/ppermute | solution.py:403
  32.0 19.4 %collective-permute-start.5 = (bf16[2,3,32,512]{3,2,1,0:T(8,128)(2,1)S(1)}, bf16[2,3,32,512]{3,2,1,0:T(8,128)(2,1)S(1)}, u32[]{:S(2)}, u32[]{:S(2)}) collective-permute-start(bf16[2,3,32,512]{3,2,1,0:T(8,128)(2,1)S(1)} %collective-permute-done.4.refs_5_), channel_id=1, source_target_pairs={{0,2},{1,3},{2,0},{3,1},{4,6},{5,7},{6,4},{7,5},{8,10},{9,11},{10,... | collective-permute-start | bytes 589832 | tf_op jit(solution)/shard_map/ppermute | solution.py:403
  35.6 22.2 %collective-permute-start.19 = (bf16[2,4,32,512]{3,2,1,0:T(8,128)(2,1)S(1)}, bf16[2,4,32,512]{3,2,1,0:T(8,128)(2,1)S(1)}, u32[]{:S(2)}, u32[]{:S(2)}) collective-permute-start(bf16[2,4,32,512]{3,2,1,0:T(8,128)(2,1)S(1)} %get-tuple-element.25.refs_4_.refs_5_.refs_7_), channel_id=1, source_target_pairs={{0,8},{1,9},{2,10},{3,11},{4,12},{5,13},{6,14},{7,15},{8,16},{9,17... | collective-permute-start | bytes 786440 | tf_op jit(solution)/shard_map/ppermute | solution.py:403
  36.8 21.0 %collective-permute-start.21 = (bf16[2,4,32,512]{3,2,1,0:T(8,128)(2,1)S(1)}, bf16[2,4,32,512]{3,2,1,0:T(8,128)(2,1)S(1)}, u32[]{:S(2)}, u32[]{:S(2)}) collective-permute-start(bf16[2,4,32,512]{3,2,1,0:T(8,128)(2,1)S(1)} %get-tuple-element.25.refs_4_.refs_5_.refs_7_), channel_id=1, source_target_pairs={{0,24},{1,25},{2,26},{3,27},{4,28},{5,29},{6,30},{7,31},{8,0},{9,1... | collective-permute-start | bytes 786440 | tf_op jit(solution)/shard_map/ppermute | solution.py:403
  38.9 31.7 %collective-permute-start.12 = (bf16[4,9,32,512]{3,2,1,0:T(8,128)(2,1)S(1)}, bf16[4,9,32,512]{3,2,1,0:T(8,128)(2,1)S(1)}, u32[]{:S(2)}, u32[]{:S(2)}) collective-permute-start(bf16[4,9,32,512]{3,2,1,0:T(8,128)(2,1)S(1)} %join_x.1.refs_2_.refs_5_), channel_id=1, source_target_pairs={{0,2},{1,3},{2,0},{3,1},{4,6},{5,7},{6,4},{7,5},{8,10},{9,11},{10,... | collective-permute-start | bytes 3538952 | tf_op jit(solution)/shard_map/ppermute | solution.py:403
  51.4 19.1 %collective-permute-start.14 = (bf16[4,9,32,512]{3,2,1,0:T(8,128)(2,1)S(1)}, bf16[4,9,32,512]{3,2,1,0:T(8,128)(2,1)S(1)}, u32[]{:S(2)}, u32[]{:S(2)}) collective-permute-start(bf16[4,9,32,512]{3,2,1,0:T(8,128)(2,1)S(1)} %collective-permute-done.13.refs_7_), channel_id=1, source_target_pairs={{0,2},{1,3},{2,0},{3,1},{4,6},{5,7},{6,4},{7,5},{8,10},{9,11},{10,... | collective-permute-start | bytes 3538952 | tf_op jit(solution)/shard_map/ppermute | solution.py:403
  56.2 10.0 %collective-permute-start.23 = (bf16[2,4,32,512]{3,2,1,0:T(8,128)(2,1)S(1)}, bf16[2,4,32,512]{3,2,1,0:T(8,128)(2,1)S(1)}, u32[]{:S(2)}, u32[]{:S(2)}) collective-permute-start(bf16[2,4,32,512]{3,2,1,0:T(8,128)(2,1)S(1)} %get-tuple-element.25.refs_4_.refs_5_.refs_7_), channel_id=1, source_target_pairs={{0,16},{1,17},{2,18},{3,19},{4,20},{5,21},{6,22},{7,23},{8,24},{9,... | collective-permute-start | bytes 786440 | tf_op jit(solution)/shard_map/ppermute | solution.py:403
  57.8 9.9 %collective-permute-start.18 = (bf16[2,4,32,512]{3,2,1,0:T(8,128)(2,1)S(1)}, bf16[2,4,32,512]{3,2,1,0:T(8,128)(2,1)S(1)}, u32[]{:S(2)}, u32[]{:S(2)}) collective-permute-start(bf16[2,4,32,512]{3,2,1,0:T(8,128)(2,1)S(1)} %get-tuple-element.25.refs_4_.refs_5_.refs_7_), channel_id=1, source_target_pairs={{0,2},{1,3},{2,0},{3,1},{4,6},{5,7},{6,4},{7,5},{8,10},{9,11},{10,... | collective-permute-start | bytes 786440 | tf_op jit(solution)/shard_map/ppermute | solution.py:403
  57.8 11.7 %collective-permute-start.20 = (bf16[2,4,32,512]{3,2,1,0:T(8,128)(2,1)S(1)}, bf16[2,4,32,512]{3,2,1,0:T(8,128)(2,1)S(1)}, u32[]{:S(2)}, u32[]{:S(2)}) collective-permute-start(bf16[2,4,32,512]{3,2,1,0:T(8,128)(2,1)S(1)} %collective-permute-done.19.refs_6_.refs_7_.refs_9_), channel_id=1, source_target_pairs={{0,2},{1,3},{2,0},{3,1},{4,6},{5,7},{6,4},{7,5},{8,10},{9,11},{10,... | collective-permute-start | bytes 786440 | tf_op jit(solution)/shard_map/ppermute | solution.py:403
  66.2 15.0 %collective-permute-start.26 = (bf16[2,8,32,512]{3,2,1,0:T(8,128)(2,1)S(1)}, bf16[2,8,32,512]{3,2,1,0:T(8,128)(2,1)S(1)}, u32[]{:S(2)}, u32[]{:S(2)}) collective-permute-start(bf16[2,8,32,512]{3,2,1,0:T(8,128)(2,1)S(1)} %get-tuple-element.20.refs_4_.refs_13_.refs_15_), channel_id=1, source_target_pairs={{0,8},{1,9},{2,10},{3,11},{4,12},{5,13},{6,14},{7,15},{8,16},{9,17... | collective-permute-start | bytes 1572872 | tf_op jit(solution)/shard_map/ppermute | solution.py:403
  67.7 20.5 %collective-permute-start.28 = (bf16[2,8,32,512]{3,2,1,0:T(8,128)(2,1)S(1)}, bf16[2,8,32,512]{3,2,1,0:T(8,128)(2,1)S(1)}, u32[]{:S(2)}, u32[]{:S(2)}) collective-permute-start(bf16[2,8,32,512]{3,2,1,0:T(8,128)(2,1)S(1)} %get-tuple-element.20.refs_4_.refs_13_.refs_15_), channel_id=1, source_target_pairs={{0,24},{1,25},{2,26},{3,27},{4,28},{5,29},{6,30},{7,31},{8,0},{9,1... | collective-permute-start | bytes 1572872 | tf_op jit(solution)/shard_map/ppermute | solution.py:403
  69.5 23.2 %collective-permute-start.30 = (bf16[2,8,32,512]{3,2,1,0:T(8,128)(2,1)S(1)}, bf16[2,8,32,512]{3,2,1,0:T(8,128)(2,1)S(1)}, u32[]{:S(2)}, u32[]{:S(2)}) collective-permute-start(bf16[2,8,32,512]{3,2,1,0:T(8,128)(2,1)S(1)} %get-tuple-element.20.refs_4_.refs_13_.refs_15_), channel_id=1, source_target_pairs={{0,16},{1,17},{2,18},{3,19},{4,20},{5,21},{6,22},{7,23},{8,24},{9,... | collective-permute-start | bytes 1572872 | tf_op jit(solution)/shard_map/ppermute | solution.py:403
  70.6 9.7 %collective-permute-start.24 = (bf16[2,4,32,512]{3,2,1,0:T(8,128)(2,1)S(1)}, bf16[2,4,32,512]{3,2,1,0:T(8,128)(2,1)S(1)}, u32[]{:S(2)}, u32[]{:S(2)}) collective-permute-start(bf16[2,4,32,512]{3,2,1,0:T(8,128)(2,1)S(1)} %collective-permute-done.23.refs_10_.refs_11_.refs_13_), channel_id=1, source_target_pairs={{0,2},{1,3},{2,0},{3,1},{4,6},{5,7},{6,4},{7,5},{8,10},{9,11},{10,... | collective-permute-start | bytes 786440 | tf_op jit(solution)/shard_map/ppermute | solution.py:403
  74.3 18.9 %collective-permute-start.16 = (bf16[6,30,512]{2,1,0:T(8,128)(2,1)S(1)}, bf16[6,30,512]{2,1,0:T(8,128)(2,1)S(1)}, u32[]{:S(2)}, u32[]{:S(2)}) collective-permute-start(bf16[6,30,512]{2,1,0:T(8,128)(2,1)S(1)} %get-tuple-element.23.refs_3_), channel_id=1, source_target_pairs={{0,224},{1,225},{2,226},{3,227},{4,228},{5,229},{6,230},{7,231},{8... | collective-permute-start | bytes 552968 | tf_op jit(solution)/shard_map/ppermute | solution.py:403
  80.3 12.4 %collective-permute-start.15 = (bf16[6,6,512]{2,1,0:T(8,128)(2,1)S(1)}, bf16[6,6,512]{2,1,0:T(8,128)(2,1)S(1)}, u32[]{:S(2)}, u32[]{:S(2)}) collective-permute-start(bf16[6,6,512]{2,1,0:T(8,128)(2,1)S(1)} %get-tuple-element.22.refs_2_), channel_id=1, source_target_pairs={{0,30},{1,31},{2,0},{3,1},{4,2},{5,3},{6,4},{7,5},{8,6},{9,7},{10,... | collective-permute-start | bytes 110600 | tf_op jit(solution)/shard_map/ppermute | solution.py:403
  81.3 11.9 %collective-permute-start.17 = (bf16[6,6,512]{2,1,0:T(8,128)(2,1)S(1)}, bf16[6,6,512]{2,1,0:T(8,128)(2,1)S(1)}, u32[]{:S(2)}, u32[]{:S(2)}) collective-permute-start(bf16[6,6,512]{2,1,0:T(8,128)(2,1)S(1)} %get-tuple-element.24.refs_4_), channel_id=1, source_target_pairs={{0,254},{1,255},{2,224},{3,225},{4,226},{5,227},{6,228},{7,229},{8... | collective-permute-start | bytes 110600 | tf_op jit(solution)/shard_map/ppermute | solution.py:403
  88.3 11.7 %collective-permute-start.25 = (bf16[2,8,32,512]{3,2,1,0:T(8,128)(2,1)S(1)}, bf16[2,8,32,512]{3,2,1,0:T(8,128)(2,1)S(1)}, u32[]{:S(2)}, u32[]{:S(2)}) collective-permute-start(bf16[2,8,32,512]{3,2,1,0:T(8,128)(2,1)S(1)} %get-tuple-element.20.refs_4_.refs_13_.refs_15_), channel_id=1, source_target_pairs={{0,2},{1,3},{2,0},{3,1},{4,6},{5,7},{6,4},{7,5},{8,10},{9,11},{10,... | collective-permute-start | bytes 1572872 | tf_op jit(solution)/shard_map/ppermute | solution.py:403
  92.6 7.4 %collective-permute-start.27 = (bf16[2,8,32,512]{3,2,1,0:T(8,128)(2,1)S(1)}, bf16[2,8,32,512]{3,2,1,0:T(8,128)(2,1)S(1)}, u32[]{:S(2)}, u32[]{:S(2)}) collective-permute-start(bf16[2,8,32,512]{3,2,1,0:T(8,128)(2,1)S(1)} %collective-permute-done.26.refs_15_.refs_17_), channel_id=1, source_target_pairs={{0,2},{1,3},{2,0},{3,1},{4,6},{5,7},{6,4},{7,5},{8,10},{9,11},{10,... | collective-permute-start | bytes 1572872 | tf_op jit(solution)/shard_map/ppermute | solution.py:403
  92.6 7.4 %collective-permute-start.29 = (bf16[2,8,32,512]{3,2,1,0:T(8,128)(2,1)S(1)}, bf16[2,8,32,512]{3,2,1,0:T(8,128)(2,1)S(1)}, u32[]{:S(2)}, u32[]{:S(2)}) collective-permute-start(bf16[2,8,32,512]{3,2,1,0:T(8,128)(2,1)S(1)} %collective-permute-done.28.refs_17_.refs_19_), channel_id=1, source_target_pairs={{0,2},{1,3},{2,0},{3,1},{4,6},{5,7},{6,4},{7,5},{8,10},{9,11},{10,... | collective-permute-start | bytes 1572872 | tf_op jit(solution)/shard_map/ppermute | solution.py:403
  93.2 6.9 %collective-permute-start.31 = (bf16[2,8,32,512]{3,2,1,0:T(8,128)(2,1)S(1)}, bf16[2,8,32,512]{3,2,1,0:T(8,128)(2,1)S(1)}, u32[]{:S(2)}, u32[]{:S(2)}) collective-permute-start(bf16[2,8,32,512]{3,2,1,0:T(8,128)(2,1)S(1)} %collective-permute-done.30.refs_19_.refs_21_), channel_id=1, source_target_pairs={{0,2},{1,3},{2,0},{3,1},{4,6},{5,7},{6,4},{7,5},{8,10},{9,11},{10,... | collective-permute-start | bytes 1572872 | tf_op jit(solution)/shard_map/ppermute | solution.py:403
  102.4 16.5 %collective-permute-start.33 = (bf16[6,30,512]{2,1,0:T(8,128)(2,1)S(1)}, bf16[6,30,512]{2,1,0:T(8,128)(2,1)S(1)}, u32[]{:S(2)}, u32[]{:S(2)}) collective-permute-start(bf16[6,30,512]{2,1,0:T(8,128)(2,1)S(1)} %get-tuple-element.29), channel_id=1, source_target_pairs={{0,32},{1,33},{2,34},{3,35},{4,36},{5,37},{6,38},{7,39},{8,40},{9,... | collective-permute-start | bytes 552968 | tf_op jit(solution)/shard_map/ppermute | solution.py:403
  104.4 7.1 %collective-permute-start.32 = (bf16[6,6,512]{2,1,0:T(8,128)(2,1)S(1)}, bf16[6,6,512]{2,1,0:T(8,128)(2,1)S(1)}, u32[]{:S(2)}, u32[]{:S(2)}) collective-permute-start(bf16[6,6,512]{2,1,0:T(8,128)(2,1)S(1)} %get-tuple-element.28), channel_id=1, source_target_pairs={{0,2},{1,3},{2,4},{3,5},{4,6},{5,7},{6,8},{7,9},{8,10},{9,11},{10,... | collective-permute-start | bytes 110600 | tf_op jit(solution)/shard_map/ppermute | solution.py:403
  104.6 14.3 %collective-permute-start.34 = (bf16[6,6,512]{2,1,0:T(8,128)(2,1)S(1)}, bf16[6,6,512]{2,1,0:T(8,128)(2,1)S(1)}, u32[]{:S(2)}, u32[]{:S(2)}) collective-permute-start(bf16[6,6,512]{2,1,0:T(8,128)(2,1)S(1)} %get-tuple-element.30), channel_id=1, source_target_pairs={{0,34},{1,35},{2,36},{3,37},{4,38},{5,39},{6,40},{7,41},{8,42},{9,... | collective-permute-start | bytes 110600 | tf_op jit(solution)/shard_map/ppermute | solution.py:403
  (16 other events, 133.3 us)

commit v3 on v2

--- a/solution.py
+++ b/solution.py
@@ -125,6 +125,13 @@
     my_x = lax.axis_index("x")
     for ref, (kind, flip, shift) in zip(refs, tags):
         c = 1 - core if flip else core
+        if kind == "all":
+            for k, dx in enumerate((0, *X_MOVES)):
+                for yh in range(2):
+                    col = lax.rem(my_x + 4 - dx, 4) * 4 + yh * 2 + c
+                    rows = pl.ds(pl.multiple_of(col * 32, 32), 32)
+                    dst[:, rows, :] = ref[k, yh, first : first + count]
+            continue
         for i in range(ref.shape[0]):
             if kind == "x":
                 col = i * 4 + (1 - my_yh if shift else my_yh) * 2 + c
@@ -488,12 +495,32 @@
     )(own, other, *after)
 
 
+def stack_kernel(*refs):
+    for k, ref in enumerate(refs[:-1]):
+        refs[-1][k] = ref[...]
+
+
+def spread_stack(both, came):
+    mine = pl.pallas_call(
+        stack_kernel,
+        out_shape=jax.ShapeDtypeStruct((4, *both.shape), BF),
+        compiler_params=pltpu.CompilerParams(vmem_limit_bytes=8 * MIB),
+        name="stack",
+    )(both, *came)
+    return (mine, swap_cores(mine)), (("all", 0, 0), ("all", 1, 0))
+
+
 def along_x(block):
     return [send(block, lambda row, x, y, c, dx=dx: (row, x + dx, y, c)) for dx in X_MOVES]
 
 
 def across_y(block):
     return send(block, lambda row, x, y, c: (row, x, 3 - y, c))
+
+
+def both_cores(mine, other):
+    blocks = (mine, swap_cores(mine), other, swap_cores(other))
+    return blocks, (("x", 0, 0), ("x", 1, 0), ("x", 0, 1), ("x", 1, 1))
 
 
 def spread_pair(both, came):
@@ -518,20 +545,22 @@
 ):
     weights = (qkv_weight, proj_weight, hidden_weight, output_weight)
     (first,) = chunks((((0, 0),),), (qkv_weight,))
-    rest, second = chunks((((0, 1), (0, 2), (0, 3)), ((1, 0), (1, 1), (1, 2), (1, 3))), weights)
+    rest, pairs, mlp1 = chunks(
+        (((0, 1), (0, 2)), ((0, 3), (1, 0), (1, 1)), ((1, 2), (1, 3))), weights
+    )
     rows = bias_rows(position_bias)
     first_y = across_y(first)
-    second_y = across_y(second)
     rest_x = along_x(rest)
+    pairs_y = across_y(pairs)
     (first,) = pair(first, first_y, ((0, 3),), ())
     first_x = along_x(first)
-    qkv0 = spread_pair(first, first_x)
-    attn1, mlp1 = pair(second, second_y, ((0, 4), (4, 12)), (first,))
-    mine = join_x(rest, rest_x, (mlp1,))
-    other = across_y(mine)
-    attn1_x = along_x(attn1)
+    qkv0 = spread_stack(first, first_x)
+    table0 = bias_table(rows[0], False, (first,))
+    rest_mine = join_x(rest, rest_x, (table0,))
+    rest_other = across_y(rest_mine)
     mlp1_x = along_x(mlp1)
-    table0 = bias_table(rows[0], False, (mine,))
+    down0, attn1 = pair(pairs, pairs_y, ((0, 4), (4, 8)), (rest_mine,))
+    down0_x = along_x(down0)
 
     def attn(k, pieces, assemble, blocks, table, counts):
         params = (qkv_bias, norm_gain, model_bias, table)
@@ -547,15 +576,20 @@
         return right, below, corner
 
     (ho,) = attn(0, (tokens,), assemble_plain, (qkv0, 0), table0, (TOK,))
-    rest0 = (mine, swap_cores(mine), other, swap_cores(other)), (("x", 0, 0), ("x", 1, 0), ("x", 0, 1), ("x", 1, 1))
+    attn1, ho = lax.optimization_barrier((attn1, ho))
+    attn1_x = along_x(attn1)
+    mlp1_mine = join_x(mlp1, mlp1_x, (ho,))
+    mlp1_other = across_y(mlp1_mine)
+    rest0 = both_cores(rest_mine, rest_other)
+    down0 = spread_pair(down0, down0_x)
     shapes = part_shapes()
     own, *halo = feed(
-        0, (tokens,), assemble_plain, finish_first, shapes, ((rest0, 0), (rest0, 1), (rest0, 5)), ho
+        0, (tokens,), assemble_plain, finish_first, shapes, ((rest0, 0), (rest0, 1), (down0, 0)), ho
     )
     table1 = bias_table(rows[1], True, tuple(halo))
     pieces = (own, *exchange(*halo, -1))
-    attn1 = spread_pair(attn1, attn1_x)
-    mlp1 = spread_pair(mlp1, mlp1_x)
+    attn1 = spread_stack(attn1, attn1_x)
+    mlp1 = both_cores(mlp1_mine, mlp1_other)
     sent_ho, kept_ho = attn(1, pieces, assemble_shifted, (attn1, 0), table1, (SENT, TOK - SENT))
     blocks = ((attn1, 3), (mlp1, 0), (mlp1, 4))
     sent = feed(1, pieces[1:], assemble_sent, finish_sent, shapes[1:], blocks, sent_ho)

time: 120 us -> 159 us (1.32)
  the two profiles are of different devices: /device:TPU:0 before, /device:TPU:8 now
where the time goes in v3:
time: 159 us
  waiting for transfers between devices  64.4 us (41%)
  starting transfers between devices  56.1 us (35%)
  Pallas kernels  31.7 us (20%)
  local copies, waits for them, and re-layouts  6.4 us (4%)
    ppermute x35, waiting for transfers between devices, send(): return lax.ppermute(block, AXES, pairs)  64.4 us
    ppermute x35, starting transfers between devices, send(): return lax.ppermute(block, AXES, pairs)  56.1 us
    pallas_call x2, Pallas kernels, attention(): pl.pallas_call(lambda *refs: attn_kernel(n, layer, tags, assemble, first,...  13.4 us
    pallas_call x2, Pallas kernels, bias_table(): pl.pallas_call(body, out_shape=jax.ShapeDtypeStruct((HEADS, KEYS, TOK), F...  8.41 us
    pallas_call x3, Pallas kernels, mlp(): pl.pallas_call(lambda *refs: mlp_kernel(n, layer, tags, firsts, assemble,...  7.83 us
    unnamed x28, local copies, waits for them, and re-layouts  5.36 us
  transfers between devices with their start and end apart: 35, of which 13 were waited for; matrix products, arithmetic and copies ran while one was open for 1% of the time, Pallas kernels for 18%

profile of v3, /device:TPU:8, one launch (start us, length us, event | category | flops | bytes accessed | tf_op | source)
XLA Modules:
  0.0 158.9 jit_solution(7403016314542139976)
XLA Ops:
  1.0 1.7 %collective-permute-start.4 = (bf16[3,32,512]{2,1,0:T(8,128)(2,1)S(1)}, bf16[3,32,512]{2,1,0:T(8,128)(2,1)S(1)}, u32[]{:S(2)}, u32[]{:S(2)}) collective-permute-start(bf16[3,32,512]{2,1,0:T(8,128)(2,1)S(1)} %chunks.3.refs_0_), channel_id=1, source_target_pairs={{0,5},{1,4},{2,7},{3,6},{4,1},{5,0},{6,3},{7,2},{8,13},{9,12},{10,... | collective-permute-start | bytes 294920 | tf_op jit(solution)/shard_map/ppermute | solution.py:410
  2.6 3.0 %collective-permute-done.4.refs_1_ = bf16[3,32,512]{2,1,0:T(8,128)(2,1)S(1)} collective-permute-done((bf16[3,32,512]{2,1,0:T(8,128)(2,1)S(1)}, bf16[3,32,512]{2,1,0:T(8,128)(2,1)S(1)}, u32[]{:S(2)}, u32[]{:S(2)}) %collective-permute-start.4) | collective-permute-done | bytes 98336 | tf_op jit(solution)/shard_map/ppermute | solution.py:410
  5.7 1.6 collective-permute-start.5
  7.3 1.7 %collective-permute-start.6 = (bf16[2,3,32,512]{3,2,1,0:T(8,128)(2,1)S(1)}, bf16[2,3,32,512]{3,2,1,0:T(8,128)(2,1)S(1)}, u32[]{:S(2)}, u32[]{:S(2)}) collective-permute-start(bf16[2,3,32,512]{3,2,1,0:T(8,128)(2,1)S(1)} %pair.2.refs_2_.refs_0_), channel_id=1, source_target_pairs={{0,24},{1,25},{2,26},{3,27},{4,28},{5,29},{6,30},{7,31},{8,0},{9,1... | collective-permute-start | bytes 589832 | tf_op jit(solution)/shard_map/ppermute | solution.py:410
  9.0 1.8 %collective-permute-start.7 = (bf16[2,3,32,512]{3,2,1,0:T(8,128)(2,1)S(1)}, bf16[2,3,32,512]{3,2,1,0:T(8,128)(2,1)S(1)}, u32[]{:S(2)}, u32[]{:S(2)}) collective-permute-start(bf16[2,3,32,512]{3,2,1,0:T(8,128)(2,1)S(1)} %pair.2.refs_2_.refs_0_), channel_id=1, source_target_pairs={{0,16},{1,17},{2,18},{3,19},{4,20},{5,21},{6,22},{7,23},{8,24},{9,... | collective-permute-start | bytes 589832 | tf_op jit(solution)/shard_map/ppermute | solution.py:410
  15.9 2.6 %collective-permute-start.2 = (bf16[5,32,512]{2,1,0:T(8,128)(2,1)S(1)}, bf16[5,32,512]{2,1,0:T(8,128)(2,1)S(1)}, u32[]{:S(2)}, u32[]{:S(2)}) collective-permute-start(bf16[5,32,512]{2,1,0:T(8,128)(2,1)S(1)} %get-tuple-element.22.refs_0_), channel_id=1, source_target_pairs={{0,24},{1,25},{2,26},{3,27},{4,28},{5,29},{6,30},{7,31},{8,0},{9,1... | collective-permute-start | bytes 491528 | tf_op jit(solution)/shard_map/ppermute | solution.py:410
  21.0 4.2 %bias_table.2.refs_4_.refs_7_ = f32[16,144,432]{2,1,0:T(8,128)S(1)} custom-call(f32[23,16,128]{2,1,0:T(8,128)S(1)} %get-tuple-element.38.refs_0_, f32[8,512]{1,0:T(8,128)S(1)} %copy-done.4, bf16[2,3,32,512]{3,2,1,0:T(8,128)(2,1)S(1)} %pair.2.refs_2_.refs_0_), custom_call_target="tpu_custom_call" | custom-call | tf_op jit(solution)/shard_map/bias_table/pallas_call | solution.py:111
  25.5 1.7 %collective-permute-start.10 = (bf16[4,5,32,512]{3,2,1,0:T(8,128)(2,1)S(1)}, bf16[4,5,32,512]{3,2,1,0:T(8,128)(2,1)S(1)}, u32[]{:S(2)}, u32[]{:S(2)}) collective-permute-start(bf16[4,5,32,512]{3,2,1,0:T(8,128)(2,1)S(1)} %join_x.2.refs_2_.refs_5_), channel_id=1, source_target_pairs={{0,5},{1,4},{2,7},{3,6},{4,1},{5,0},{6,3},{7,2},{8,13},{9,12},{10,... | collective-permute-start | bytes 1966088 | tf_op jit(solution)/shard_map/ppermute | solution.py:410
  28.2 2.6 %collective-permute-start.27 = (bf16[8,32,512]{2,1,0:T(8,128)(2,1)S(1)}, bf16[8,32,512]{2,1,0:T(8,128)(2,1)S(1)}, u32[]{:S(2)}, u32[]{:S(2)}) collective-permute-start(bf16[8,32,512]{2,1,0:T(8,128)(2,1)S(1)} %get-tuple-element.32.refs_0_), channel_id=1, source_target_pairs={{0,24},{1,25},{2,26},{3,27},{4,28},{5,29},{6,30},{7,31},{8,0},{9,1... | collective-permute-start | bytes 786440 | tf_op jit(solution)/shard_map/ppermute | solution.py:410
  30.8 17.4 %collective-permute-done.refs_1_ = bf16[8,32,512]{2,1,0:T(8,128)(2,1)S(1)} collective-permute-done((bf16[8,32,512]{2,1,0:T(8,128)(2,1)S(1)}, bf16[8,32,512]{2,1,0:T(8,128)(2,1)S(1)}, u32[]{:S(2)}, u32[]{:S(2)}) %collective-permute-start) | collective-permute-done | bytes 262176 | tf_op jit(solution)/shard_map/ppermute | solution.py:410
  48.2 3.0 %collective-permute-start.28 = (bf16[8,32,512]{2,1,0:T(8,128)(2,1)S(1)}, bf16[8,32,512]{2,1,0:T(8,128)(2,1)S(1)}, u32[]{:S(2)}, u32[]{:S(2)}) collective-permute-start(bf16[8,32,512]{2,1,0:T(8,128)(2,1)S(1)} %get-tuple-element.32.refs_0_), channel_id=1, source_target_pairs={{0,16},{1,17},{2,18},{3,19},{4,20},{5,21},{6,22},{7,23},{8,24},{9,... | collective-permute-start | bytes 786440 | tf_op jit(solution)/shard_map/ppermute | solution.py:410
  51.4 3.2 %collective-permute-start.15 = (bf16[2,4,32,512]{3,2,1,0:T(8,128)(2,1)S(1)}, bf16[2,4,32,512]{3,2,1,0:T(8,128)(2,1)S(1)}, u32[]{:S(2)}, u32[]{:S(2)}) collective-permute-start(bf16[2,4,32,512]{3,2,1,0:T(8,128)(2,1)S(1)} %get-tuple-element.25.refs_9_), channel_id=1, source_target_pairs={{0,24},{1,25},{2,26},{3,27},{4,28},{5,29},{6,30},{7,31},{8,0},{9,1... | collective-permute-start | bytes 786440 | tf_op jit(solution)/shard_map/ppermute | solution.py:410
  54.6 4.3 %collective-permute-done.28.refs_3_ = bf16[8,32,512]{2,1,0:T(8,128)(2,1)S(1)} collective-permute-done((bf16[8,32,512]{2,1,0:T(8,128)(2,1)S(1)}, bf16[8,32,512]{2,1,0:T(8,128)(2,1)S(1)}, u32[]{:S(2)}, u32[]{:S(2)}) %collective-permute-start.28) | collective-permute-done | bytes 262176 | tf_op jit(solution)/shard_map/ppermute | solution.py:410
  58.9 4.2 %collective-permute-done.13.refs_11_ = bf16[2,4,32,512]{3,2,1,0:T(8,128)(2,1)S(1)} collective-permute-done((bf16[2,4,32,512]{3,2,1,0:T(8,128)(2,1)S(1)}, bf16[2,4,32,512]{3,2,1,0:T(8,128)(2,1)S(1)}, u32[]{:S(2)}, u32[]{:S(2)}) %collective-permute-start.13) | collective-permute-done | bytes 262176 | tf_op jit(solution)/shard_map/ppermute | solution.py:410
  63.1 1.9 %collective-permute-start.17 = (bf16[2,4,32,512]{3,2,1,0:T(8,128)(2,1)S(1)}, bf16[2,4,32,512]{3,2,1,0:T(8,128)(2,1)S(1)}, u32[]{:S(2)}, u32[]{:S(2)}) collective-permute-start(bf16[2,4,32,512]{3,2,1,0:T(8,128)(2,1)S(1)} %get-tuple-element.25.refs_9_), channel_id=1, source_target_pairs={{0,16},{1,17},{2,18},{3,19},{4,20},{5,21},{6,22},{7,23},{8,24},{9,... | collective-permute-start | bytes 786440 | tf_op jit(solution)/shard_map/ppermute | solution.py:410
  65.6 6.7 %attention.2.refs_1_.refs_4_ = bf16[432,512]{1,0:T(8,128)(2,1)S(1)} custom-call(bf16[12,36,512]{2,1,0:T(8,128)(2,1)S(1)} %copy-done.7, bf16[4,2,3,32,512]{4,3,2,1,0:T(8,128)(2,1)S(1)} %stack.2.refs_1_, bf16[4,2,3,32,512]{4,3,2,1,0:T(8,128)(2,1)S(1)} %collective-permute-done.8.refs_2_, s32[8,512]{1,0:T(8,128)S(1)} %copy-done.13, f32[2,1536]{1,0:T(2,128)S(1)} %copy-done.10, ...), custom_call_target="tpu_custom_call" | custom-call | flops 10000000000 | bytes 8000000 | tf_op jit(solution)/shard_map/attention/pallas_call | solution.py:219
  73.3 2.8 %collective-permute-start.23 = (bf16[2,4,32,512]{3,2,1,0:T(8,128)(2,1)S(1)}, bf16[2,4,32,512]{3,2,1,0:T(8,128)(2,1)S(1)}, u32[]{:S(2)}, u32[]{:S(2)}) collective-permute-start(bf16[2,4,32,512]{3,2,1,0:T(8,128)(2,1)S(1)} %get-tuple-element.30.refs_0_), channel_id=1, source_target_pairs={{0,24},{1,25},{2,26},{3,27},{4,28},{5,29},{6,30},{7,31},{8,0},{9,1... | collective-permute-start | bytes 786440 | tf_op jit(solution)/shard_map/ppermute | solution.py:410
  76.4 5.8 %collective-permute-done.22.refs_1_ = bf16[2,4,32,512]{3,2,1,0:T(8,128)(2,1)S(1)} collective-permute-done((bf16[2,4,32,512]{3,2,1,0:T(8,128)(2,1)S(1)}, bf16[2,4,32,512]{3,2,1,0:T(8,128)(2,1)S(1)}, u32[]{:S(2)}, u32[]{:S(2)}) %collective-permute-start.22) | collective-permute-done | bytes 262176 | tf_op jit(solution)/shard_map/ppermute | solution.py:410
  82.2 4.9 %collective-permute-done.23.refs_2_ = bf16[2,4,32,512]{3,2,1,0:T(8,128)(2,1)S(1)} collective-permute-done((bf16[2,4,32,512]{3,2,1,0:T(8,128)(2,1)S(1)}, bf16[2,4,32,512]{3,2,1,0:T(8,128)(2,1)S(1)}, u32[]{:S(2)}, u32[]{:S(2)}) %collective-permute-start.23) | collective-permute-done | bytes 262176 | tf_op jit(solution)/shard_map/ppermute | solution.py:410
  88.5 1.6 collective-permute-start.30
  90.3 3.2 %mlp.3 = (bf16[6,30,512]{2,1,0:T(8,128)(2,1)S(1)}, bf16[6,6,512]{2,1,0:T(8,128)(2,1)S(1)}, bf16[6,30,512]{2,1,0:T(8,128)(2,1)S(1)}, bf16[6,6,512]{2,1,0:T(8,128)(2,1)S(1)}) custom-call(bf16[12,36,512]{2,1,0:T(8,128)(2,1)S(1)} %copy-done.7, bf16[432,512]{1,0:T(8,128)(2,1)S(1)} %attention.2.refs_1_.refs_4_, f32[2,2048]{1,0:T(2,128)S(1)} %copy-done.9, ...), custom_call_target="tpu_custom_call" | custom-call | flops 10000000000 | bytes 8000000 | tf_op jit(solution)/shard_map/mlp/pallas_call | solution.py:281
  93.6 5.9 %collective-permute-start.20 = (bf16[6,30,512]{2,1,0:T(8,128)(2,1)S(1)}, bf16[6,30,512]{2,1,0:T(8,128)(2,1)S(1)}, u32[]{:S(2)}, u32[]{:S(2)}) collective-permute-start(bf16[6,30,512]{2,1,0:T(8,128)(2,1)S(1)} %get-tuple-element.28.refs_3_), channel_id=1, source_target_pairs={{0,224},{1,225},{2,226},{3,227},{4,228},{5,229},{6,230},{7,231},{8... | collective-permute-start | bytes 552968 | tf_op jit(solution)/shard_map/ppermute | solution.py:410
  99.7 13.4 %collective-permute-done.30.refs_9_.refs_11_ = bf16[4,8,32,512]{3,2,1,0:T(8,128)(2,1)S(1)} collective-permute-done((bf16[4,8,32,512]{3,2,1,0:T(8,128)(2,1)S(1)}, bf16[4,8,32,512]{3,2,1,0:T(8,128)(2,1)S(1)}, u32[]{:S(2)}, u32[]{:S(2)}) %collective-permute-start.30) | collective-permute-done | bytes 1048608 | tf_op jit(solution)/shard_map/ppermute | solution.py:410
  113.1 8.9 %collective-permute-start.19 = (bf16[6,6,512]{2,1,0:T(8,128)(2,1)S(1)}, bf16[6,6,512]{2,1,0:T(8,128)(2,1)S(1)}, u32[]{:S(2)}, u32[]{:S(2)}) collective-permute-start(bf16[6,6,512]{2,1,0:T(8,128)(2,1)S(1)} %get-tuple-element.27.refs_2_), channel_id=1, source_target_pairs={{0,30},{1,31},{2,0},{3,1},{4,2},{5,3},{6,4},{7,5},{8,6},{9,7},{10,... | collective-permute-start | bytes 110600 | tf_op jit(solution)/shard_map/ppermute | solution.py:410
  122.0 1.8 %collective-permute-done.19.refs_1_.refs_0_ = bf16[6,6,512]{2,1,0:T(8,128)(2,1)S(1)} collective-permute-done((bf16[6,6,512]{2,1,0:T(8,128)(2,1)S(1)}, bf16[6,6,512]{2,1,0:T(8,128)(2,1)S(1)}, u32[]{:S(2)}, u32[]{:S(2)}) %collective-permute-start.19) | collective-permute-done | bytes 36896 | tf_op jit(solution)/shard_map/ppermute | solution.py:410
  123.8 10.7 %collective-permute-start.21 = (bf16[6,6,512]{2,1,0:T(8,128)(2,1)S(1)}, bf16[6,6,512]{2,1,0:T(8,128)(2,1)S(1)}, u32[]{:S(2)}, u32[]{:S(2)}) collective-permute-start(bf16[6,6,512]{2,1,0:T(8,128)(2,1)S(1)} %get-tuple-element.29.refs_4_), channel_id=1, source_target_pairs={{0,254},{1,255},{2,224},{3,225},{4,226},{5,227},{6,228},{7,229},{8... | collective-permute-start | bytes 110600 | tf_op jit(solution)/shard_map/ppermute | solution.py:410
  134.4 4.2 %bias_table.3.refs_10_ = f32[16,144,432]{2,1,0:T(8,128)S(1)} custom-call(f32[23,16,128]{2,1,0:T(8,128)S(1)} %get-tuple-element.37.refs_0_, f32[8,512]{1,0:T(8,128)S(1)} %copy-done.5, bf16[6,6,512]{2,1,0:T(8,128)(2,1)S(1)} %get-tuple-element.27.refs_2_, bf16[6,30,512]{2,1,0:T(8,128)(2,1)S(1)} %get-tuple-element.28.refs_3_, ...), custom_call_target="tpu_custom_call" | custom-call | tf_op jit(solution)/shard_map/bias_table/pallas_call | solution.py:111
  138.7 6.8 %attention.3 = (bf16[252,512]{1,0:T(8,128)(2,1)S(1)}, bf16[180,512]{1,0:T(8,128)(2,1)S(1)}) custom-call(bf16[6,30,512]{2,1,0:T(8,128)(2,1)S(1)} %get-tuple-element.26.refs_0_, bf16[6,6,512]{2,1,0:T(8,128)(2,1)S(1)} %collective-permute-done.19.refs_1_.refs_0_, bf16[6,30,512]{2,1,0:T(8,128)(2,1)S(1)} %collective-permute-done.20.refs_2_.refs_1_, ...), custom_call_target="tpu_custom_call" | custom-call | flops 10000000000 | bytes 8000000 | tf_op jit(solution)/shard_map/attention/pallas_call | solution.py:219
  145.5 2.5 %mlp.5 = (bf16[6,6,512]{2,1,0:T(8,128)(2,1)S(1)}, bf16[6,30,512]{2,1,0:T(8,128)(2,1)S(1)}, bf16[6,6,512]{2,1,0:T(8,128)(2,1)S(1)}) custom-call(bf16[6,6,512]{2,1,0:T(8,128)(2,1)S(1)} %collective-permute-done.19.refs_1_.refs_0_, bf16[6,30,512]{2,1,0:T(8,128)(2,1)S(1)} %collective-permute-done.20.refs_2_.refs_1_, ...), custom_call_target="tpu_custom_call" | custom-call | flops 10000000000 | bytes 8000000 | tf_op jit(solution)/shard_map/mlp/pallas_call | solution.py:281
  148.2 2.2 %mlp.4.own = bf16[6,30,512]{2,1,0:T(8,128)(2,1)S(1)} custom-call(bf16[6,30,512]{2,1,0:T(8,128)(2,1)S(1)} %get-tuple-element.26.refs_0_, bf16[180,512]{1,0:T(8,128)(2,1)S(1)} %get-tuple-element.31.refs_1_, f32[2,2048]{1,0:T(2,128)S(1)} %copy-done.9, f32[2,2,512]{2,1,0:T(2,128)S(1)} %copy-done.11, f32[2,4,512]{2,1,0:T(4,128)S(1)} %copy-done.8, ...), custom_call_target="tpu_custom_call" | custom-call | flops 10000000000 | bytes 8000000 | tf_op jit(solution)/shard_map/mlp/pallas_call | solution.py:281
  150.4 4.9 %collective-permute-done.32.right = bf16[6,6,512]{2,1,0:T(8,128)(2,1)S(1)} collective-permute-done((bf16[6,6,512]{2,1,0:T(8,128)(2,1)S(1)}, bf16[6,6,512]{2,1,0:T(8,128)(2,1)S(1)}, u32[]{:S(2)}, u32[]{:S(2)}) %collective-permute-start.32) | collective-permute-done | bytes 36896 | tf_op jit(solution)/shard_map/ppermute | solution.py:410
  155.3 2.7 %collective-permute-done.34.corner = bf16[6,6,512]{2,1,0:T(8,128)(2,1)S(1)} collective-permute-done((bf16[6,6,512]{2,1,0:T(8,128)(2,1)S(1)}, bf16[6,6,512]{2,1,0:T(8,128)(2,1)S(1)}, u32[]{:S(2)}, u32[]{:S(2)}) %collective-permute-start.34) | collective-permute-done | bytes 36896 | tf_op jit(solution)/shard_map/ppermute | solution.py:410
  (83 shorter events, 14.7 us)
Async XLA Ops:
  5.7 12.9 %collective-permute-start.5 = (bf16[2,3,32,512]{3,2,1,0:T(8,128)(2,1)S(1)}, bf16[2,3,32,512]{3,2,1,0:T(8,128)(2,1)S(1)}, u32[]{:S(2)}, u32[]{:S(2)}) collective-permute-start(bf16[2,3,32,512]{3,2,1,0:T(8,128)(2,1)S(1)} %pair.2.refs_2_.refs_0_), channel_id=1, source_target_pairs={{0,8},{1,9},{2,10},{3,11},{4,12},{5,13},{6,14},{7,15},{8,16},{9,17... | collective-permute-start | bytes 589832 | tf_op jit(solution)/shard_map/ppermute | solution.py:410
  7.3 11.8 %collective-permute-start.6 = (bf16[2,3,32,512]{3,2,1,0:T(8,128)(2,1)S(1)}, bf16[2,3,32,512]{3,2,1,0:T(8,128)(2,1)S(1)}, u32[]{:S(2)}, u32[]{:S(2)}) collective-permute-start(bf16[2,3,32,512]{3,2,1,0:T(8,128)(2,1)S(1)} %pair.2.refs_2_.refs_0_), channel_id=1, source_target_pairs={{0,24},{1,25},{2,26},{3,27},{4,28},{5,29},{6,30},{7,31},{8,0},{9,1... | collective-permute-start | bytes 589832 | tf_op jit(solution)/shard_map/ppermute | solution.py:410
  9.0 10.1 %collective-permute-start.7 = (bf16[2,3,32,512]{3,2,1,0:T(8,128)(2,1)S(1)}, bf16[2,3,32,512]{3,2,1,0:T(8,128)(2,1)S(1)}, u32[]{:S(2)}, u32[]{:S(2)}) collective-permute-start(bf16[2,3,32,512]{3,2,1,0:T(8,128)(2,1)S(1)} %pair.2.refs_2_.refs_0_), channel_id=1, source_target_pairs={{0,16},{1,17},{2,18},{3,19},{4,20},{5,21},{6,22},{7,23},{8,24},{9,... | collective-permute-start | bytes 589832 | tf_op jit(solution)/shard_map/ppermute | solution.py:410
  15.3 10.0 %collective-permute-start.1 = (bf16[5,32,512]{2,1,0:T(8,128)(2,1)S(1)}, bf16[5,32,512]{2,1,0:T(8,128)(2,1)S(1)}, u32[]{:S(2)}, u32[]{:S(2)}) collective-permute-start(bf16[5,32,512]{2,1,0:T(8,128)(2,1)S(1)} %get-tuple-element.22.refs_0_), channel_id=1, source_target_pairs={{0,8},{1,9},{2,10},{3,11},{4,12},{5,13},{6,14},{7,15},{8,16},{9,17... | collective-permute-start | bytes 491528 | tf_op jit(solution)/shard_map/ppermute | solution.py:410
  15.9 9.3 %collective-permute-start.2 = (bf16[5,32,512]{2,1,0:T(8,128)(2,1)S(1)}, bf16[5,32,512]{2,1,0:T(8,128)(2,1)S(1)}, u32[]{:S(2)}, u32[]{:S(2)}) collective-permute-start(bf16[5,32,512]{2,1,0:T(8,128)(2,1)S(1)} %get-tuple-element.22.refs_0_), channel_id=1, source_target_pairs={{0,24},{1,25},{2,26},{3,27},{4,28},{5,29},{6,30},{7,31},{8,0},{9,1... | collective-permute-start | bytes 491528 | tf_op jit(solution)/shard_map/ppermute | solution.py:410
  19.2 46.3 %collective-permute-start.8 = (bf16[4,2,3,32,512]{4,3,2,1,0:T(8,128)(2,1)S(1)}, bf16[4,2,3,32,512]{4,3,2,1,0:T(8,128)(2,1)S(1)}, u32[]{:S(2)}, u32[]{:S(2)}) collective-permute-start(bf16[4,2,3,32,512]{4,3,2,1,0:T(8,128)(2,1)S(1)} %stack.2.refs_1_), channel_id=1, source_target_pairs={{0,2},{1,3},{2,0},{3,1},{4,6},{5,7},{6,4},{7,5},{8,10},{9,11},{10,... | collective-permute-start | bytes 2359304 | tf_op jit(solution)/shard_map/ppermute | solution.py:410
  25.5 39.5 %collective-permute-start.10 = (bf16[4,5,32,512]{3,2,1,0:T(8,128)(2,1)S(1)}, bf16[4,5,32,512]{3,2,1,0:T(8,128)(2,1)S(1)}, u32[]{:S(2)}, u32[]{:S(2)}) collective-permute-start(bf16[4,5,32,512]{3,2,1,0:T(8,128)(2,1)S(1)} %join_x.2.refs_2_.refs_5_), channel_id=1, source_target_pairs={{0,5},{1,4},{2,7},{3,6},{4,1},{5,0},{6,3},{7,2},{8,13},{9,12},{10,... | collective-permute-start | bytes 1966088 | tf_op jit(solution)/shard_map/ppermute | solution.py:410
  27.1 21.1 %collective-permute-start = (bf16[8,32,512]{2,1,0:T(8,128)(2,1)S(1)}, bf16[8,32,512]{2,1,0:T(8,128)(2,1)S(1)}, u32[]{:S(2)}, u32[]{:S(2)}) collective-permute-start(bf16[8,32,512]{2,1,0:T(8,128)(2,1)S(1)} %get-tuple-element.21.refs_0_), channel_id=1, source_target_pairs={{0,5},{1,4},{2,7},{3,6},{4,1},{5,0},{6,3},{7,2},{8,13},{9,12},{10,... | collective-permute-start | bytes 786440 | tf_op jit(solution)/shard_map/ppermute | solution.py:410
  27.6 23.7 %collective-permute-start.26 = (bf16[8,32,512]{2,1,0:T(8,128)(2,1)S(1)}, bf16[8,32,512]{2,1,0:T(8,128)(2,1)S(1)}, u32[]{:S(2)}, u32[]{:S(2)}) collective-permute-start(bf16[8,32,512]{2,1,0:T(8,128)(2,1)S(1)} %get-tuple-element.32.refs_0_), channel_id=1, source_target_pairs={{0,8},{1,9},{2,10},{3,11},{4,12},{5,13},{6,14},{7,15},{8,16},{9,17... | collective-permute-start | bytes 786440 | tf_op jit(solution)/shard_map/ppermute | solution.py:410
  28.2 23.2 %collective-permute-start.27 = (bf16[8,32,512]{2,1,0:T(8,128)(2,1)S(1)}, bf16[8,32,512]{2,1,0:T(8,128)(2,1)S(1)}, u32[]{:S(2)}, u32[]{:S(2)}) collective-permute-start(bf16[8,32,512]{2,1,0:T(8,128)(2,1)S(1)} %get-tuple-element.32.refs_0_), channel_id=1, source_target_pairs={{0,24},{1,25},{2,26},{3,27},{4,28},{5,29},{6,30},{7,31},{8,0},{9,1... | collective-permute-start | bytes 786440 | tf_op jit(solution)/shard_map/ppermute | solution.py:410
  48.2 10.7 %collective-permute-start.28 = (bf16[8,32,512]{2,1,0:T(8,128)(2,1)S(1)}, bf16[8,32,512]{2,1,0:T(8,128)(2,1)S(1)}, u32[]{:S(2)}, u32[]{:S(2)}) collective-permute-start(bf16[8,32,512]{2,1,0:T(8,128)(2,1)S(1)} %get-tuple-element.32.refs_0_), channel_id=1, source_target_pairs={{0,16},{1,17},{2,18},{3,19},{4,20},{5,21},{6,22},{7,23},{8,24},{9,... | collective-permute-start | bytes 786440 | tf_op jit(solution)/shard_map/ppermute | solution.py:410
  51.3 11.8 %collective-permute-start.13 = (bf16[2,4,32,512]{3,2,1,0:T(8,128)(2,1)S(1)}, bf16[2,4,32,512]{3,2,1,0:T(8,128)(2,1)S(1)}, u32[]{:S(2)}, u32[]{:S(2)}) collective-permute-start(bf16[2,4,32,512]{3,2,1,0:T(8,128)(2,1)S(1)} %get-tuple-element.25.refs_9_), channel_id=1, source_target_pairs={{0,8},{1,9},{2,10},{3,11},{4,12},{5,13},{6,14},{7,15},{8,16},{9,17... | collective-permute-start | bytes 786440 | tf_op jit(solution)/shard_map/ppermute | solution.py:410
  51.4 13.6 %collective-permute-start.15 = (bf16[2,4,32,512]{3,2,1,0:T(8,128)(2,1)S(1)}, bf16[2,4,32,512]{3,2,1,0:T(8,128)(2,1)S(1)}, u32[]{:S(2)}, u32[]{:S(2)}) collective-permute-start(bf16[2,4,32,512]{3,2,1,0:T(8,128)(2,1)S(1)} %get-tuple-element.25.refs_9_), channel_id=1, source_target_pairs={{0,24},{1,25},{2,26},{3,27},{4,28},{5,29},{6,30},{7,31},{8,0},{9,1... | collective-permute-start | bytes 786440 | tf_op jit(solution)/shard_map/ppermute | solution.py:410
  58.9 31.4 %collective-permute-start.9 = (bf16[4,5,32,512]{3,2,1,0:T(8,128)(2,1)S(1)}, bf16[4,5,32,512]{3,2,1,0:T(8,128)(2,1)S(1)}, u32[]{:S(2)}, u32[]{:S(2)}) collective-permute-start(bf16[4,5,32,512]{3,2,1,0:T(8,128)(2,1)S(1)} %join_x.2.refs_2_.refs_5_), channel_id=1, source_target_pairs={{0,2},{1,3},{2,0},{3,1},{4,6},{5,7},{6,4},{7,5},{8,10},{9,11},{10,... | collective-permute-start | bytes 1966088 | tf_op jit(solution)/shard_map/ppermute | solution.py:410
  63.1 9.7 %collective-permute-start.17 = (bf16[2,4,32,512]{3,2,1,0:T(8,128)(2,1)S(1)}, bf16[2,4,32,512]{3,2,1,0:T(8,128)(2,1)S(1)}, u32[]{:S(2)}, u32[]{:S(2)}) collective-permute-start(bf16[2,4,32,512]{3,2,1,0:T(8,128)(2,1)S(1)} %get-tuple-element.25.refs_9_), channel_id=1, source_target_pairs={{0,16},{1,17},{2,18},{3,19},{4,20},{5,21},{6,22},{7,23},{8,24},{9,... | collective-permute-start | bytes 786440 | tf_op jit(solution)/shard_map/ppermute | solution.py:410
  65.0 8.3 %collective-permute-start.12 = (bf16[2,4,32,512]{3,2,1,0:T(8,128)(2,1)S(1)}, bf16[2,4,32,512]{3,2,1,0:T(8,128)(2,1)S(1)}, u32[]{:S(2)}, u32[]{:S(2)}) collective-permute-start(bf16[2,4,32,512]{3,2,1,0:T(8,128)(2,1)S(1)} %get-tuple-element.25.refs_9_), channel_id=1, source_target_pairs={{0,2},{1,3},{2,0},{3,1},{4,6},{5,7},{6,4},{7,5},{8,10},{9,11},{10,... | collective-permute-start | bytes 786440 | tf_op jit(solution)/shard_map/ppermute | solution.py:410
  65.0 11.1 %collective-permute-start.14 = (bf16[2,4,32,512]{3,2,1,0:T(8,128)(2,1)S(1)}, bf16[2,4,32,512]{3,2,1,0:T(8,128)(2,1)S(1)}, u32[]{:S(2)}, u32[]{:S(2)}) collective-permute-start(bf16[2,4,32,512]{3,2,1,0:T(8,128)(2,1)S(1)} %collective-permute-done.13.refs_11_), channel_id=1, source_target_pairs={{0,2},{1,3},{2,0},{3,1},{4,6},{5,7},{6,4},{7,5},{8,10},{9,11},{10,... | collective-permute-start | bytes 786440 | tf_op jit(solution)/shard_map/ppermute | solution.py:410
  65.5 24.8 %collective-permute-start.11 = (bf16[4,5,32,512]{3,2,1,0:T(8,128)(2,1)S(1)}, bf16[4,5,32,512]{3,2,1,0:T(8,128)(2,1)S(1)}, u32[]{:S(2)}, u32[]{:S(2)}) collective-permute-start(bf16[4,5,32,512]{3,2,1,0:T(8,128)(2,1)S(1)} %collective-permute-done.10.refs_7_), channel_id=1, source_target_pairs={{0,2},{1,3},{2,0},{3,1},{4,6},{5,7},{6,4},{7,5},{8,10},{9,11},{10,... | collective-permute-start | bytes 1966088 | tf_op jit(solution)/shard_map/ppermute | solution.py:410
  72.8 9.4 %collective-permute-start.22 = (bf16[2,4,32,512]{3,2,1,0:T(8,128)(2,1)S(1)}, bf16[2,4,32,512]{3,2,1,0:T(8,128)(2,1)S(1)}, u32[]{:S(2)}, u32[]{:S(2)}) collective-permute-start(bf16[2,4,32,512]{3,2,1,0:T(8,128)(2,1)S(1)} %get-tuple-element.30.refs_0_), channel_id=1, source_target_pairs={{0,8},{1,9},{2,10},{3,11},{4,12},{5,13},{6,14},{7,15},{8,16},{9,17... | collective-permute-start | bytes 786440 | tf_op jit(solution)/shard_map/ppermute | solution.py:410
  73.3 13.8 %collective-permute-start.23 = (bf16[2,4,32,512]{3,2,1,0:T(8,128)(2,1)S(1)}, bf16[2,4,32,512]{3,2,1,0:T(8,128)(2,1)S(1)}, u32[]{:S(2)}, u32[]{:S(2)}) collective-permute-start(bf16[2,4,32,512]{3,2,1,0:T(8,128)(2,1)S(1)} %get-tuple-element.30.refs_0_), channel_id=1, source_target_pairs={{0,24},{1,25},{2,26},{3,27},{4,28},{5,29},{6,30},{7,31},{8,0},{9,1... | collective-permute-start | bytes 786440 | tf_op jit(solution)/shard_map/ppermute | solution.py:410
  76.1 12.4 %collective-permute-start.24 = (bf16[2,4,32,512]{3,2,1,0:T(8,128)(2,1)S(1)}, bf16[2,4,32,512]{3,2,1,0:T(8,128)(2,1)S(1)}, u32[]{:S(2)}, u32[]{:S(2)}) collective-permute-start(bf16[2,4,32,512]{3,2,1,0:T(8,128)(2,1)S(1)} %get-tuple-element.30.refs_0_), channel_id=1, source_target_pairs={{0,16},{1,17},{2,18},{3,19},{4,20},{5,21},{6,22},{7,23},{8,24},{9,... | collective-permute-start | bytes 786440 | tf_op jit(solution)/shard_map/ppermute | solution.py:410
  82.2 7.9 %collective-permute-start.16 = (bf16[2,4,32,512]{3,2,1,0:T(8,128)(2,1)S(1)}, bf16[2,4,32,512]{3,2,1,0:T(8,128)(2,1)S(1)}, u32[]{:S(2)}, u32[]{:S(2)}) collective-permute-start(bf16[2,4,32,512]{3,2,1,0:T(8,128)(2,1)S(1)} %collective-permute-done.15.refs_13_), channel_id=1, source_target_pairs={{0,2},{1,3},{2,0},{3,1},{4,6},{5,7},{6,4},{7,5},{8,10},{9,11},{10,... | collective-permute-start | bytes 786440 | tf_op jit(solution)/shard_map/ppermute | solution.py:410
  88.5 24.6 %collective-permute-start.30 = (bf16[4,8,32,512]{3,2,1,0:T(8,128)(2,1)S(1)}, bf16[4,8,32,512]{3,2,1,0:T(8,128)(2,1)S(1)}, u32[]{:S(2)}, u32[]{:S(2)}) collective-permute-start(bf16[4,8,32,512]{3,2,1,0:T(8,128)(2,1)S(1)} %join_x.3.refs_7_.refs_9_), channel_id=1, source_target_pairs={{0,5},{1,4},{2,7},{3,6},{4,1},{5,0},{6,3},{7,2},{8,13},{9,12},{10,... | collective-permute-start | bytes 3145736 | tf_op jit(solution)/shard_map/ppermute | solution.py:410
  90.2 48.5 %collective-permute-start.25 = (bf16[4,2,4,32,512]{4,3,2,1,0:T(8,128)(2,1)S(1)}, bf16[4,2,4,32,512]{4,3,2,1,0:T(8,128)(2,1)S(1)}, u32[]{:S(2)}, u32[]{:S(2)}) collective-permute-start(bf16[4,2,4,32,512]{4,3,2,1,0:T(8,128)(2,1)S(1)} %stack.3.refs_4_.refs_5_.refs_7_), channel_id=1, source_target_pairs={{0,2},{1,3},{2,0},{3,1},{4,6},{5,7},{6,4},{7,5},{8,10},{9,11},{10,... | collective-permute-start | bytes 3145736 | tf_op jit(solution)/shard_map/ppermute | solution.py:410
  93.6 45.1 %collective-permute-start.20 = (bf16[6,30,512]{2,1,0:T(8,128)(2,1)S(1)}, bf16[6,30,512]{2,1,0:T(8,128)(2,1)S(1)}, u32[]{:S(2)}, u32[]{:S(2)}) collective-permute-start(bf16[6,30,512]{2,1,0:T(8,128)(2,1)S(1)} %get-tuple-element.28.refs_3_), channel_id=1, source_target_pairs={{0,224},{1,225},{2,226},{3,227},{4,228},{5,229},{6,230},{7,231},{8... | collective-permute-start | bytes 552968 | tf_op jit(solution)/shard_map/ppermute | solution.py:410
  99.5 46.0 %collective-permute-start.29 = (bf16[4,8,32,512]{3,2,1,0:T(8,128)(2,1)S(1)}, bf16[4,8,32,512]{3,2,1,0:T(8,128)(2,1)S(1)}, u32[]{:S(2)}, u32[]{:S(2)}) collective-permute-start(bf16[4,8,32,512]{3,2,1,0:T(8,128)(2,1)S(1)} %join_x.3.refs_7_.refs_9_), channel_id=1, source_target_pairs={{0,2},{1,3},{2,0},{3,1},{4,6},{5,7},{6,4},{7,5},{8,10},{9,11},{10,... | collective-permute-start | bytes 3145736 | tf_op jit(solution)/shard_map/ppermute | solution.py:410
  113.1 32.4 %collective-permute-start.31 = (bf16[4,8,32,512]{3,2,1,0:T(8,128)(2,1)S(1)}, bf16[4,8,32,512]{3,2,1,0:T(8,128)(2,1)S(1)}, u32[]{:S(2)}, u32[]{:S(2)}) collective-permute-start(bf16[4,8,32,512]{3,2,1,0:T(8,128)(2,1)S(1)} %collective-permute-done.30.refs_9_.refs_11_), channel_id=1, source_target_pairs={{0,2},{1,3},{2,0},{3,1},{4,6},{5,7},{6,4},{7,5},{8,10},{9,11},{10,... | collective-permute-start | bytes 3145736 | tf_op jit(solution)/shard_map/ppermute | solution.py:410
  113.1 10.7 %collective-permute-start.19 = (bf16[6,6,512]{2,1,0:T(8,128)(2,1)S(1)}, bf16[6,6,512]{2,1,0:T(8,128)(2,1)S(1)}, u32[]{:S(2)}, u32[]{:S(2)}) collective-permute-start(bf16[6,6,512]{2,1,0:T(8,128)(2,1)S(1)} %get-tuple-element.27.refs_2_), channel_id=1, source_target_pairs={{0,30},{1,31},{2,0},{3,1},{4,2},{5,3},{6,4},{7,5},{8,6},{9,7},{10,... | collective-permute-start | bytes 110600 | tf_op jit(solution)/shard_map/ppermute | solution.py:410
  123.8 14.9 %collective-permute-start.21 = (bf16[6,6,512]{2,1,0:T(8,128)(2,1)S(1)}, bf16[6,6,512]{2,1,0:T(8,128)(2,1)S(1)}, u32[]{:S(2)}, u32[]{:S(2)}) collective-permute-start(bf16[6,6,512]{2,1,0:T(8,128)(2,1)S(1)} %get-tuple-element.29.refs_4_), channel_id=1, source_target_pairs={{0,254},{1,255},{2,224},{3,225},{4,226},{5,227},{6,228},{7,229},{8... | collective-permute-start | bytes 110600 | tf_op jit(solution)/shard_map/ppermute | solution.py:410
  148.0 10.0 %collective-permute-start.33 = (bf16[6,30,512]{2,1,0:T(8,128)(2,1)S(1)}, bf16[6,30,512]{2,1,0:T(8,128)(2,1)S(1)}, u32[]{:S(2)}, u32[]{:S(2)}) collective-permute-start(bf16[6,30,512]{2,1,0:T(8,128)(2,1)S(1)} %get-tuple-element.35), channel_id=1, source_target_pairs={{0,32},{1,33},{2,34},{3,35},{4,36},{5,37},{6,38},{7,39},{8,40},{9,... | collective-permute-start | bytes 552968 | tf_op jit(solution)/shard_map/ppermute | solution.py:410
  148.1 7.2 %collective-permute-start.32 = (bf16[6,6,512]{2,1,0:T(8,128)(2,1)S(1)}, bf16[6,6,512]{2,1,0:T(8,128)(2,1)S(1)}, u32[]{:S(2)}, u32[]{:S(2)}) collective-permute-start(bf16[6,6,512]{2,1,0:T(8,128)(2,1)S(1)} %get-tuple-element.34), channel_id=1, source_target_pairs={{0,2},{1,3},{2,4},{3,5},{4,6},{5,7},{6,8},{7,9},{8,10},{9,11},{10,... | collective-permute-start | bytes 110600 | tf_op jit(solution)/shard_map/ppermute | solution.py:410
  148.1 9.8 %collective-permute-start.34 = (bf16[6,6,512]{2,1,0:T(8,128)(2,1)S(1)}, bf16[6,6,512]{2,1,0:T(8,128)(2,1)S(1)}, u32[]{:S(2)}, u32[]{:S(2)}) collective-permute-start(bf16[6,6,512]{2,1,0:T(8,128)(2,1)S(1)} %get-tuple-element.36), channel_id=1, source_target_pairs={{0,34},{1,35},{2,36},{3,37},{4,38},{5,39},{6,40},{7,41},{8,42},{9,... | collective-permute-start | bytes 110600 | tf_op jit(solution)/shard_map/ppermute | solution.py:410
  (17 other events, 350.3 us)
